TPU v7x, 32 devices: a whole 2x2x4 slice. The times are simulated.
32 devices in a mesh: group: 4 (over y, x), fsdp: 2 (over core), tensor: 4 (over z).
Axes of the slice: x: 2, y: 2, z: 4, core: 2. Of those that a mesh axis runs over, the one named last changes fastest.
Arguments:
- patches: bfloat16 [4, 2, 8, 577, 1024], P('group', None, ('fsdp', 'tensor')), may hold values from -6 to 6
- output_grad: bfloat16 [4, 2, 8, 577, 1024], P('group', None, ('fsdp', 'tensor')), may hold values from -6 to 6
- live_counts: int32 [4, 2, 2], P('group'), may hold values from 1 to 4, as said below
- attn_master: float32 [4, 1024, 1024], P(None, 'fsdp', 'tensor')
- mlp_master: float32 [2, 1024, 4096], P(None, 'fsdp', 'tensor')
- vector_master: float32 [12, 1024], replicated
- attn_moments: float32 [4, 2, 4, 1024, 1024], P('group', None, None, 'fsdp', 'tensor'), as said below
- mlp_moments: float32 [4, 2, 2, 1024, 4096], P('group', None, None, 'fsdp', 'tensor'), as said below
- vector_moments: float32 [4, 2, 12, 1024], P('group'), as said below
- attn_outer: float32 [4, 1024, 1024], P(None, 'fsdp', 'tensor'), may hold values from -0.125 to 0.125
- mlp_outer: float32 [2, 1024, 4096], P(None, 'fsdp', 'tensor'), may hold values from -0.125 to 0.125
- vector_outer: float32 [12, 1024], replicated, may hold values from -0.625 to 0.625
Outputs:
- block_output: bfloat16 [4, 2, 8, 577, 1024], P('group', None, ('fsdp', 'tensor'))
- patches_grad: float32 [4, 2, 8, 577, 1024], P('group', None, ('fsdp', 'tensor'))
- attn_inner: float32 [4, 2, 4, 1024, 1024], P('group', None, None, 'fsdp', 'tensor')
- attn_state: float32 [3, 4, 1024, 1024], P(None, None, 'fsdp', 'tensor')
- attn_copy: bfloat16 [4, 1024, 1024], P(None, 'fsdp', 'tensor')
- mlp_inner: float32 [4, 2, 2, 1024, 4096], P('group', None, None, 'fsdp', 'tensor')
- mlp_state: float32 [3, 2, 1024, 4096], P(None, None, 'fsdp', 'tensor')
- mlp_copy: bfloat16 [2, 1024, 4096], P(None, 'fsdp', 'tensor')
- vector_inner: float32 [4, 2, 12, 1024], P('group')
- vector_state: float32 [3, 12, 1024], replicated
- vector_copy: bfloat16 [12, 1024], replicated
Inputs may be any that keep to these rules, and one draw needn't show every extreme that they name: live_counts[g, m, f] images are live, and they stand first, among the f-th block of 4 image slots of micro-batch m in group g; some entry equals 4. `attn_moments`: second moments are positive. `mlp_moments`: second moments are positive. `vector_moments`: second moments are positive.
All inputs are finite; a program needn't handle non-finite values.
Results may differ from a plain program's by a relative error of at most 0.012.
The roundings to bfloat16 on the way count: a program that leaves them out, or rounds other values in their place, can miss the bound.
Values may be sent and summed in bfloat16 or wider, within the bound.
A program may use at most 320 MiB of HBM per device.

v0:
```python
from functools import partial

import jax
import jax.numpy as jnp
from jax import lax
from jax.sharding import PartitionSpec as P

HD = 64
FF = 4096
STEP = 8


EPSILON = 1e-06
INNER_RATE = 0.02
VECTOR_RATE = 0.2
WEIGHT_DECAY = 0.1
OUTER_RATE = 0.7
OUTER_MOMENTUM = 0.9


def normalize(source, gain_row, shift_row):
    centre = source - jnp.mean(source, axis=-1, keepdims=True)
    spread = jnp.mean(centre * centre, axis=-1, keepdims=True)
    return centre * lax.rsqrt(spread + EPSILON) * gain_row + shift_row


def gelu_exact(source):
    return jax.nn.gelu(source, approximate=False)


def gelu_slope(source):
    return (
        0.5 * (1.0 + lax.erf(source * 0.7071067811865476))
        + source * jnp.exp(-0.5 * source * source) * 0.3989422804014327
    )


def inner_adamw(master, gradient, moments, step_rate, decay_rate):
    first_moment = 0.9 * moments[0] + 0.1 * gradient
    second_moment = 0.95 * moments[1] + 0.05 * gradient * gradient
    step_ratio = (
        first_moment / (1.0 - 0.9**STEP) / (jnp.sqrt(second_moment / (1.0 - 0.95**STEP)) + 1e-08)
    )
    return (master - step_rate * (step_ratio + decay_rate * master), second_moment)


def outer_nesterov(master, outer_old, difference):
    momentum = OUTER_MOMENTUM * outer_old + difference
    updated = master - OUTER_RATE * (difference + OUTER_MOMENTUM * momentum)
    return (jnp.stack([difference, momentum, updated]), updated.astype(jnp.bfloat16))


def attend_forward(score_scale, operands):
    queries_low, keys_low, values_low = operands
    scores = (
        jnp.einsum("qhe,khe->hqk", queries_low, keys_low, preferred_element_type=jnp.float32)
        * score_scale
    )
    highest = jnp.max(scores, axis=-1, keepdims=True)
    exponent = jnp.exp(scores - highest)
    totals = jnp.sum(exponent, axis=-1, keepdims=True)
    probs_low = (exponent / totals).astype(jnp.bfloat16)
    attended = jnp.einsum("hqk,khe->qhe", probs_low, values_low, preferred_element_type=jnp.float32)
    return (attended.astype(jnp.bfloat16), (highest + jnp.log(totals))[..., 0])


def attend_backward(score_scale, operands):
    queries_low, keys_low, values_low, log_totals, grad_attended = operands
    scores = (
        jnp.einsum("qhe,khe->hqk", queries_low, keys_low, preferred_element_type=jnp.float32)
        * score_scale
    )
    probs_full = jnp.exp(scores - log_totals[..., None])
    grad_probs = jnp.einsum(
        "qhe,khe->hqk", grad_attended, values_low, preferred_element_type=jnp.float32
    )
    grad_values = jnp.einsum(
        "hqk,qhe->khe",
        probs_full.astype(jnp.bfloat16),
        grad_attended,
        preferred_element_type=jnp.float32,
    )
    weighted = jnp.sum(probs_full * grad_probs, axis=-1, keepdims=True)
    grad_scores = (probs_full * (grad_probs - weighted)).astype(jnp.bfloat16)
    grad_queries = (
        jnp.einsum("hqk,khe->qhe", grad_scores, keys_low, preferred_element_type=jnp.float32)
        * score_scale
    )
    grad_keys = (
        jnp.einsum("hqk,qhe->khe", grad_scores, queries_low, preferred_element_type=jnp.float32)
        * score_scale
    )
    return (
        grad_queries.astype(jnp.bfloat16),
        grad_keys.astype(jnp.bfloat16),
        grad_values.astype(jnp.bfloat16),
    )


def local(
    patches,
    output_grad,
    live_counts,
    attn_master,
    mlp_master,
    vector_master,
    attn_moments,
    mlp_moments,
    vector_moments,
    attn_outer,
    mlp_outer,
    vector_outer,
):
    narrow = jnp.bfloat16
    single = jnp.float32
    tensor_index = lax.axis_index("tensor")
    fsdp_index = lax.axis_index("fsdp")
    micro_count = patches.shape[1]
    local_images = patches.shape[2]
    seq_len = patches.shape[3]
    width = patches.shape[4]
    head_cols = attn_master.shape[2]
    hidden_cols = mlp_master.shape[2]
    score_scale = HD ** (-0.5)
    attn_all, mlp_all = (
        lax.all_gather(attn_master.astype(narrow), "fsdp", axis=1, tiled=True),
        lax.all_gather(mlp_master.astype(narrow), "fsdp", axis=1, tiled=True),
    )
    bias_query = lax.dynamic_slice_in_dim(vector_master[4], tensor_index * head_cols, head_cols)
    bias_value = lax.dynamic_slice_in_dim(vector_master[5], tensor_index * head_cols, head_cols)
    head_width = attn_all.shape[2]
    heads_here = head_width // HD
    bias_hidden = lax.dynamic_slice_in_dim(
        vector_master[8:].reshape(-1), tensor_index * hidden_cols, hidden_cols
    )
    owner_counts = jnp.sum(
        jnp.where(jnp.arange(live_counts.shape[2]) == fsdp_index, live_counts[0], 0), axis=-1
    )
    slot_index = tensor_index * local_images + jnp.arange(local_images)
    alive_all = (slot_index[None, :] < owner_counts[:, None]).astype(single)
    forward_attend = partial(attend_forward, score_scale)
    backward_attend = partial(attend_backward, score_scale)
    qkv_acc = jnp.zeros((3, width, head_width), single)
    out_acc = jnp.zeros((width, head_width), single)
    fc_in_acc = jnp.zeros((width, hidden_cols), single)
    fc_out_acc = jnp.zeros((width, hidden_cols), single)
    hidden_bias_acc = jnp.zeros((hidden_cols,), single)
    query_bias_acc = jnp.zeros((head_width,), single)
    value_bias_acc = jnp.zeros((head_width,), single)
    vector_acc = jnp.zeros((6, width), single)
    outputs_mixed = []
    outputs_grad = []
    for batch_index in range(micro_count):
        inputs = patches[0, batch_index].astype(single)
        alive = alive_all[batch_index][:, None, None]
        normed_one = normalize(inputs, vector_master[0], vector_master[1]).astype(narrow)
        rows_attn = lax.all_gather(normed_one, "tensor", axis=0, tiled=True)
        image_count = rows_attn.shape[0]
        shape_heads = (image_count, seq_len, heads_here, HD)
        projected = jnp.einsum(
            "isd,jde->jise", rows_attn, attn_all[:3], preferred_element_type=single
        )
        queries_low = (projected[0] + bias_query).astype(narrow).reshape(shape_heads)
        keys_low = projected[1].astype(narrow).reshape(shape_heads)
        values_low = (projected[2] + bias_value).astype(narrow).reshape(shape_heads)
        attended, log_totals = lax.map(forward_attend, (queries_low, keys_low, values_low))
        attended = attended.reshape(image_count, seq_len, head_width)
        branch_one = lax.psum_scatter(
            jnp.einsum("ise,de->isd", attended, attn_all[3], preferred_element_type=single),
            "tensor",
            scatter_dimension=0,
            tiled=True,
        )
        resid_one = inputs + branch_one + vector_master[6]
        normed_two = normalize(resid_one, vector_master[2], vector_master[3]).astype(narrow)
        rows_mlp = lax.all_gather(normed_two, "tensor", axis=0, tiled=True)
        pre_act = (
            jnp.einsum("isd,df->isf", rows_mlp, mlp_all[0], preferred_element_type=single)
            + bias_hidden
        )
        hidden = gelu_exact(pre_act).astype(narrow)
        branch_two = lax.psum_scatter(
            jnp.einsum("isf,df->isd", hidden, mlp_all[1], preferred_element_type=single),
            "tensor",
            scatter_dimension=0,
            tiled=True,
        )
        outputs_mixed.append((alive * (resid_one + branch_two + vector_master[7])).astype(narrow))
        grad_out = alive * output_grad[0, batch_index].astype(single)
        rows_grad_two = lax.all_gather(grad_out.astype(narrow), "tensor", axis=0, tiled=True)
        fc_out_acc = fc_out_acc + jnp.einsum(
            "isd,isf->df", rows_grad_two, hidden, preferred_element_type=single
        )
        grad_hidden = jnp.einsum(
            "isd,df->isf", rows_grad_two, mlp_all[1], preferred_element_type=single
        )
        grad_pre = (grad_hidden * gelu_slope(pre_act)).astype(narrow)
        fc_in_acc = fc_in_acc + jnp.einsum(
            "isd,isf->df", rows_mlp, grad_pre, preferred_element_type=single
        )
        hidden_bias_acc = hidden_bias_acc + jnp.sum(grad_pre.astype(single), axis=(0, 1))
        grad_normed_two = lax.psum_scatter(
            jnp.einsum("isf,df->isd", grad_pre, mlp_all[0], preferred_element_type=single),
            "tensor",
            scatter_dimension=0,
            tiled=True,
        )
        unused_two, norm_pull_two = jax.vjp(
            normalize, resid_one, vector_master[2], vector_master[3]
        )
        back_resid, gain_two, shift_two = norm_pull_two(grad_normed_two)
        grad_resid = grad_out + back_resid
        rows_grad_one = lax.all_gather(grad_resid.astype(narrow), "tensor", axis=0, tiled=True)
        out_acc = out_acc + jnp.einsum(
            "isd,ise->de", rows_grad_one, attended, preferred_element_type=single
        )
        grad_attended = jnp.einsum(
            "isd,de->ise", rows_grad_one, attn_all[3], preferred_element_type=single
        ).astype(narrow)
        grad_queries, grad_keys, grad_values = lax.map(
            backward_attend,
            (queries_low, keys_low, values_low, log_totals, grad_attended.reshape(shape_heads)),
        )
        grad_queries = grad_queries.reshape(image_count, seq_len, head_width)
        grad_keys = grad_keys.reshape(image_count, seq_len, head_width)
        grad_values = grad_values.reshape(image_count, seq_len, head_width)
        grad_stack = jnp.stack([grad_queries, grad_keys, grad_values])
        qkv_acc = qkv_acc + jnp.einsum(
            "isd,jise->jde", rows_attn, grad_stack, preferred_element_type=single
        )
        query_bias_acc = query_bias_acc + jnp.sum(grad_queries.astype(single), axis=(0, 1))
        value_bias_acc = value_bias_acc + jnp.sum(grad_values.astype(single), axis=(0, 1))
        summed = jnp.einsum("ise,de->isd", grad_queries, attn_all[0], preferred_element_type=single)
        summed = summed + jnp.einsum(
            "ise,de->isd", grad_keys, attn_all[1], preferred_element_type=single
        )
        grad_normed_one = lax.psum_scatter(
            summed
            + jnp.einsum("ise,de->isd", grad_values, attn_all[2], preferred_element_type=single),
            "tensor",
            scatter_dimension=0,
            tiled=True,
        )
        unused_one, norm_pull_one = jax.vjp(normalize, inputs, vector_master[0], vector_master[1])
        back_inputs, gain_one, shift_one = norm_pull_one(grad_normed_one)
        outputs_grad.append(grad_resid + back_inputs)
        vector_acc = vector_acc + jnp.stack(
            [
                gain_one,
                shift_one,
                gain_two,
                shift_two,
                jnp.sum(grad_resid, axis=(0, 1)),
                jnp.sum(grad_out, axis=(0, 1)),
            ]
        )
    attn_grad_full = jnp.concatenate([qkv_acc, out_acc[None]], 0)
    query_row = lax.dynamic_update_slice_in_dim(
        jnp.zeros((width,), single), query_bias_acc, tensor_index * head_cols, 0
    )
    value_row = lax.dynamic_update_slice_in_dim(
        jnp.zeros((width,), single), value_bias_acc, tensor_index * head_cols, 0
    )
    mlp_grad_cols = jnp.stack([fc_in_acc, fc_out_acc])
    attn_grad, mlp_grad = (
        lax.psum_scatter(attn_grad_full, "fsdp", scatter_dimension=1, tiled=True),
        lax.psum_scatter(mlp_grad_cols, "fsdp", scatter_dimension=1, tiled=True),
    )
    hidden_rows = lax.dynamic_update_slice_in_dim(
        jnp.zeros((FF,), single), hidden_bias_acc, tensor_index * hidden_cols, 0
    ).reshape(-1, width)
    vector_part = jnp.concatenate(
        [vector_acc[:4], jnp.stack([query_row, value_row]), vector_acc[4:], hidden_rows], 0
    )
    vector_grad = lax.psum(vector_part, ("fsdp", "tensor"))
    new_attn, second_attn = inner_adamw(
        attn_master, attn_grad, attn_moments[0], INNER_RATE, WEIGHT_DECAY
    )
    new_mlp, second_mlp = inner_adamw(
        mlp_master, mlp_grad, mlp_moments[0], INNER_RATE, WEIGHT_DECAY
    )
    new_vector, second_vector = inner_adamw(
        vector_master, vector_grad, vector_moments[0], VECTOR_RATE, 0.0
    )
    diff_attn, diff_mlp, diff_vector = lax.psum(
        (attn_master - new_attn, mlp_master - new_mlp, vector_master - new_vector), "group"
    )
    groups = lax.axis_size("group")
    attn_state, attn_copy = outer_nesterov(attn_master, attn_outer, diff_attn / groups)
    mlp_state, mlp_copy = outer_nesterov(mlp_master, mlp_outer, diff_mlp / groups)
    vector_state, vector_copy = outer_nesterov(vector_master, vector_outer, diff_vector / groups)
    block_output = jnp.stack(outputs_mixed)[None]
    patches_grad = jnp.stack(outputs_grad)[None]
    attn_inner = jnp.stack([attn_grad, second_attn])[None]
    mlp_inner = jnp.stack([mlp_grad, second_mlp])[None]
    vector_inner = jnp.stack([vector_grad, second_vector])[None]
    return (
        block_output,
        patches_grad,
        attn_inner,
        attn_state,
        attn_copy,
        mlp_inner,
        mlp_state,
        mlp_copy,
        vector_inner,
        vector_state,
        vector_copy,
    )


def solution(mesh):
    placed = (
        P("group", None, ("fsdp", "tensor"), None, None),
        P("group", None, ("fsdp", "tensor"), None, None),
        P("group", None, None),
        P(None, "fsdp", "tensor"),
        P(None, "fsdp", "tensor"),
        P(),
        P("group", None, None, "fsdp", "tensor"),
        P("group", None, None, "fsdp", "tensor"),
        P("group", None, None, None),
        P(None, "fsdp", "tensor"),
        P(None, "fsdp", "tensor"),
        P(),
    )
    return jax.shard_map(
        local,
        mesh=mesh,
        in_specs=placed,
        out_specs=(
            P("group", None, ("fsdp", "tensor"), None, None),
            P("group", None, ("fsdp", "tensor"), None, None),
            P("group", None, None, "fsdp", "tensor"),
            P(None, None, "fsdp", "tensor"),
            P(None, "fsdp", "tensor"),
            P("group", None, None, "fsdp", "tensor"),
            P(None, None, "fsdp", "tensor"),
            P(None, "fsdp", "tensor"),
            P("group", None, None, None),
            P(),
            P(),
        ),
        check_vma=False,
    )
```

profile of v0, /device:TPU:0, one launch (start us, length us, event | category | flops | bytes accessed | tf_op | source)
XLA Modules:
  0.0 2521.2 jit_solution(1555532051777853854)
XLA Ops:
  23.5 93.8 %all-gather.19.cloned.1.call-done = bf16[4,577,1024]{2,1,0:T(8,128)(2,1)} async-done(((bf16[1,577,1024]{2,1,0:T(8,128)(2,1)}), bf16[4,577,1024]{2,1,0:T(8,128)(2,1)}) %all-gather.19.cloned.1.call-update) | async-done | bytes 4726800 | tf_op jit(solution)/shard_map/all_gather | solution.py:157
  126.6 81.9 %all-gather.11.cloned.1.call-done = bf16[4,577,1024]{2,1,0:T(8,128)(2,1)} async-done(((bf16[1,577,1024]{2,1,0:T(8,128)(2,1)}), bf16[4,577,1024]{2,1,0:T(8,128)(2,1)}) %all-gather.11.cloned.1.call-update) | async-done | bytes 4726800 | tf_op jit(solution)/shard_map/all_gather | solution.py:157
  240.4 25.3 %while.53 = (s32[]{:T(128)}, bf16[4,577,4,64]{1,3,2,0:T(8,128)(2,1)}, f32[4,4,577]{2,1,0:T(4,128)S(1)}, bf16[4,577,4,64]{1,3,2,0:T(8,128)(2,1)}, bf16[4,577,4,64...) while((s32[]{:T(128)}, bf16[4,577,4,64]{1,3,2,0:T(8,128)(2,1)}, ...), condition=%wide.region_16.17_spmd, body=%wide.region_13.16_spmd.sunk | while | flops 353050112 | bytes 17370320 | solution.py:166
  289.1 21.4 while.52
  322.4 112.7 %reduce-scatter.15.cloned.1.call-done = f32[1,577,1024]{2,1,0:T(8,128)} async-done(((f32[4,577,1024]{2,1,0:T(8,128)}), f32[1,577,1024]{2,1,0:T(8,128)}) %reduce-scatter.15.cloned.1.call-update) | async-done | bytes 2363408 | tf_op jit(solution)/shard_map/reduce_scatter | solution.py:168
  435.1 167.2 %reduce-scatter.11.cloned.1.call-done = f32[1,577,1024]{2,1,0:T(8,128)} async-done(((f32[4,577,1024]{2,1,0:T(8,128)}), f32[1,577,1024]{2,1,0:T(8,128)}) %reduce-scatter.11.cloned.1.call-update) | async-done | bytes 2363408 | tf_op jit(solution)/shard_map/reduce_scatter | solution.py:168
  629.3 83.4 %all-gather.21.cloned.1.call-done = bf16[4,577,1024]{2,1,0:T(8,128)(2,1)} async-done(((bf16[1,577,1024]{2,1,0:T(8,128)(2,1)}), bf16[4,577,1024]{2,1,0:T(8,128)(2,1)}) %all-gather.21.cloned.1.call-update) | async-done | bytes 4726800 | tf_op jit(solution)/shard_map/all_gather | solution.py:176
  722.9 80.9 %all-gather.15.cloned.1.call-done = bf16[4,577,1024]{2,1,0:T(8,128)(2,1)} async-done(((bf16[1,577,1024]{2,1,0:T(8,128)(2,1)}), bf16[4,577,1024]{2,1,0:T(8,128)(2,1)}) %all-gather.15.cloned.1.call-update) | async-done | bytes 4726800 | tf_op jit(solution)/shard_map/all_gather | solution.py:176
  803.8 20.2 fusion.210
  824.0 70.3 %all-gather.23.cloned.1.call-done = bf16[4,577,1024]{2,1,0:T(8,128)(2,1)} async-done(((bf16[1,577,1024]{2,1,0:T(8,128)(2,1)}), bf16[4,577,1024]{2,1,0:T(8,128)(2,1)}) %all-gather.23.cloned.1.call-update) | async-done | bytes 4726800 | tf_op jit(solution)/shard_map/all_gather | solution.py:190
  917.0 67.8 %all-gather.27.cloned.1.call-done = bf16[4,577,1024]{2,1,0:T(8,128)(2,1)} async-done(((bf16[1,577,1024]{2,1,0:T(8,128)(2,1)}), bf16[4,577,1024]{2,1,0:T(8,128)(2,1)}) %all-gather.27.cloned.1.call-update) | async-done | bytes 4726800 | tf_op jit(solution)/shard_map/all_gather | solution.py:190
  1007.1 46.6 %fusion.116 = (bf16[4,577,1024]{2,1,0:T(8,128)(2,1)S(1)}, bf16[4,577,1024]{2,1,0:T(8,128)(2,1)}) fusion(f32[4,577,1024]{2,1,0:T(8,128)} %get-tuple-element.421, f32[1024]{0:T(1024)S(1)} %dynamic_slice.61, u8[577,1024]{1,0:T(8,128)(4,1)} %get-tuple-element.249, u8[577,1024]{1,0:T(8,128)(4,1)S(1)} %get-tuple-element.248, ...), kind=kLoop, calls=%fused_computation.127 | loop fusion | flops 333238272 | bytes 30728192 | tf_op jit(solution)/shard_map/convert_element_type | solution.py:181
  1074.5 74.4 %reduce-scatter.19.cloned.1.call-done = f32[1,577,1024]{2,1,0:T(8,128)} async-done(((f32[4,577,1024]{2,1,0:T(8,128)}), f32[1,577,1024]{2,1,0:T(8,128)}) %reduce-scatter.19.cloned.1.call-update) | async-done | bytes 2363408 | tf_op jit(solution)/shard_map/reduce_scatter | solution.py:202
  1148.9 166.6 %reduce-scatter.23.cloned.1.call-done = f32[1,577,1024]{2,1,0:T(8,128)} async-done(((f32[4,577,1024]{2,1,0:T(8,128)}), f32[1,577,1024]{2,1,0:T(8,128)}) %reduce-scatter.23.cloned.1.call-update) | async-done | bytes 2363408 | tf_op jit(solution)/shard_map/reduce_scatter | solution.py:202
  1320.8 161.4 %reduce-scatter.13.cloned.1.call-done = f32[1,577,1024]{2,1,0:T(8,128)} async-done(((f32[4,577,1024]{2,1,0:T(8,128)}), f32[1,577,1024]{2,1,0:T(8,128)}) %reduce-scatter.13.cloned.1.call-update) | async-done | bytes 2363408 | tf_op jit(solution)/shard_map/reduce_scatter | solution.py:182
  1482.1 167.2 %reduce-scatter.17.cloned.1.call-done = f32[1,577,1024]{2,1,0:T(8,128)} async-done(((f32[4,577,1024]{2,1,0:T(8,128)}), f32[1,577,1024]{2,1,0:T(8,128)}) %reduce-scatter.17.cloned.1.call-update) | async-done | bytes 2363408 | tf_op jit(solution)/shard_map/reduce_scatter | solution.py:182
  1700.8 51.3 %all-gather.29.cloned.1.call-done = bf16[4,577,1024]{2,1,0:T(8,128)(2,1)} async-done(((bf16[1,577,1024]{2,1,0:T(8,128)(2,1)}), bf16[4,577,1024]{2,1,0:T(8,128)(2,1)}) %all-gather.29.cloned.1.call-update) | async-done | bytes 4726800 | tf_op jit(solution)/shard_map/all_gather | solution.py:213
  1760.2 48.8 %while.55 = (s32[]{:T(128)}, bf16[4,577,4,64]{1,3,2,0:T(8,128)(2,1)S(1)}, bf16[4,577,4,64]{1,3,2,0:T(8,128)(2,1)}, bf16[4,577,4,64]{1,3,2,0:T(8,128)(2,1)}, bf16...) while((s32[]{:T(128)}, ...), condition=%wide.region_35.36_spmd, body=%wide.region_33.35_spmd.sunk | while | flops 869015040 | bytes 49660196 | solution.py:220
  1808.9 34.2 %all-gather.25.cloned.1.call-done = bf16[4,577,1024]{2,1,0:T(8,128)(2,1)} async-done(((bf16[1,577,1024]{2,1,0:T(8,128)(2,1)}), bf16[4,577,1024]{2,1,0:T(8,128)(2,1)}) %all-gather.25.cloned.1.call-update) | async-done | bytes 4726800 | tf_op jit(solution)/shard_map/all_gather | solution.py:213
  1858.7 53.2 %while.54 = (s32[]{:T(128)}, bf16[4,577,4,64]{1,3,2,0:T(8,128)(2,1)S(1)}, bf16[4,577,4,64]{1,3,2,0:T(8,128)(2,1)}, bf16[4,577,4,64]{1,3,2,0:T(8,128)(2,1)}, bf16...) while((s32[]{:T(128)}, ...), condition=%wide.region_26.27_spmd, body=%wide.region_24.26_spmd.sunk | while | flops 869015040 | bytes 49660196 | solution.py:220
  2025.6 79.9 %all-reduce.3.cloned.1.call-done = (f32[4,512,256]{1,2,0:T(8,128)}, f32[2,512,1024]{2,1,0:T(8,128)}) async-done(((f32[4,512,256]{1,2,0:T(8,128)}, f32[2,512,1024]{2,1,0:T(8,128)}), (f32[4,512,256]{1,2,0:T(8,128)}, f32[2,512,1024]{2,1,0:T(8,128)})) %all-reduce.3.cloned.1.call-update) | async-done | bytes 6291472 | tf_op jit(solution)/shard_map/psum | solution.py:285
  2146.0 125.0 %reduce-scatter.21.cloned.1.call-done = f32[1,577,1024]{2,1,0:T(8,128)} async-done(((f32[4,577,1024]{2,1,0:T(8,128)}), f32[1,577,1024]{2,1,0:T(8,128)}) %reduce-scatter.21.cloned.1.call-update) | async-done | bytes 2363408 | tf_op jit(solution)/shard_map/reduce_scatter | solution.py:237
  2273.4 164.4 %reduce-scatter.25.cloned.1.call-done = f32[1,577,1024]{2,1,0:T(8,128)} async-done(((f32[4,577,1024]{2,1,0:T(8,128)}), f32[1,577,1024]{2,1,0:T(8,128)}) %reduce-scatter.25.cloned.1.call-update) | async-done | bytes 2363408 | tf_op jit(solution)/shard_map/reduce_scatter | solution.py:237
  2448.6 29.2 %psum.30 = f32[12,1024]{1,0:T(8,128)S(1)} all-reduce(f32[12,1024]{1,0:T(8,128)S(1)} %concatenate.7), channel_id=1, replica_groups=mesh['group'=4,'fsdp'=2,'tensor'=4] {'fsdp','tensor'}, use_global_device_ids=true, to_apply=%region_61.62 | all-reduce | flops 12288 | bytes 98304 | tf_op jit(solution)/shard_map/psum | solution.py:275
  (490 shorter events, 626.4 us)
Async XLA Ops:
  7.2 16.3 all-gather.13.cloned.1.call-start
  10.1 107.3 %all-gather.19.cloned.1.call-start = ((), (), s32[]{:S(2)}) async-start(), calls=%async_computation.16 | async-start | bytes 5980160 | tf_op jit(solution)/shard_map/all_gather | solution.py:157
  19.3 189.2 %all-gather.11.cloned.1.call-start = ((), (), s32[]{:S(2)}) async-start(), calls=%async_computation.10 | async-start | bytes 5980160 | tf_op jit(solution)/shard_map/all_gather | solution.py:157
  20.0 415.1 %reduce-scatter.15.cloned.1.call-start = ((), (), s32[]{:S(2)}) async-start(), calls=%async_computation.17 | async-start | bytes 11960320 | tf_op jit(solution)/shard_map/reduce_scatter | solution.py:168
  273.1 329.1 %reduce-scatter.11.cloned.1.call-start = ((), (), s32[]{:S(2)}) async-start(), calls=%async_computation.12 | async-start | bytes 11960320 | tf_op jit(solution)/shard_map/reduce_scatter | solution.py:168
  318.4 310.9 %all-gather.17.cloned.1.call-start = ((), (), s32[]{:S(2)}) async-start(), calls=%async_computation.14 | async-start | bytes 6291456 | tf_op jit(solution)/shard_map/all_gather | solution.py:127
  322.3 390.3 %all-gather.21.cloned.1.call-start = ((), (), s32[]{:S(2)}) async-start(), calls=%async_computation.18 | async-start | bytes 5980160 | tf_op jit(solution)/shard_map/all_gather | solution.py:176
  609.2 194.6 %all-gather.15.cloned.1.call-start = ((), (), s32[]{:S(2)}) async-start(), calls=%async_computation.13 | async-start | bytes 5980160 | tf_op jit(solution)/shard_map/all_gather | solution.py:176
  609.9 284.4 %all-gather.23.cloned.1.call-start = ((), (), s32[]{:S(2)}) async-start(), calls=%async_computation.20 | async-start | bytes 5980160 | tf_op jit(solution)/shard_map/all_gather | solution.py:190
  623.7 361.1 %all-gather.27.cloned.1.call-start = ((), (), s32[]{:S(2)}) async-start(), calls=%async_computation.24 | async-start | bytes 5980160 | tf_op jit(solution)/shard_map/all_gather | solution.py:190
  628.2 520.7 %reduce-scatter.19.cloned.1.call-start = ((), (), s32[]{:S(2)}) async-start(), calls=%async_computation.21 | async-start | bytes 11960320 | tf_op jit(solution)/shard_map/reduce_scatter | solution.py:202
  916.9 398.6 %reduce-scatter.23.cloned.1.call-start = ((), (), s32[]{:S(2)}) async-start(), calls=%async_computation.25 | async-start | bytes 11960320 | tf_op jit(solution)/shard_map/reduce_scatter | solution.py:202
  1007.1 475.1 %reduce-scatter.13.cloned.1.call-start = ((), (), s32[]{:S(2)}) async-start(), calls=%async_computation.15 | async-start | bytes 11960320 | tf_op jit(solution)/shard_map/reduce_scatter | solution.py:182
  1063.8 585.5 %reduce-scatter.17.cloned.1.call-start = ((), (), s32[]{:S(2)}) async-start(), calls=%async_computation.19 | async-start | bytes 11960320 | tf_op jit(solution)/shard_map/reduce_scatter | solution.py:182
  1074.4 574.9 %copy-start.63 = (f32[1,1024]{1,0:T(1,128)S(1)}, f32[1,1024]{1,0:T(1,128)}, u32[]{:S(2)}) copy-start(f32[1,1024]{1,0:T(1,128)} %get-tuple-element.390) | copy-start | bytes 12292
  1074.5 677.7 %all-gather.29.cloned.1.call-start = ((), (), s32[]{:S(2)}) async-start(), calls=%async_computation.26 | async-start | bytes 5980160 | tf_op jit(solution)/shard_map/all_gather | solution.py:213
  1660.6 182.5 %all-gather.25.cloned.1.call-start = ((), (), s32[]{:S(2)}) async-start(), calls=%async_computation.22 | async-start | bytes 5980160 | tf_op jit(solution)/shard_map/all_gather | solution.py:213
  1665.2 286.8 %reduce-scatter.29.cloned.1.call-start = ((), (), s32[]{:S(2)}) async-start(), calls=%async_computation.29 | async-start | bytes 12582912 | tf_op jit(solution)/shard_map/reduce_scatter | solution.py:267
  1700.6 261.0 %reduce-scatter.27.cloned.1.call-start = ((), (), s32[]{:S(2)}) async-start(), calls=%async_computation.28 | async-start | bytes 6291456 | tf_op jit(solution)/shard_map/reduce_scatter | solution.py:266
  1937.4 168.1 %all-reduce.3.cloned.1.call-start = ((), (), s32[]{:S(2)}) async-start(), calls=%async_computation.30 | async-start | bytes 12582912 | tf_op jit(solution)/shard_map/psum | solution.py:285
  1968.7 302.4 %reduce-scatter.21.cloned.1.call-start = ((), (), s32[]{:S(2)}) async-start(), calls=%async_computation.23 | async-start | bytes 11960320 | tf_op jit(solution)/shard_map/reduce_scatter | solution.py:237
  1981.9 455.9 %reduce-scatter.25.cloned.1.call-start = ((), (), s32[]{:S(2)}) async-start(), calls=%async_computation.27 | async-start | bytes 11960320 | tf_op jit(solution)/shard_map/reduce_scatter | solution.py:237
  2146.0 291.8 %copy-start.39 = (f32[577]{0:T(1024)S(1)}, f32[577]{0:T(1024)}, u32[]{:S(2)}) copy-start(f32[577]{0:T(1024)} %copy-done.38) | copy-start | bytes 6928
  2146.0 291.8 %copy-start.49 = (f32[577]{0:T(1024)S(1)}, f32[577]{0:T(1024)}, u32[]{:S(2)}) copy-start(f32[577]{0:T(1024)} %copy-done.48) | copy-start | bytes 6928
  (94 other events, 2274.0 us)
Sparse Core Ops, SparseCore 0:
  10.2 13.2 all-gather.12
  25.6 91.6 all-gather.18
  119.5 88.9 all-gather.10
  273.3 161.7 reduce-scatter.14
  438.0 164.2 reduce-scatter.10
  604.3 14.5 all-gather.16
  621.0 91.6 all-gather.20
  714.8 88.9 all-gather.14
  805.4 88.9 all-gather.22
  895.8 88.9 all-gather.26
  987.1 161.7 reduce-scatter.18
  1151.3 164.2 reduce-scatter.22
  1317.9 164.2 reduce-scatter.12
  1485.0 164.2 reduce-scatter.16
  1660.7 91.3 all-gather.28
  1754.1 88.9 all-gather.24
  1845.8 15.2 reduce-scatter.28
  1937.5 10.6 reduce-scatter.26
  1968.8 136.6 all-reduce.2
  2107.6 163.3 reduce-scatter.20
  2273.5 164.2 reduce-scatter.24
where the time goes:
time: 2530 us; the launch traced here: 2520 us
  waiting for transfers between devices  1790 us (71%)
  matrix products  322 us (13%)
  other arithmetic  213 us (8%)
  local copies, waits for them, and re-layouts  124 us (5%)
  blocking collectives  46.8 us (2%)
    reduce_scatter x2, waiting for transfers between devices, local(): lax.psum_scatter(jnp.einsum('isf,df->isd', hidden, mlp_all[1], preferred_...  329 us
    reduce_scatter x2, waiting for transfers between devices, local(): lax.psum_scatter(summed + jnp.einsum('ise,de->isd', grad_values, attn_all...  289 us
    reduce_scatter x2, waiting for transfers between devices, local(): lax.psum_scatter(jnp.einsum('ise,de->isd', attended, attn_all[3], preferr...  280 us
    reduce_scatter x2, waiting for transfers between devices, local(): lax.psum_scatter(jnp.einsum('isf,df->isd', grad_pre, mlp_all[0], preferre...  241 us
    all_gather x2, waiting for transfers between devices, local(): rows_attn = lax.all_gather(normed_one, 'tensor', axis=0, tiled=True)  176 us
    all_gather x2, waiting for transfers between devices, local(): rows_mlp = lax.all_gather(normed_two, 'tensor', axis=0, tiled=True)  164 us
    all_gather x2, waiting for transfers between devices, local(): lax.all_gather(grad_out.astype(narrow), 'tensor', axis=0, tiled=True)  138 us
    all_gather x2, waiting for transfers between devices, local(): lax.all_gather(grad_resid.astype(narrow), 'tensor', axis=0, tiled=True)  85.5 us
  transfers between devices with their start and end apart: 21, of which 18 were waited for; matrix products, arithmetic and copies ran while one was open for 21% of the time, Pallas kernels for 0%

commit v1 on v0

v1 whole, which is shorter than its diff:
```python
import jax
import jax.numpy as jnp
from jax import lax
from jax.sharding import PartitionSpec as P

HD = 64
STEP = 8
IMG_DEV = 4


EPSILON = 1e-06
INNER_RATE = 0.02
VECTOR_RATE = 0.2
WEIGHT_DECAY = 0.1
OUTER_RATE = 0.7
OUTER_MOMENTUM = 0.9


def normalize(source, gain_row, shift_row):
    centre = source - jnp.mean(source, axis=-1, keepdims=True)
    spread = jnp.mean(centre * centre, axis=-1, keepdims=True)
    return centre * lax.rsqrt(spread + EPSILON) * gain_row + shift_row


def gelu_exact(source):
    return jax.nn.gelu(source, approximate=False)


def gelu_slope(source):
    return (
        0.5 * (1.0 + lax.erf(source * 0.7071067811865476))
        + source * jnp.exp(-0.5 * source * source) * 0.3989422804014327
    )


def inner_adamw(master, gradient, moments, step_rate, decay_rate):
    first_moment = 0.9 * moments[0] + 0.1 * gradient
    second_moment = 0.95 * moments[1] + 0.05 * gradient * gradient
    step_ratio = (
        first_moment / (1.0 - 0.9**STEP) / (jnp.sqrt(second_moment / (1.0 - 0.95**STEP)) + 1e-08)
    )
    return (master - step_rate * (step_ratio + decay_rate * master), second_moment)


def outer_nesterov(master, outer_old, difference):
    momentum = OUTER_MOMENTUM * outer_old + difference
    updated = master - OUTER_RATE * (difference + OUTER_MOMENTUM * momentum)
    return (jnp.stack([difference, momentum, updated]), updated.astype(jnp.bfloat16))


def attend(queries, keys, values, score_scale):
    scores = jnp.einsum("iqhe,ikhe->ihqk", queries, keys, preferred_element_type=jnp.float32) * score_scale
    highest = jnp.max(scores, axis=-1, keepdims=True)
    exponent = jnp.exp(scores - highest)
    totals = jnp.sum(exponent, axis=-1, keepdims=True)
    return exponent / totals


def gather_weight(low):
    whole = lax.all_gather(low, "tensor", axis=2, tiled=True)
    return lax.all_gather(whole, "fsdp", axis=1, tiled=True)


def scatter_gradient(gradient):
    low = gradient.astype(jnp.bfloat16)
    half = lax.psum_scatter(low, "fsdp", scatter_dimension=1, tiled=True)
    return lax.psum_scatter(half, "tensor", scatter_dimension=2, tiled=True).astype(jnp.float32)


def local(
    patches,
    output_grad,
    live_counts,
    attn_master,
    mlp_master,
    vector_master,
    attn_moments,
    mlp_moments,
    vector_moments,
    attn_outer,
    mlp_outer,
    vector_outer,
):
    narrow = jnp.bfloat16
    single = jnp.float32
    tensor_index = lax.axis_index("tensor")
    fsdp_index = lax.axis_index("fsdp")
    micro_count, local_images, seq_len, width = patches.shape[1:]
    score_scale = HD ** (-0.5)
    attn_low = attn_master.astype(narrow)
    mlp_low = mlp_master.astype(narrow)
    tensor_size = lax.axis_size("tensor")
    image_slot = (fsdp_index * tensor_size + tensor_index) * local_images + jnp.arange(local_images)
    block = IMG_DEV
    counts = jnp.take(live_counts[0], image_slot // block, axis=1)
    alive = ((image_slot % block)[None, :] < counts).astype(single).reshape(-1, 1, 1)
    inputs = patches[0].astype(single).reshape(-1, seq_len, width)
    cotangent = output_grad[0].astype(single).reshape(-1, seq_len, width)
    image_count = inputs.shape[0]
    w_qkv = gather_weight(attn_low[:3])
    w_out = gather_weight(attn_low[3:])[0]
    w_in = gather_weight(mlp_low[:1])[0]
    w_down = gather_weight(mlp_low[1:])[0]
    vec = vector_master
    bias_hidden = vec[8:].reshape(-1)
    normed_one = normalize(inputs, vec[0], vec[1]).astype(narrow)
    projected = jnp.einsum("isd,jde->jise", normed_one, w_qkv, preferred_element_type=single)
    heads = width // HD
    shape_heads = (image_count, seq_len, heads, HD)
    queries = (projected[0] + vec[4]).astype(narrow).reshape(shape_heads)
    keys = projected[1].astype(narrow).reshape(shape_heads)
    values = (projected[2] + vec[5]).astype(narrow).reshape(shape_heads)
    probs = attend(queries, keys, values, score_scale)
    probs_low = probs.astype(narrow)
    attended = jnp.einsum("ihqk,ikhe->iqhe", probs_low, values, preferred_element_type=single)
    attended = attended.astype(narrow).reshape(image_count, seq_len, width)
    branch_one = jnp.einsum("ise,de->isd", attended, w_out, preferred_element_type=single)
    resid_one = inputs + branch_one + vec[6]
    normed_two = normalize(resid_one, vec[2], vec[3]).astype(narrow)
    pre_act = jnp.einsum("isd,df->isf", normed_two, w_in, preferred_element_type=single) + bias_hidden
    hidden = gelu_exact(pre_act).astype(narrow)
    grad_out = alive * cotangent
    grad_two = grad_out.astype(narrow)
    grad_down = jnp.einsum("isd,isf->df", grad_two, hidden, preferred_element_type=single)
    g_down = scatter_gradient(grad_down[None])
    branch_two = jnp.einsum("isf,df->isd", hidden, w_down, preferred_element_type=single)
    block_output = (alive * (resid_one + branch_two + vec[7])).astype(narrow)
    grad_hidden = jnp.einsum("isd,df->isf", grad_two, w_down, preferred_element_type=single)
    grad_pre = (grad_hidden * gelu_slope(pre_act)).astype(narrow)
    grad_in = jnp.einsum("isd,isf->df", normed_two, grad_pre, preferred_element_type=single)
    g_in = scatter_gradient(grad_in[None])
    grad_normed_two = jnp.einsum("isf,df->isd", grad_pre, w_in, preferred_element_type=single)
    unused_two, pull_two = jax.vjp(normalize, resid_one, vec[2], vec[3])
    back_resid, gain_two, shift_two = pull_two(grad_normed_two)
    grad_resid = grad_out + back_resid
    grad_one = grad_resid.astype(narrow)
    grad_wo = jnp.einsum("isd,ise->de", grad_one, attended, preferred_element_type=single)
    g_out = scatter_gradient(grad_wo[None])
    grad_attended = jnp.einsum("isd,de->ise", grad_one, w_out, preferred_element_type=single)
    grad_attended = grad_attended.astype(narrow).reshape(shape_heads)
    grad_probs = jnp.einsum("iqhe,ikhe->ihqk", grad_attended, values, preferred_element_type=single)
    grad_values = jnp.einsum("ihqk,iqhe->ikhe", probs_low, grad_attended, preferred_element_type=single)
    weighted = jnp.sum(probs * grad_probs, axis=-1, keepdims=True)
    grad_scores = (probs * (grad_probs - weighted)).astype(narrow)
    grad_queries = jnp.einsum("ihqk,ikhe->iqhe", grad_scores, keys, preferred_element_type=single) * score_scale
    grad_keys = jnp.einsum("ihqk,iqhe->ikhe", grad_scores, queries, preferred_element_type=single) * score_scale
    stack = jnp.stack([grad_queries.astype(narrow), grad_keys.astype(narrow), grad_values.astype(narrow)])
    stack = stack.reshape(3, image_count, seq_len, width)
    grad_qkv = jnp.einsum("isd,jise->jde", normed_one, stack, preferred_element_type=single)
    g_qkv = scatter_gradient(grad_qkv)
    grad_normed_one = jnp.einsum("jise,jde->isd", stack, w_qkv, preferred_element_type=single)
    unused_one, pull_one = jax.vjp(normalize, inputs, vec[0], vec[1])
    back_inputs, gain_one, shift_one = pull_one(grad_normed_one)
    patches_grad = grad_resid + back_inputs
    vector_part = jnp.concatenate(
        [
            jnp.stack(
                [
                    gain_one,
                    shift_one,
                    gain_two,
                    shift_two,
                    jnp.sum(stack[0].astype(single), axis=(0, 1)),
                    jnp.sum(stack[2].astype(single), axis=(0, 1)),
                    jnp.sum(grad_resid, axis=(0, 1)),
                    jnp.sum(grad_out, axis=(0, 1)),
                ]
            ),
            jnp.sum(grad_pre.astype(single), axis=(0, 1)).reshape(-1, width),
        ]
    )
    vector_grad = lax.psum(vector_part, ("fsdp", "tensor"))
    attn_grad = jnp.concatenate([g_qkv, g_out])
    mlp_grad = jnp.concatenate([g_in, g_down])
    new_attn, second_attn = inner_adamw(attn_master, attn_grad, attn_moments[0], INNER_RATE, WEIGHT_DECAY)
    new_mlp, second_mlp = inner_adamw(mlp_master, mlp_grad, mlp_moments[0], INNER_RATE, WEIGHT_DECAY)
    new_vector, second_vector = inner_adamw(vec, vector_grad, vector_moments[0], VECTOR_RATE, 0.0)
    diff_attn, diff_mlp = lax.psum(
        ((attn_master - new_attn).astype(narrow), (mlp_master - new_mlp).astype(narrow)), "group"
    )
    diff_vector = lax.psum(vec - new_vector, "group")
    groups = lax.axis_size("group")
    attn_state, attn_copy = outer_nesterov(attn_master, attn_outer, diff_attn.astype(single) / groups)
    mlp_state, mlp_copy = outer_nesterov(mlp_master, mlp_outer, diff_mlp.astype(single) / groups)
    vector_state, vector_copy = outer_nesterov(vec, vector_outer, diff_vector / groups)
    shape_out = patches.shape
    return (
        block_output.reshape(shape_out),
        patches_grad.reshape(shape_out),
        jnp.stack([attn_grad, second_attn])[None],
        attn_state,
        attn_copy,
        jnp.stack([mlp_grad, second_mlp])[None],
        mlp_state,
        mlp_copy,
        jnp.stack([vector_grad, second_vector])[None],
        vector_state,
        vector_copy,
    )


def solution(mesh):
    placed = (
        P("group", None, ("fsdp", "tensor"), None, None),
        P("group", None, ("fsdp", "tensor"), None, None),
        P("group", None, None),
        P(None, "fsdp", "tensor"),
        P(None, "fsdp", "tensor"),
        P(),
        P("group", None, None, "fsdp", "tensor"),
        P("group", None, None, "fsdp", "tensor"),
        P("group", None, None, None),
        P(None, "fsdp", "tensor"),
        P(None, "fsdp", "tensor"),
        P(),
    )
    return jax.shard_map(
        local,
        mesh=mesh,
        in_specs=placed,
        out_specs=(
            P("group", None, ("fsdp", "tensor"), None, None),
            P("group", None, ("fsdp", "tensor"), None, None),
            P("group", None, None, "fsdp", "tensor"),
            P(None, None, "fsdp", "tensor"),
            P(None, "fsdp", "tensor"),
            P("group", None, None, "fsdp", "tensor"),
            P(None, None, "fsdp", "tensor"),
            P(None, "fsdp", "tensor"),
            P("group", None, None, None),
            P(),
            P(),
        ),
        check_vma=False,
    )
```

time: 2530 us -> 1130 us (0.45)
  waiting for transfers between devices: 1790 us -> 474 us
  other arithmetic: 213 us -> 182 us
    reduce_scatter x10 -> x8, waiting for transfers between devices: 1140 us -> 204 us  [the longest x4 188 us: scatter_gradient(): lax.psum_scatter(half, 'tensor', scatter_dimension=2, tiled=True)]
    all_gather x10 -> x8, waiting for transfers between devices: 566 us -> 268 us  [the longest x4 251 us: gather_weight(): whole = lax.all_gather(low, 'tensor', axis=2, tiled=True)]
    psum x1, waiting for transfers between devices: 79.9 us -> 0.01 us  [local(): lax.psum(((attn_master - new_attn).astype(narrow), (mlp_master - new_mlp)...]
    dot_general x84 -> x17, matrix products: 322 us -> 280 us  [the longest x1 39.2 us: local(): jnp.einsum('iqhe,ikhe->ihqk', grad_attended, values, preferred_element_ty...]
    convert_element_type x15 -> x7, other arithmetic: 29.3 us -> 53 us  [the longest x1 39.2 us: local(): grad_scores = (probs * (grad_probs - weighted)).astype(narrow)]
    unnamed x189 -> x157, local copies, waits for them, and re-layouts: 50.9 us -> 53.4 us
  transfers between devices with their start and end apart: 21 -> 17, of which waited for: 18 -> 9; matrix products, arithmetic and copies ran while one was open for 21% -> 36% of each run, Pallas kernels for 0% -> 0%
where the time goes in v1:
time: 1130 us
  waiting for transfers between devices  474 us (42%)
  matrix products  303 us (27%)
  other arithmetic  182 us (16%)
  local copies, waits for them, and re-layouts  108 us (10%)
  blocking collectives  46.4 us (4%)
  between operations  15.1 us (1%)
    all_gather x4, waiting for transfers between devices, gather_weight(): whole = lax.all_gather(low, 'tensor', axis=2, tiled=True)  251 us
    reduce_scatter x4, waiting for transfers between devices, scatter_gradient(): lax.psum_scatter(half, 'tensor', scatter_dimension=2, tiled=True)  188 us
    unnamed x157, local copies, waits for them, and re-layouts  53.4 us
    convert_element_type x1, other arithmetic, local(): hidden = gelu_exact(pre_act).astype(narrow)  46.9 us
    convert_element_type x1, other arithmetic, local(): grad_scores = (probs * (grad_probs - weighted)).astype(narrow)  39.2 us
    dot_general x1, matrix products, local(): jnp.einsum('iqhe,ikhe->ihqk', grad_attended, values, preferred_element_ty...  39.2 us
    psum x1, blocking collectives, local(): vector_grad = lax.psum(vector_part, ('fsdp', 'tensor'))  28.8 us
    dot_general x1, matrix products, local(): jnp.einsum('isd,df->isf', normed_two, w_in, preferred_element_type=single)  27.9 us
  transfers between devices with their start and end apart: 17, of which 9 were waited for; matrix products, arithmetic and copies ran while one was open for 36% of the time, Pallas kernels for 0%

profile of v1, /device:TPU:0, one launch (start us, length us, event | category | flops | bytes accessed | tf_op | source)
XLA Modules:
  0.0 1130.4 jit_solution(4393395515950830453)
XLA Ops:
  15.4 60.9 %all-gather.9.cloned.1.call-done = bf16[3,512,1024]{2,1,0:T(8,128)(2,1)} async-done(((bf16[3,512,256]{2,1,0:T(8,128)(2,1)}), bf16[3,512,1024]{2,1,0:T(8,128)(2,1)}) %all-gather.9.cloned.1.call-update) | async-done | bytes 3145744 | tf_op jit(solution)/shard_map/all_gather | solution.py:60
  76.4 30.5 %all-gather.13.cloned.1.call-done = bf16[1,512,1024]{2,1,0:T(8,128)(2,1)} async-done(((bf16[1,512,256]{2,1,0:T(8,128)(2,1)}), bf16[1,512,1024]{2,1,0:T(8,128)(2,1)}) %all-gather.13.cloned.1.call-update) | async-done | bytes 1048592 | tf_op jit(solution)/shard_map/all_gather | solution.py:60
  106.9 81.2 %all-gather.17.cloned.1.call-done = bf16[1,512,4096]{2,1,0:T(8,128)(2,1)} async-done(((bf16[1,512,1024]{2,1,0:T(8,128)(2,1)}), bf16[1,512,4096]{2,1,0:T(8,128)(2,1)}) %all-gather.17.cloned.1.call-update) | async-done | bytes 4194320 | tf_op jit(solution)/shard_map/all_gather | solution.py:60
  190.9 78.5 %all-gather.21.cloned.1.call-done = bf16[1,512,4096]{2,1,0:T(8,128)(2,1)} async-done(((bf16[1,512,1024]{2,1,0:T(8,128)(2,1)}), bf16[1,512,4096]{2,1,0:T(8,128)(2,1)}) %all-gather.21.cloned.1.call-update) | async-done | bytes 4194320 | tf_op jit(solution)/shard_map/all_gather | solution.py:60
  269.7 16.4 %all-gather.11.cloned.1.call-done = bf16[3,1024,1024]{2,1,0:T(8,128)(2,1)} async-done(((bf16[3,512,1024]{2,1,0:T(8,128)(2,1)}), bf16[3,1024,1024]{2,1,0:T(8,128)(2,1)}) %all-gather.11.cloned.1.call-update) | async-done | bytes 6291472 | tf_op jit(solution)/shard_map/all_gather | solution.py:61
  332.0 23.1 %fusion.156 = (f32[2,16,577]{2,1,0:T(8,128)S(1)}, f32[2,16,577,577]{2,3,1,0:T(8,128)}) fusion(bf16[2,577,16,64]{1,3,2,0:T(8,128)(2,1)} %bitcast.296, f32[2,577,16,64]{1,3,2,0:T(8,128)} %bitcast.293, f32[16,64]{1,0:T(8,128)S(1)} %add.245), kind=kOutput, calls=%fused_computation.230 | convolution fusion | flops 1398002304 | bytes 49783040 | tf_op jit(solution)/shard_map/sub | solution.py:54
  355.1 19.7 %fusion.99 = bf16[2,16,64,577]{3,2,1,0:T(8,128)(2,1)} fusion(f32[2,577,16,64]{1,3,2,0:T(8,128)} %bitcast.299, f32[16,64]{1,0:T(8,128)S(1)} %add.242, f32[2,16,577,577]{2,3,1,0:T(8,128)} %get-tuple-element.104, f32[2,16,577]{2,1,0:T(8,128)S(1)} %get-tuple-element.103), kind=kOutput, calls=%fused_computation.157 | convolution fusion | flops 1388529664 | bytes 49783040 | tf_op jit(solution)/shard_map/ihqk,ikhe->iqhe/dot_general | solution.py:115
  383.9 27.9 %fusion.61 = (u8[577,4096]{1,0:T(8,128)(4,1)}, u8[577,4096]{1,0:T(8,128)(4,1)}, f32[2,577,4096]{2,1,0:T(8,128)}) fusion(f32[4096]{0:T(1024)S(1)} %bitcast.306, bf16[1,1024,4096]{2,1,0:T(8,128)(2,1)} %all-gather.19.cloned.1.call-done, f32[2,577,1024]{2,1,0:T(8,128)} %copy-done, f32[1024]{0:T(1024)S(1)} %bitcast.325, f32[1024]{0:T(1024)S(1)} %bitcast.314, ...), kind=kOutput, calls=%fused_computation.108 | convolution fusion | flops 9747810304 | bytes 36783120 | tf_op jit(solution)/shard_map/isd,df->isf/dot_general | solution.py:120
  411.8 22.8 %convert_reduce_fusion = (f32[4096]{0:T(1024)}, bf16[2,577,4096]{2,1,0:T(8,128)(2,1)}) fusion(f32[2,577,4096]{2,1,0:T(8,128)} %get-tuple-element.107, f32[4096]{0:T(1024)S(1)} %bitcast.307, bf16[1,1024,4096]{2,1,0:T(8,128)(2,1)} %all-gather.23.cloned.1.call-done, f32[2]{0:T(128)S(1)} %fusion.136, bf16[1,2,1,577,1024]{4,1,3,2,0:T(2,128)(2,1)S(1)} %copy-done.17), kind=kOutput, calls=%fused_computation.24 | convolution fusion | flops 9745442816 | bytes 39145480 | tf_op jit(solution)/shard_map/isd,df->isf/dot_general | solution.py:128
  434.7 17.4 %fusion.146 = (f32[1024]{0:T(1024)}, f32[2,577]{1,0:T(2,128)S(1)}, f32[2,577,1024]{2,1,0:T(8,128)}) fusion(f32[1024]{0:T(1024)S(1)} %bitcast.315, f32[2,577,1024]{2,1,0:T(8,128)S(1)} %bitcast.290, f32[2,577]{1,0:T(2,128)S(1)} %broadcast_multiply_fusion, bf16[2,577,4096]{2,1,0:T(8,128)(2,1)} %get-tuple-element.117, ...), kind=kOutput, calls=%fused_computation.221 | convolution fusion | flops 9686360064 | bytes 27313168 | tf_op jit(solution)/shard_map/isf,df->isd/dot_general | solution.py:132
  476.0 19.5 %convert_reduce_fusion.2 = (f32[16,64]{1,0:T(8,128)}, bf16[2,16,64,577]{3,2,1,0:T(8,128)(2,1)}) fusion(bf16[2,577,16,64]{1,3,2,0:T(8,128)(2,1)S(1)} %bitcast.302, f32[2,16,577,577]{2,3,1,0:T(8,128)} %get-tuple-element.104, f32[2,16,577]{2,1,0:T(8,128)S(1)} %get-tuple-element.103), kind=kOutput, calls=%fused_computation.81 | convolution fusion | flops 1388528640 | bytes 47419648 | tf_op jit(solution)/shard_map/ihqk,iqhe->ikhe/dot_general | solution.py:142
  495.5 39.2 %multiply_reduce_fusion = (f32[2,16,577]{2,1,0:T(8,128)S(1)}, f32[2,16,577,577]{2,3,1,0:T(8,128)}) fusion(f32[2,16,577,577]{2,3,1,0:T(8,128)} %get-tuple-element.104, f32[2,16,577]{2,1,0:T(8,128)S(1)} %get-tuple-element.103, bf16[2,577,16,64]{1,3,2,0:T(8,128)(2,1)S(1)} %bitcast.303, f32[2,577,16,64]{1,3,2,0:T(8,128)} %bitcast.300, f32[16,64]{1,0:T(8,128)S(1)} %copy-done.56), kind=kOutput, calls=%fused_computation.2 | convolution fusion | flops 1397983232 | bytes 92471808 | tf_op jit(solution)/shard_map/iqhe,ikhe->ihqk/dot_general | solution.py:141
  534.8 39.2 %multiply_convert_fusion = bf16[2,16,577,577]{2,3,1,0:T(8,128)(2,1)} fusion(f32[2,16,577,577]{2,3,1,0:T(8,128)} %get-tuple-element.110, f32[2,16,577]{2,1,0:T(8,128)S(1)} %get-tuple-element.109, f32[2,16,577,577]{2,3,1,0:T(8,128)} %get-tuple-element.104, f32[2,16,577]{2,1,0:T(8,128)S(1)} %get-tuple-element.103), kind=kLoop, calls=%fused_computation.1 | loop fusion | flops 42614912 | bytes 106684992 | tf_op jit(solution)/shard_map/convert_element_type | solution.py:144
  626.4 18.4 %fusion.31 = bf16[1,1024,4096]{2,1,0:T(8,128)(2,1)} fusion(bf16[2,577,4096]{2,1,0:T(8,128)(2,1)} %get-tuple-element.117, f32[2,577,1024]{2,1,0:T(8,128)} %copy-done, f32[1024]{0:T(1024)S(1)} %bitcast.326, f32[1024]{0:T(1024)S(1)} %bitcast.318, f32[2,577]{1,0:T(2,128)S(1)} %copy-done.41, f32[2,577]{1,0:T(2,128)S(1)} %copy-done.29), kind=kOutput, calls=%fused_computation.57 | convolution fusion | flops 9690556416 | bytes 22586384 | tf_op jit(solution)/shard_map/isd,isf->df/dot_general | solution.py:130
  645.5 46.9 %fusion.7 = bf16[2,577,4096]{2,1,0:T(8,128)(2,1)S(1)} fusion(f32[2,577,4096]{2,1,0:T(8,128)} %get-tuple-element.107, f32[4096]{0:T(1024)S(1)} %bitcast.308, u8[577,4096]{1,0:T(8,128)(4,1)} %get-tuple-element.45, u8[577,4096]{1,0:T(8,128)(4,1)} %get-tuple-element.44), kind=kLoop, calls=%fused_computation.12 | loop fusion | flops 335601664 | bytes 33103872 | tf_op jit(solution)/shard_map/convert_element_type | solution.py:121
  696.3 15.0 %fusion.32 = bf16[1,1024,4096]{2,1,0:T(8,128)(2,1)} fusion(bf16[2,577,4096]{2,1,0:T(8,128)(2,1)S(1)} %fusion.7, f32[2]{0:T(128)S(1)} %copy-done.65, bf16[1,2,1,577,1024]{4,1,3,2,0:T(2,128)(2,1)S(1)} %copy-done.18), kind=kOutput, calls=%fused_computation.58 | convolution fusion | flops 9688193024 | bytes 20205576 | tf_op jit(solution)/shard_map/isd,isf->df/dot_general | solution.py:124
  713.3 16.1 %reduce-scatter.21.cloned.1.call-done = bf16[1,512,4096]{2,1,0:T(8,128)(2,1)} async-done(((bf16[1,1024,4096]{2,1,0:T(8,128)(2,1)}), bf16[1,512,4096]{2,1,0:T(8,128)(2,1)}) %reduce-scatter.21.cloned.1.call-update) | async-done | bytes 4194320 | tf_op jit(solution)/shard_map/reduce_scatter | solution.py:66
  746.6 15.2 %bitcast_reduce_fusion = (f32[1024]{0:T(1024)}, f32[2,577]{1,0:T(2,128)S(1)}, f32[2,577,1024,1]{2,1,3,0:T(8,128)}) fusion(f32[1024]{0:T(1024)S(1)} %bitcast.311, f32[2,577]{1,0:T(2,128)S(1)} %copy-done.27, bf16[1,2,1,577,1024]{4,1,3,2,0:T(2,128)(2,1)S(1)} %copy-done.2, bf16[3,1024,1024]{2,1,0:T(8,128)(2,1)} %all-gather.11.cloned.1.call-done, ...), kind=kOutput, calls=%fused_computation.99 | convolution fusion | flops 7274518528 | bytes 20489232 | tf_op jit(solution)/shard_map/jise,jde->isd/dot_general | solution.py:151
  761.8 16.6 %fusion.76 = bf16[1,2,1,577,1024]{4,3,1,2,0:T(8,128)(2,1)} fusion(f32[2,577,1024]{2,1,0:T(8,128)S(1)} %bitcast.292, f32[1024]{0:T(1024)S(1)} %bitcast.324, f32[2]{0:T(128)S(1)} %copy-done.65, bf16[2,577,4096]{2,1,0:T(8,128)(2,1)} %copy-done.13, bf16[1,1024,4096]{2,1,0:T(8,128)(2,1)} %all-gather.23.cloned.1.call-done), kind=kOutput, calls=%fused_computation.133 | convolution fusion | flops 9685180416 | bytes 24936456 | tf_op jit(solution)/shard_map/isf,df->isd/dot_general | solution.py:126
  779.4 41.9 %reduce-scatter.11.cloned.1.call-done = bf16[3,512,256]{1,2,0:T(8,128)(2,1)} async-done(((bf16[3,512,1024]{1,2,0:T(8,128)(2,1)}), bf16[3,512,256]{1,2,0:T(8,128)(2,1)}) %reduce-scatter.11.cloned.1.call-update) | async-done | bytes 786448 | tf_op jit(solution)/shard_map/reduce_scatter | solution.py:67
  829.7 70.8 %reduce-scatter.19.cloned.1.call-done = bf16[1,512,1024]{2,1,0:T(8,128)(2,1)} async-done(((bf16[1,512,4096]{2,1,0:T(8,128)(2,1)}), bf16[1,512,1024]{2,1,0:T(8,128)(2,1)}) %reduce-scatter.19.cloned.1.call-update) | async-done | bytes 1048592 | tf_op jit(solution)/shard_map/reduce_scatter | solution.py:67
  904.3 75.6 %reduce-scatter.23.cloned.1.call-done = bf16[1,512,1024]{2,1,0:T(8,128)(2,1)} async-done(((bf16[1,512,4096]{2,1,0:T(8,128)(2,1)}), bf16[1,512,1024]{2,1,0:T(8,128)(2,1)}) %reduce-scatter.23.cloned.1.call-update) | async-done | bytes 1048592 | tf_op jit(solution)/shard_map/reduce_scatter | solution.py:67
  1017.3 28.8 %psum.30 = f32[12,1024]{1,0:T(8,128)S(1)} all-reduce(f32[12,1024]{1,0:T(8,128)S(1)} %concatenate.56), channel_id=1, replica_groups=mesh['group'=4,'fsdp'=2,'tensor'=4] {'fsdp','tensor'}, use_global_device_ids=true, to_apply=%region_30.31 | all-reduce | flops 12288 | bytes 98304 | tf_op jit(solution)/shard_map/psum | solution.py:172
  1046.9 17.7 %psum.31 = f32[12,1024]{1,0:T(8,128)S(1)} all-reduce(f32[12,1024]{1,0:T(8,128)S(1)} %get-tuple-element.90), channel_id=1, replica_groups=mesh['group'=4,'fsdp'=2,'tensor'=4] {'group'}, use_global_device_ids=true, to_apply=%region_31.32 | all-reduce | flops 12288 | bytes 98304 | tf_op jit(solution)/shard_map/psum | solution.py:181
  (266 shorter events, 276.1 us)
Async XLA Ops:
  7.2 69.1 %all-gather.9.cloned.1.call-start = ((), (), s32[]{:S(2)}) async-start(), calls=%async_computation.8 | async-start | bytes 3932160 | tf_op jit(solution)/shard_map/all_gather | solution.py:60
  9.9 97.0 %all-gather.13.cloned.1.call-start = ((), (), s32[]{:S(2)}) async-start(), calls=%async_computation.10 | async-start | bytes 1310720 | tf_op jit(solution)/shard_map/all_gather | solution.py:60
  10.7 177.4 %all-gather.17.cloned.1.call-start = ((), (), s32[]{:S(2)}) async-start(), calls=%async_computation.12 | async-start | bytes 5242880 | tf_op jit(solution)/shard_map/all_gather | solution.py:60
  14.8 254.7 %all-gather.21.cloned.1.call-start = ((), (), s32[]{:S(2)}) async-start(), calls=%async_computation.14 | async-start | bytes 5242880 | tf_op jit(solution)/shard_map/all_gather | solution.py:60
  14.8 174.2 %copy-start.66 = (s32[1,2,2]{2,1,0:T(2,128)S(1)}, s32[1,2,2]{2,1,0:T(2,128)}, u32[]{:S(2)}) copy-start(s32[1,2,2]{2,1,0:T(2,128)} %param.14) | copy-start | bytes 52
  14.8 174.4 %copy-start.1 = (bf16[1,2,1,577,1024]{4,1,3,2,0:T(2,128)(2,1)S(1)}, bf16[1,2,1,577,1024]{4,1,3,2,0:T(2,128)(2,1)}, u32[]{:S(2)}) copy-start(bf16[1,2,1,577,1024]{4,1,3,2,0:T(2,128)(2,1)} %param.12) | copy-start | bytes 7090180
  15.3 270.8 %all-gather.11.cloned.1.call-start = ((), (), s32[]{:S(2)}) async-start(), calls=%async_computation.9 | async-start | bytes 9437184 | tf_op jit(solution)/shard_map/all_gather | solution.py:61
  76.3 298.5 %all-gather.15.cloned.1.call-start = ((), (), s32[]{:S(2)}) async-start(), calls=%async_computation.11 | async-start | bytes 3145728 | tf_op jit(solution)/shard_map/all_gather | solution.py:61
  106.9 277.0 %all-gather.19.cloned.1.call-start = ((), (), s32[]{:S(2)}) async-start(), calls=%async_computation.13 | async-start | bytes 12582912 | tf_op jit(solution)/shard_map/all_gather | solution.py:61
  188.1 223.7 %all-gather.23.cloned.1.call-start = ((), (), s32[]{:S(2)}) async-start(), calls=%async_computation.15 | async-start | bytes 12582912 | tf_op jit(solution)/shard_map/all_gather | solution.py:61
  188.2 223.6 %copy-start.30 = (f32[1,8,4,128]{3,1,2,0:T(8,128)}, f32[1,8,4,128]{3,1,2,0:T(8,128)S(1)}, u32[]{:S(2)}) copy-start(f32[1,8,4,128]{3,1,2,0:T(8,128)S(1)} %copy.159) | copy-start | bytes 49156
  188.9 195.0 %copy-start.59 = (f32[1,1024]{1,0:T(1,128)}, f32[1,1024]{1,0:T(1,128)S(1)}, u32[]{:S(2)}) copy-start(f32[1,1024]{1,0:T(1,128)S(1)} %get-tuple-element.97) | copy-start | bytes 12292
  188.9 267.8 %copy-start.44 = (f32[1,1024]{1,0:T(1,128)}, f32[1,1024]{1,0:T(1,128)S(1)}, u32[]{:S(2)}) copy-start(f32[1,1024]{1,0:T(1,128)S(1)} %get-tuple-element.95) | copy-start | bytes 12292
  189.2 267.5 %copy-start.64 = (f32[2]{0:T(128)}, f32[2]{0:T(128)S(1)}, u32[]{:S(2)}) copy-start(f32[2]{0:T(128)S(1)} %fusion.136) | copy-start | bytes 28
  269.5 441.9 %reduce-scatter.13.cloned.1.call-start = ((), (), s32[]{:S(2)}) async-start(), calls=%async_computation.18 | async-start | bytes 3145728 | tf_op jit(solution)/shard_map/reduce_scatter | solution.py:66
  534.7 177.4 %reduce-scatter.9.cloned.1.call-start = ((), (), s32[]{:S(2)}) async-start(), calls=%async_computation.16 | async-start | bytes 9437184 | tf_op jit(solution)/shard_map/reduce_scatter | solution.py:66
  625.8 86.9 %reduce-scatter.17.cloned.1.call-start = ((), (), s32[]{:S(2)}) async-start(), calls=%async_computation.20 | async-start | bytes 12582912 | tf_op jit(solution)/shard_map/reduce_scatter | solution.py:66
  644.8 84.6 %reduce-scatter.21.cloned.1.call-start = ((), (), s32[]{:S(2)}) async-start(), calls=%async_computation.22 | async-start | bytes 12582912 | tf_op jit(solution)/shard_map/reduce_scatter | solution.py:66
  711.3 67.1 %reduce-scatter.15.cloned.1.call-start = ((), (), s32[]{:S(2)}) async-start(), calls=%async_computation.19 | async-start | bytes 1310720 | tf_op jit(solution)/shard_map/reduce_scatter | solution.py:67
  712.1 109.3 %reduce-scatter.11.cloned.1.call-start = ((), (), s32[]{:S(2)}) async-start(), calls=%async_computation.17 | async-start | bytes 3932160 | tf_op jit(solution)/shard_map/reduce_scatter | solution.py:67
  712.6 187.8 %reduce-scatter.19.cloned.1.call-start = ((), (), s32[]{:S(2)}) async-start(), calls=%async_computation.21 | async-start | bytes 5242880 | tf_op jit(solution)/shard_map/reduce_scatter | solution.py:67
  713.2 266.6 %reduce-scatter.23.cloned.1.call-start = ((), (), s32[]{:S(2)}) async-start(), calls=%async_computation.23 | async-start | bytes 5242880 | tf_op jit(solution)/shard_map/reduce_scatter | solution.py:67
  729.4 354.9 %all-reduce.3.cloned.1.call-start = ((), (), s32[]{:S(2)}) async-start(), calls=%async_computation.24 | async-start | bytes 6291456 | tf_op jit(solution)/shard_map/psum | solution.py:178
  761.8 229.1 %copy-start.36 = (f32[2,577]{1,0:T(2,128)}, f32[2,577]{1,0:T(2,128)S(1)}, u32[]{:S(2)}) copy-start(f32[2,577]{1,0:T(2,128)S(1)} %multiply_multiply_fusion.11) | copy-start | bytes 13852
  (66 other events, 1920.3 us)
Sparse Core Ops, SparseCore 0:
  10.1 66.1 all-gather.8
  78.4 28.3 all-gather.12
  109.0 79.0 all-gather.16
  190.1 79.2 all-gather.20
  270.8 15.2 all-gather.10
  287.5 11.7 all-gather.14
  300.9 21.0 all-gather.18
  323.5 21.0 all-gather.22
  534.8 10.7 reduce-scatter.12
  625.9 15.6 reduce-scatter.8
  645.0 17.9 reduce-scatter.16
  711.4 17.9 reduce-scatter.20
  731.7 28.3 reduce-scatter.14
  762.4 58.8 reduce-scatter.10
  823.6 76.8 reduce-scatter.18
  902.6 77.2 reduce-scatter.22
  990.9 88.6 all-reduce.2

commit v2 on v1

v2 whole, which is shorter than its diff:
```python
import functools

import jax
import jax.numpy as jnp
from jax import lax
from jax.experimental import pallas as pl
from jax.experimental.pallas import tpu as pltpu
from jax.sharding import PartitionSpec as P

HD = 64
STEP = 8
IMG_DEV = 4
EPSILON = 1e-06
INNER_RATE = 0.02
VECTOR_RATE = 0.2
WEIGHT_DECAY = 0.1
OUTER_RATE = 0.7
OUTER_MOMENTUM = 0.9
QUARTERS = 4
LOW = jnp.bfloat16
F32 = jnp.float32
NN = (((1,), (0,)), ((), ()))
NT = (((1,), (1,)), ((), ()))
TN = (((0,), (0,)), ((), ()))


def dot(a, b, dims=NN):
    return lax.dot_general(a, b, dims, preferred_element_type=F32)


MESH = pl.DeviceIdType.MESH


def params(identity=None):
    if identity is None:
        return pltpu.CompilerParams(vmem_limit_bytes=60 * 2**20)
    return pltpu.CompilerParams(vmem_limit_bytes=60 * 2**20, collective_id=identity, has_side_effects=True)


def partner():
    return (lax.axis_index("group"), 1 - lax.axis_index("fsdp"), lax.axis_index("tensor"))


def greet_partner():
    barrier = pltpu.get_barrier_semaphore()
    pl.semaphore_signal(barrier, inc=1, device_id=partner(), device_id_type=MESH)
    pl.semaphore_wait(barrier, 1)


def to_partner(sent, received, sends, receives, n):
    return pltpu.make_async_remote_copy(
        src_ref=sent.at[n],
        dst_ref=received.at[n],
        send_sem=sends.at[n],
        recv_sem=receives.at[n],
        device_id=partner(),
        device_id_type=MESH,
    )


def bands(depth):
    f = lax.axis_index("fsdp")
    return pl.ds(pl.multiple_of(f * depth, depth), depth), pl.ds(pl.multiple_of((1 - f) * depth, depth), depth)


def exchange_scratch(steps, shape):
    dma = pltpu.SemaphoreType.DMA
    return [
        pltpu.VMEM((steps, *shape), F32),
        pltpu.VMEM((steps, *shape), LOW),
        pltpu.VMEM((steps, *shape), LOW),
        dma((steps,)),
        dma((steps,)),
    ]


def cost(flops, moved, special=0):
    return pl.CostEstimate(flops=int(flops), bytes_accessed=int(moved), transcendentals=int(special))


def padded(rows):
    return -(-rows // 16) * 16


def centred(source):
    centre = source - jnp.mean(source, axis=-1, keepdims=True)
    spread = jnp.mean(centre * centre, axis=-1, keepdims=True)
    inverse = lax.rsqrt(spread + EPSILON)
    return centre * inverse, inverse


def norm_back(upstream, normal, inverse, gain):
    pulled = upstream * gain
    mean_one = jnp.mean(pulled, axis=-1, keepdims=True)
    mean_two = jnp.mean(pulled * normal, axis=-1, keepdims=True)
    return inverse * (pulled - mean_one - normal * mean_two)


def project_kernel(images, seq, x_ref, w_ref, vec_ref, n_ref, out_ref, n_scr):
    j, t = pl.program_id(0), pl.program_id(1)
    span = n_scr.shape[0] // images

    @pl.when((j == 0) & (t == 0))
    def _():
        n_scr[...] = jnp.zeros_like(n_scr)
        for i in range(images):
            normal, _ = centred(x_ref[i].astype(F32))
            n_scr[pl.ds(i * span, seq), :] = (normal * vec_ref[0:1] + vec_ref[1:2]).astype(LOW)
        n_ref[...] = n_scr[...]

    cols = out_ref.shape[-1]
    out = dot(n_scr[...], w_ref[0, 0])
    at = pl.ds(pl.multiple_of(t * cols, cols), cols)
    bias = jnp.where(j == 0, vec_ref[4:5, at], jnp.where(j == 2, vec_ref[5:6, at], 0.0))
    out_ref[0] = (out + bias).astype(LOW)


def project(patches, w_attn, vec):
    images, seq, width = patches.shape
    shards, _, _, cols = w_attn.shape
    rows = images * padded(seq)
    return pl.pallas_call(
        functools.partial(project_kernel, images, seq),
        grid=(3, shards),
        in_specs=[
            pl.BlockSpec((images, seq, width), lambda j, t: (0, 0, 0)),
            pl.BlockSpec((1, 1, width, cols), lambda j, t: (t, j, 0, 0)),
            pl.BlockSpec(vec.shape, lambda j, t: (0, 0)),
        ],
        out_specs=[
            pl.BlockSpec((rows, width), lambda j, t: (0, 0)),
            pl.BlockSpec((1, rows, cols), lambda j, t: (j, 0, t)),
        ],
        out_shape=[
            jax.ShapeDtypeStruct((rows, width), LOW),
            jax.ShapeDtypeStruct((3, rows, width), LOW),
        ],
        scratch_shapes=[pltpu.VMEM((rows, width), LOW)],
        compiler_params=params(),
        cost_estimate=cost(6 * rows * width * width, 16 * rows * width),
        name="project",
    )(patches, w_attn, vec)


def half_lanes(value, which):
    lane = lax.broadcasted_iota(jnp.int32, value.shape, 1)
    return jnp.where((lane >= HD) == bool(which), value, jnp.zeros_like(value))


def attend_kernel(seq, q_ref, k_ref, v_ref, out_ref):
    span = q_ref.shape[1]
    scale = HD**-0.5
    q, k, v = q_ref[0], k_ref[0], v_ref[0]
    parts = []
    for h in range(2):
        scores = dot(q, half_lanes(k, h), NT)
        lane = lax.broadcasted_iota(jnp.int32, scores.shape, 1)
        scores = jnp.where(lane < seq, scores, -1e30)
        top = jnp.max(scores, axis=1, keepdims=True)
        raised = jnp.exp((scores - top) * scale)
        total = jnp.sum(raised, axis=1, keepdims=True)
        probs = (raised * (1.0 / total)).astype(LOW)
        parts.append(dot(probs, v))
    lane = lax.broadcasted_iota(jnp.int32, (span, 2 * HD), 1)
    out_ref[...] = jnp.where(lane < HD, parts[0], parts[1]).astype(LOW)


def attend(qkv, images, seq):
    _, rows, width = qkv.shape
    span = rows // images
    pair = 2 * HD

    def take(j):
        return pl.BlockSpec((1, span, pair), lambda i, h: (j, i, h))

    return pl.pallas_call(
        functools.partial(attend_kernel, seq),
        grid=(images, width // pair),
        in_specs=[take(0), take(1), take(2)],
        out_specs=pl.BlockSpec((span, pair), lambda i, h: (i, h)),
        out_shape=jax.ShapeDtypeStruct((rows, width), LOW),
        compiler_params=params(),
        cost_estimate=cost(16 * rows * span * width, 8 * rows * width, rows * span * (width // HD)),
        name="attend",
    )(qkv, qkv, qkv)


def mix_kernel(seq, alive_ref, att_ref, x_ref, g_ref, w_ref, vec_ref, resid_ref, n_ref, g2_ref, x_scr):
    i = pl.program_id(0)
    shards, _, _, cols = w_ref.shape
    x_scr[...] = jnp.zeros_like(x_scr)
    x_scr[0:seq, :] = x_ref[0].astype(F32)
    total = x_scr[...] + vec_ref[6:7]
    for t in range(shards):
        total = total + dot(att_ref[:, t * cols : (t + 1) * cols], w_ref[t, 0], NT)
    resid_ref[...] = total
    normal, _ = centred(total)
    n_ref[...] = (normal * vec_ref[2:3] + vec_ref[3:4]).astype(LOW)
    x_scr[0:seq, :] = g_ref[0].astype(F32) * alive_ref[i]
    g2_ref[...] = x_scr[...].astype(LOW)


def mix(alive, attended, patches, cotangent, w_attn, vec):
    images, seq, width = patches.shape
    rows = attended.shape[0]
    span = rows // images
    shards, _, _, cols = w_attn.shape
    block = pl.BlockSpec((span, width), lambda i: (i, 0))
    whole = jax.ShapeDtypeStruct((rows, width), LOW)
    return pl.pallas_call(
        functools.partial(mix_kernel, seq),
        grid=(images,),
        in_specs=[
            pl.BlockSpec(memory_space=pltpu.SMEM),
            block,
            pl.BlockSpec((1, seq, width), lambda i: (i, 0, 0)),
            pl.BlockSpec((1, seq, width), lambda i: (i, 0, 0)),
            pl.BlockSpec((shards, 1, width, cols), lambda i: (0, 3, 0, 0)),
            pl.BlockSpec(vec.shape, lambda i: (0, 0)),
        ],
        out_specs=[block, block, block],
        out_shape=[jax.ShapeDtypeStruct((rows, width), F32), whole, whole],
        scratch_shapes=[pltpu.VMEM((span, width), F32)],
        compiler_params=params(),
        cost_estimate=cost(2 * rows * width * width, 16 * rows * width),
        name="mix",
    )(alive, attended, patches, cotangent, w_attn, vec)


def mlp_kernel(first, pairwise, chunk, n_ref, g_ref, w1_ref, w2_ref, bias_ref, *refs):
    if not first:
        yi_ref, gi_ref, *refs = refs
    y_ref, gn_ref, dw_ref, db_ref, h_scr, p_scr, nt_scr, gt_scr, *exchange = refs
    step = pl.program_id(0)
    rows = n_ref.shape[0]
    each, _, width, cols = w1_ref.shape

    @pl.when(step == 0)
    def _():
        if pairwise:
            greet_partner()
        nt_scr[...] = n_ref[...].T
        gt_scr[...] = g_ref[...].T
        if first:
            y_ref[...] = jnp.zeros_like(y_ref)
            gn_ref[...] = jnp.zeros_like(gn_ref)
        else:
            y_ref[...] = yi_ref[...]
            gn_ref[...] = gi_ref[...]

    w1 = jnp.concatenate([w1_ref[t, 0] for t in range(each)], axis=1)
    w2 = jnp.concatenate([w2_ref[t, 0] for t in range(each)], axis=1)
    bias = jnp.concatenate([bias_ref[t] for t in range(each)], axis=1)

    def body(c, sums):
        at = pl.ds(pl.multiple_of(c * chunk, chunk), chunk)
        pre = dot(n_ref[at, :], w1) + bias
        cdf = 0.5 * (1.0 + lax.erf(pre * 0.7071067811865476))
        hidden = (pre * cdf).astype(LOW)
        slope = cdf + pre * jnp.exp(-0.5 * pre * pre) * 0.3989422804014327
        gp = dot(g_ref[at, :], w2) * slope
        gl = gp.astype(LOW)
        h_scr[at, :] = hidden
        p_scr[at, :] = gl
        y_ref[at, :] += dot(hidden, w2, NT)
        gn_ref[at, :] += dot(gl, w1, NT)
        return sums + jnp.sum(gl.astype(F32), axis=0, keepdims=True)

    sums = lax.fori_loop(0, rows // chunk, body, jnp.zeros((1, each * cols), F32))
    for t in range(each):
        db_ref[t] = sums[:, t * cols : (t + 1) * cols]
    if pairwise:
        own, sent, received, sends, receives = exchange
        ours, theirs = bands(width // 2)
        sent[step, 0] = dot(nt_scr[theirs, :], p_scr[...]).astype(LOW)
        sent[step, 1] = dot(gt_scr[theirs, :], h_scr[...]).astype(LOW)
        to_partner(sent, received, sends, receives, step).start()
        own[step, 0] = dot(nt_scr[ours, :], p_scr[...])
        own[step, 1] = dot(gt_scr[ours, :], h_scr[...])

        @pl.when(step == pl.num_programs(0) - 1)
        def _():
            for n in range(own.shape[0]):
                to_partner(sent, received, sends, receives, n).wait()
                for which in range(2):
                    total = (own[n, which] + received[n, which].astype(F32)).astype(LOW)
                    for t in range(each):
                        dw_ref[n * each + t, which] = total[:, t * cols : (t + 1) * cols]

        return
    shards, depth = dw_ref.shape[0], dw_ref.shape[3]
    d1 = dot(nt_scr[...], p_scr[...]).astype(LOW)
    d2 = dot(gt_scr[...], h_scr[...]).astype(LOW)
    for f in range(shards):
        for t in range(each):
            dw_ref[f, t, 0] = d1[f * depth : (f + 1) * depth, t * cols : (t + 1) * cols]
            dw_ref[f, t, 1] = d2[f * depth : (f + 1) * depth, t * cols : (t + 1) * cols]


def mlp(quarter, quarters, normed, grad_two, w_mlp, bias, carried, fsdp):
    rows, width = normed.shape
    shards, _, _, hidden = w_mlp.shape
    cols = hidden // quarters
    each = 2
    first, pairwise = carried is None, fsdp == 2
    single = pl.Buffered(1)
    full = pl.BlockSpec((rows, width), lambda s: (0, 0), pipeline_mode=single)
    depth = width // fsdp
    steps = shards // each
    acc_shape = jax.ShapeDtypeStruct((rows, width), F32)
    if pairwise:
        out_w = pl.BlockSpec((shards, 2, depth, cols), lambda s: (0, 0, 0, 0), pipeline_mode=single)
        w_shape = jax.ShapeDtypeStruct((shards, 2, depth, cols), LOW)
        extra = exchange_scratch(steps, (2, depth, each * cols))
    else:
        out_w = pl.BlockSpec((fsdp, each, 2, depth, cols), lambda s: (0, s, 0, 0, 0))
        w_shape = jax.ShapeDtypeStruct((fsdp, shards, 2, depth, cols), LOW)
        extra = []
    return pl.pallas_call(
        functools.partial(mlp_kernel, first, pairwise, rows // 4),
        grid=(steps,),
        in_specs=[
            full,
            full,
            pl.BlockSpec((each, 1, width, cols), lambda s: (s, 0, 0, quarter)),
            pl.BlockSpec((each, 1, width, cols), lambda s: (s, 1, 0, quarter)),
            pl.BlockSpec((each, 1, cols), lambda s: (s, 0, quarter)),
        ]
        + ([] if first else [full, full]),
        out_specs=[full, full, out_w, pl.BlockSpec((each, 1, cols), lambda s: (s, 0, 0))],
        out_shape=[acc_shape, acc_shape, w_shape, jax.ShapeDtypeStruct((shards, 1, cols), F32)],
        scratch_shapes=[
            pltpu.VMEM((rows, each * cols), LOW),
            pltpu.VMEM((rows, each * cols), LOW),
            pltpu.VMEM((width, rows), LOW),
            pltpu.VMEM((width, rows), LOW),
            *extra,
        ],
        compiler_params=params(2 + quarter if pairwise else None),
        cost_estimate=cost(12 * rows * width * cols * shards, 24 * rows * width),
        name=f"mlp_{quarter}",
    )(normed, grad_two, w_mlp, w_mlp, bias, *([] if first else carried))


def turn_kernel(seq, pairwise, alive_ref, resid_ref, y_ref, gn_ref, g2_ref, att_ref, w_ref, vec_ref,
                out_ref, gr_ref, ga_ref, dw_ref, sums_ref, dw_scr, *exchange):
    i = pl.program_id(0)
    if pairwise:
        pl.when(i == 0)(greet_partner)
    shards, _, _, cols = w_ref.shape
    resid = resid_ref[...]
    out_ref[0] = ((resid + y_ref[...] + vec_ref[7:8]) * alive_ref[i]).astype(LOW)[0:seq]
    normal, inverse = centred(resid)
    upstream = gn_ref[...]
    grad_out = g2_ref[...].astype(F32)
    grad_resid = grad_out + norm_back(upstream, normal, inverse, vec_ref[2:3])
    gr_ref[...] = grad_resid
    low = grad_resid.astype(LOW)
    rows = [
        jnp.sum(upstream * normal, axis=0, keepdims=True),
        jnp.sum(upstream, axis=0, keepdims=True),
        jnp.sum(grad_resid, axis=0, keepdims=True),
        jnp.sum(grad_out, axis=0, keepdims=True),
    ]
    rows = jnp.concatenate(rows, axis=0)

    @pl.when(i == 0)
    def _():
        sums_ref[...] = rows

    @pl.when(i != 0)
    def _():
        sums_ref[...] += rows

    for t in range(shards):
        ga_ref[:, t * cols : (t + 1) * cols] = dot(low, w_ref[t, 0]).astype(LOW)
    part = dot(low.T, att_ref[...])

    @pl.when(i == 0)
    def _():
        dw_scr[...] = part

    @pl.when(i != 0)
    def _():
        dw_scr[...] += part

    @pl.when(i == pl.num_programs(0) - 1)
    def _():
        if pairwise:
            sent, received, sends, receives = exchange
            ours, theirs = bands(dw_scr.shape[0] // 2)
            sent[0] = dw_scr[theirs, :].astype(LOW)
            copy = to_partner(sent, received, sends, receives, 0)
            copy.start()
            copy.wait()
            total = (dw_scr[ours, :] + received[0].astype(F32)).astype(LOW)
            for t in range(shards):
                dw_ref[t, 0] = total[:, t * cols : (t + 1) * cols]
            return
        depth = dw_ref.shape[3]
        for f in range(dw_ref.shape[0]):
            for t in range(shards):
                dw_ref[f, t, 0] = dw_scr[f * depth : (f + 1) * depth, t * cols : (t + 1) * cols].astype(LOW)


def turn(alive, resid, branch, grad_normed, grad_two, attended, w_attn, vec, images, seq, fsdp):
    rows, width = resid.shape
    span = rows // images
    shards, _, _, cols = w_attn.shape
    depth = width // fsdp
    pairwise = fsdp == 2
    lead = () if pairwise else (fsdp,)
    block = pl.BlockSpec((span, width), lambda i: (i, 0))
    return pl.pallas_call(
        functools.partial(turn_kernel, seq, pairwise),
        grid=(images,),
        in_specs=[
            pl.BlockSpec(memory_space=pltpu.SMEM),
            block, block, block, block, block,
            pl.BlockSpec((shards, 1, width, cols), lambda i: (0, 3, 0, 0)),
            pl.BlockSpec(vec.shape, lambda i: (0, 0)),
        ],
        out_specs=[
            pl.BlockSpec((1, seq, width), lambda i: (i, 0, 0)),
            block, block,
            pl.BlockSpec((*lead, shards, 1, depth, cols), lambda i: (0,) * (4 + len(lead))),
            pl.BlockSpec((4, width), lambda i: (0, 0)),
        ],
        out_shape=[
            jax.ShapeDtypeStruct((images, seq, width), LOW),
            jax.ShapeDtypeStruct((rows, width), F32),
            jax.ShapeDtypeStruct((rows, width), LOW),
            jax.ShapeDtypeStruct((*lead, shards, 1, depth, cols), LOW),
            jax.ShapeDtypeStruct((4, width), F32),
        ],
        scratch_shapes=[pltpu.VMEM((width, width), F32)] + (exchange_scratch(1, (depth, width))[1:] if pairwise else []),
        compiler_params=params(6 if pairwise else None),
        cost_estimate=cost(4 * rows * width * width, 24 * rows * width),
        name="turn",
    )(alive, resid, branch, grad_normed, grad_two, attended, w_attn, vec)


def unattend_kernel(seq, q_ref, k_ref, v_ref, g_ref, dq_ref, dk_ref, dv_ref):
    span = q_ref.shape[1]
    scale = HD**-0.5
    q, k, v, g = q_ref[0], k_ref[0], v_ref[0], g_ref[...]
    parts = []
    for h in range(2):
        scores = dot(half_lanes(k, h), q, NT)
        row = lax.broadcasted_iota(jnp.int32, scores.shape, 0)
        scores = jnp.where(row < seq, scores, -1e30)
        top = jnp.max(scores, axis=0, keepdims=True)
        raised = jnp.exp((scores - top) * scale)
        total = jnp.sum(raised, axis=0, keepdims=True)
        probs = raised * (1.0 / total)
        gp = dot(half_lanes(v, h), g, NT)
        delta = jnp.sum(probs * gp, axis=0, keepdims=True)
        gs = (probs * (gp - delta)).astype(LOW)
        dv = dot(probs.astype(LOW), g)
        dk = dot(gs, q)
        dq = dot(gs, k, TN)
        parts.append((dq, dk, dv))
    lane = lax.broadcasted_iota(jnp.int32, (span, 2 * HD), 1) < HD
    dq_ref[0] = (jnp.where(lane, parts[0][0], parts[1][0]) * scale).astype(LOW)
    dk_ref[0] = (jnp.where(lane, parts[0][1], parts[1][1]) * scale).astype(LOW)
    dv_ref[0] = jnp.where(lane, parts[0][2], parts[1][2]).astype(LOW)


def unattend(qkv, grad_attended, images, seq):
    _, rows, width = qkv.shape
    span = rows // images
    pair = 2 * HD

    def take(j):
        return pl.BlockSpec((1, span, pair), lambda i, h: (j, i, h))

    out = pl.BlockSpec((1, span, pair), lambda i, h: (0, i, h))
    shape = jax.ShapeDtypeStruct((1, rows, width), LOW)
    return pl.pallas_call(
        functools.partial(unattend_kernel, seq),
        grid=(images, width // pair),
        in_specs=[take(0), take(1), take(2), pl.BlockSpec((span, pair), lambda i, h: (i, h))],
        out_specs=[out, out, out],
        out_shape=[shape, shape, shape],
        compiler_params=params(),
        cost_estimate=cost(40 * rows * span * width, 14 * rows * width, rows * span * (width // HD)),
        name="unattend",
    )(qkv, qkv, qkv, grad_attended)


def close_kernel(seq, images, pairwise, n_ref, dq_ref, dk_ref, dv_ref, w_ref, x_ref, gr_ref, vec_ref,
                 out_ref, dw_ref, sums_ref, acc_scr, nt_scr, *exchange):
    j = pl.program_id(0)
    if pairwise:
        own, sent, received, sends, receives = exchange
        pl.when(j == 0)(greet_partner)
    shards, _, _, cols = w_ref.shape
    span = n_ref.shape[0] // images

    @pl.when(j == 0)
    def _():
        nt_scr[...] = n_ref[...].T
        acc_scr[...] = jnp.zeros_like(acc_scr)
        sums_ref[2:3, :] = jnp.sum(dq_ref[0].astype(F32), axis=0, keepdims=True)
        sums_ref[3:4, :] = jnp.sum(dv_ref[0].astype(F32), axis=0, keepdims=True)

    def part(ref):
        if pairwise:
            ours, theirs = bands(nt_scr.shape[0] // 2)
            for t in range(shards):
                sent[j, t] = dot(nt_scr[theirs, :], ref[0, :, t * cols : (t + 1) * cols]).astype(LOW)
            to_partner(sent, received, sends, receives, j).start()
        for t in range(shards):
            block = ref[0, :, t * cols : (t + 1) * cols]
            acc_scr[...] += dot(block, w_ref[t, 0], NT)
            if pairwise:
                own[j, t] = dot(nt_scr[ours, :], block)
                continue
            depth = dw_ref.shape[3]
            dw = dot(nt_scr[...], block).astype(LOW)
            for f in range(dw_ref.shape[0]):
                dw_ref[f, t, 0] = dw[f * depth : (f + 1) * depth]

    @pl.when(j == 0)
    def _():
        part(dq_ref)

    @pl.when(j == 1)
    def _():
        part(dk_ref)

    @pl.when(j == 2)
    def _():
        part(dv_ref)
        gain = jnp.zeros((1, vec_ref.shape[1]), F32)
        shift = jnp.zeros((1, vec_ref.shape[1]), F32)
        for i in range(images):
            normal, inverse = centred(x_ref[i].astype(F32))
            upstream = acc_scr[i * span : i * span + seq, :]
            out_ref[i] = gr_ref[i * span : i * span + seq, :] + norm_back(upstream, normal, inverse, vec_ref[0:1])
            gain += jnp.sum(upstream * normal, axis=0, keepdims=True)
            shift += jnp.sum(upstream, axis=0, keepdims=True)
        sums_ref[0:1, :] = gain
        sums_ref[1:2, :] = shift
        if pairwise:
            for n in range(own.shape[0]):
                to_partner(sent, received, sends, receives, n).wait()
                for t in range(shards):
                    dw_ref[t, n] = (own[n, t] + received[n, t].astype(F32)).astype(LOW)


def close(normed, grads, w_attn, patches, grad_resid, vec, fsdp):
    images, seq, width = patches.shape
    rows = normed.shape[0]
    shards, _, _, cols = w_attn.shape
    depth = width // fsdp
    pairwise = fsdp == 2
    if pairwise:
        dw_spec = pl.BlockSpec((shards, 3, depth, cols), lambda j: (0, 0, 0, 0), pipeline_mode=pl.Buffered(1))
        dw_shape = jax.ShapeDtypeStruct((shards, 3, depth, cols), LOW)
        extra = exchange_scratch(3, (shards, depth, cols))
    else:
        dw_spec = pl.BlockSpec((fsdp, shards, 1, depth, cols), lambda j: (0, 0, j, 0, 0))
        dw_shape = jax.ShapeDtypeStruct((fsdp, shards, 3, depth, cols), LOW)
        extra = []
    single = pl.Buffered(1)
    stack = pl.BlockSpec((1, rows, width), lambda j: (0, 0, 0), pipeline_mode=single)
    full = pl.BlockSpec((rows, width), lambda j: (0, 0), pipeline_mode=single)
    return pl.pallas_call(
        functools.partial(close_kernel, seq, images, pairwise),
        grid=(3,),
        in_specs=[
            full, stack, stack, stack,
            pl.BlockSpec((shards, 1, width, cols), lambda j: (0, j, 0, 0)),
            pl.BlockSpec((images, seq, width), lambda j: (0, 0, 0), pipeline_mode=single),
            full,
            pl.BlockSpec(vec.shape, lambda j: (0, 0)),
        ],
        out_specs=[
            pl.BlockSpec((images, seq, width), lambda j: (0, 0, 0), pipeline_mode=single),
            dw_spec,
            pl.BlockSpec((4, width), lambda j: (0, 0)),
        ],
        out_shape=[
            jax.ShapeDtypeStruct((images, seq, width), F32),
            dw_shape,
            jax.ShapeDtypeStruct((4, width), F32),
        ],
        scratch_shapes=[pltpu.VMEM((rows, width), F32), pltpu.VMEM((width, rows), LOW), *extra],
        compiler_params=params(7 if pairwise else None),
        cost_estimate=cost(12 * rows * width * width, 30 * rows * width),
        name="close",
    )(normed, *grads, w_attn, patches, grad_resid, vec)


def gather_kernel(a_in, m_in, a_out, m_out, a_hold, m_hold, zs, zr, xs, xr, ys, yr, xfs, xfr, yfs, yfr, cs, cr, ls):
    g, f, z = lax.axis_index("group"), lax.axis_index("fsdp"), lax.axis_index("tensor")
    last = lax.axis_size("tensor") - 1
    x_at, y_at = g % 2, g // 2
    east, north = y_at * 2 + (1 - x_at), (1 - y_at) * 2 + x_at
    depth = a_in.shape[1]
    band = depth // 4
    shared = band * 3 // 8
    rest = band - 2 * shared

    def place(column):
        cx, cy = column % 2, column // 2
        return 2 * (cx + cy - 2 * cx * cy) + cy

    mine, of_east, of_north = place(g), place(east), place(north)
    z_row = mine * band - shared * (mine % 2)
    lead_east = of_east * band + shared * (of_east % 2)
    lead_north = of_north * band + shared * (of_north % 2)
    chunks = ((a_in, a_out, 0, a_in.shape[0]), (m_in, m_out, 0, 1), (m_in, m_out, 1, 1))

    def tile(n):
        return pl.multiple_of(n, 16)

    def held(n, t, row, rows):
        _, out, j, many = chunks[n]
        return out.at[t, pl.ds(j, many), pl.ds(tile(f * depth + row), rows), :]

    def owned(n, row, rows):
        source, _, j, many = chunks[n]
        return source.at[pl.ds(j, many), pl.ds(tile(row), rows), :]

    def send(src, dst, sems, semr, n, t, to):
        return pltpu.make_async_remote_copy(
            src_ref=src, dst_ref=dst, send_sem=sems.at[n, t], recv_sem=semr.at[n, t], device_id=to, device_id_type=MESH
        )

    def along(n, t, up, src):
        return pltpu.make_async_remote_copy(
            src_ref=src,
            dst_ref=held(n, t, z_row, band + shared),
            send_sem=zs.at[n, t, 0 if up else 1],
            recv_sem=zr.at[n, t],
            device_id=(g, f, z + 1 if up else z - 1),
            device_id_type=MESH,
        )

    def to_east(n, t):
        part = held(n, t, mine * band, band)
        return send(part, part, xs, xr, n, t, (east, f, z))

    def to_north(n, t):
        part = held(n, t, mine * band, band)
        return send(part, part, ys, yr, n, t, (north, f, z))

    def north_to_east(n, t):
        part = held(n, t, lead_north, shared)
        return send(part, part, xfs, xfr, n, t, (east, f, z))

    def east_to_north(n, t):
        part = held(n, t, lead_east + shared, rest)
        return send(part, part, yfs, yfr, n, t, (north, f, z))

    def across(n, t, src):
        return send(src, held(n, t, 0, depth), cs, cr, n, t, (g, 1 - f, z))

    barrier = pltpu.get_barrier_semaphore()

    def greet(to):
        pl.semaphore_signal(barrier, inc=1, device_id=to, device_id_type=MESH)

    for to in ((east, f, z), (north, f, z), (g, 1 - f, z)):
        greet(to)

    @pl.when(z > 0)
    def _():
        greet((g, f, z - 1))

    @pl.when(z < last)
    def _():
        greet((g, f, z + 1))

    pl.semaphore_wait(barrier, 3 + jnp.minimum(z, 1) + jnp.minimum(last - z, 1))

    load_a = pltpu.make_async_copy(a_in, a_hold, ls.at[0])
    load_m = pltpu.make_async_copy(m_in, m_hold, ls.at[1])
    load_a.start()
    load_m.start()

    items = [(n, k, up) for n in range(3) for k in range(1, last + 1) for up in (True, False)]

    def when_real(k, up, run):
        @pl.when(z - k >= 0 if up else z + k <= last)
        def _():
            run(z - k if up else z + k)

    def own(n):
        @pl.when(z < last)
        def _():
            along(n, z, True, owned(n, z_row, band + shared)).start()

        @pl.when(z > 0)
        def _():
            along(n, z, False, owned(n, z_row, band + shared)).start()

        across(n, z, owned(n, 0, depth)).start()

    def land(n, k, up):
        def run(t):
            along(n, t, up, held(n, t, z_row, band + shared)).wait_recv()

            @pl.when(z < last if up else z > 0)
            def _():
                along(n, t, up, held(n, t, z_row, band + shared)).start()

            to_east(n, t).start()
            to_north(n, t).start()

        when_real(k, up, run)

    def relay(n, k, up):
        def run(t):
            to_east(n, t).wait_recv()
            east_to_north(n, t).start()
            to_north(n, t).wait_recv()
            north_to_east(n, t).start()

        when_real(k, up, run)

    def finish(n, k, up):
        def run(t):
            east_to_north(n, t).wait_recv()
            north_to_east(n, t).wait_recv()
            across(n, t, held(n, t, 0, depth)).start()

        when_real(k, up, run)

    for at in range(len(items) + 4):
        if at % (2 * last) == 0 and at // (2 * last) < 3:
            own(at // (2 * last))
        if at < len(items):
            land(*items[at])
        if 0 <= at - 2 < len(items):
            relay(*items[at - 2])
        if 0 <= at - 4 < len(items):
            finish(*items[at - 4])

    load_a.wait()
    load_m.wait()
    rows = pl.ds(tile(f * depth), depth)
    keep_a = pltpu.make_async_copy(a_hold, a_out.at[z, :, rows, :], ls.at[2])
    keep_m = pltpu.make_async_copy(m_hold, m_out.at[z, :, rows, :], ls.at[3])
    keep_a.start()
    keep_m.start()
    keep_a.wait()
    keep_m.wait()

    for n in range(3):
        @pl.when(z < last)
        def _():
            along(n, z, True, owned(n, z_row, band + shared)).wait_send()

        @pl.when(z > 0)
        def _():
            along(n, z, False, owned(n, z_row, band + shared)).wait_send()

        across(n, z, owned(n, 0, depth)).wait()

    def settle(n, k, up):
        def run(t):
            @pl.when(z < last if up else z > 0)
            def _():
                along(n, t, up, held(n, t, z_row, band + shared)).wait_send()

            to_east(n, t).wait_send()
            to_north(n, t).wait_send()
            east_to_north(n, t).wait_send()
            north_to_east(n, t).wait_send()
            across(n, t, held(n, t, 0, depth)).wait()

        when_real(k, up, run)

    for item in items:
        settle(*item)


def gather(attn_low, mlp_low, shards):
    _, depth, a_cols = attn_low.shape
    _, _, m_cols = mlp_low.shape
    width = 2 * depth
    anywhere = pl.BlockSpec(memory_space=pl.ANY)
    dma = pltpu.SemaphoreType.DMA
    return pl.pallas_call(
        gather_kernel,
        in_specs=[anywhere, anywhere],
        out_specs=[anywhere, anywhere],
        out_shape=[
            jax.ShapeDtypeStruct((shards, 4, width, a_cols), LOW),
            jax.ShapeDtypeStruct((shards, 2, width, m_cols), LOW),
        ],
        scratch_shapes=[
            pltpu.VMEM(attn_low.shape, LOW),
            pltpu.VMEM(mlp_low.shape, LOW),
            dma((3, shards, 2)),
        ]
        + [dma((3, shards))] * 11
        + [dma((4,))],
        compiler_params=pltpu.CompilerParams(
            collective_id=1, has_side_effects=True, vmem_limit_bytes=60 * 2**20
        ),
        name="gather",
    )(attn_low, mlp_low)


def inner_adamw(master, gradient, first, second, step_rate, decay_rate):
    first_moment = 0.9 * first + 0.1 * gradient
    second_moment = 0.95 * second + 0.05 * gradient * gradient
    step_ratio = (
        first_moment / (1.0 - 0.9**STEP) / (jnp.sqrt(second_moment / (1.0 - 0.95**STEP)) + 1e-08)
    )
    return (master - step_rate * (step_ratio + decay_rate * master), second_moment)


def outer_nesterov(master, outer_old, difference):
    momentum = OUTER_MOMENTUM * outer_old + difference
    updated = master - OUTER_RATE * (difference + OUTER_MOMENTUM * momentum)
    return (jnp.stack([difference, momentum, updated]), updated.astype(LOW))


def gather_weights(shard):
    whole = lax.all_gather(shard, "tensor", axis=0)
    return lax.all_gather(whole, "fsdp", axis=2, tiled=True)


def scatter_gradient(gradient):
    half = gradient if gradient.ndim == 4 else lax.psum_scatter(gradient, "fsdp", scatter_dimension=0)
    return lax.psum_scatter(half, "tensor", scatter_dimension=0)


def local(
    patches,
    output_grad,
    live_counts,
    attn_master,
    mlp_master,
    vector_master,
    attn_moments,
    mlp_moments,
    vector_moments,
    attn_outer,
    mlp_outer,
    vector_outer,
):
    vec = vector_master
    tensor_size, fsdp = lax.axis_size("tensor"), lax.axis_size("fsdp")
    groups = lax.axis_size("group")
    local_images, seq, width = patches.shape[2:]
    slot = (lax.axis_index("fsdp") * tensor_size + lax.axis_index("tensor")) * local_images
    slot = slot + jnp.arange(local_images)
    counts = jnp.take(live_counts[0], slot // IMG_DEV, axis=1)
    alive = ((slot % IMG_DEV)[None, :] < counts).astype(F32).reshape(-1)
    x = patches.reshape(-1, seq, width)
    cotangent = output_grad.reshape(-1, seq, width)
    images = x.shape[0]

    if (groups, fsdp) == (4, 2):
        w_attn, w_mlp = gather(attn_master.astype(LOW), mlp_master.astype(LOW), tensor_size)
    else:
        w_attn = gather_weights(attn_master.astype(LOW))
        w_mlp = gather_weights(mlp_master.astype(LOW))

    normed_one, qkv = project(x, w_attn, vec)
    attended = attend(qkv, images, seq)
    resid, normed_two, grad_two = mix(alive, attended, x, cotangent, w_attn, vec)
    bias = vec[8:].reshape(tensor_size, 1, -1)
    carried = None
    mlp_grads, bias_parts = [], []
    for quarter in range(QUARTERS):
        *carried, dw, db = mlp(quarter, QUARTERS, normed_two, grad_two, w_mlp, bias, carried, fsdp)
        mlp_grads.append(scatter_gradient(dw))
        bias_parts.append(db)
    branch, grad_normed = carried
    block_output, grad_resid, grad_attended, dw_out, sums_two = turn(
        alive, resid, branch, grad_normed, grad_two, attended, w_attn, vec, images, seq, fsdp
    )
    out_grad = scatter_gradient(dw_out)
    grads = unattend(qkv, grad_attended, images, seq)
    patches_grad, dw_qkv, sums_one = close(normed_one, grads, w_attn, x, grad_resid, vec, fsdp)
    qkv_grad = scatter_gradient(dw_qkv)

    hidden_bias = jnp.concatenate(bias_parts, axis=-1).reshape(-1, width)
    vector_part = jnp.concatenate([sums_one[:2], sums_two[:2], sums_one[2:], sums_two[2:], hidden_bias])
    vector_grad = lax.psum(vector_part, ("fsdp", "tensor"))

    attn_grad = jnp.concatenate([qkv_grad, out_grad]).astype(F32)
    mlp_grad = jnp.concatenate(mlp_grads, axis=-1).astype(F32)
    attn_first, attn_second = attn_moments[0]
    mlp_first, mlp_second = mlp_moments[0]
    new_attn, second_attn = inner_adamw(
        attn_master, attn_grad, attn_first, attn_second, INNER_RATE, WEIGHT_DECAY
    )
    new_mlp, second_mlp = inner_adamw(mlp_master, mlp_grad, mlp_first, mlp_second, INNER_RATE, WEIGHT_DECAY)
    new_vector, second_vector = inner_adamw(
        vec, vector_grad, vector_moments[0, 0], vector_moments[0, 1], VECTOR_RATE, 0.0
    )
    diff_attn, diff_mlp = lax.psum(((attn_master - new_attn).astype(LOW), (mlp_master - new_mlp).astype(LOW)), "group")
    diff_vector = lax.psum(vec - new_vector, "group")
    attn_state, attn_copy = outer_nesterov(attn_master, attn_outer, diff_attn.astype(F32) / groups)
    mlp_state, mlp_copy = outer_nesterov(mlp_master, mlp_outer, diff_mlp.astype(F32) / groups)
    vector_state, vector_copy = outer_nesterov(vec, vector_outer, diff_vector / groups)
    return (
        block_output.reshape(patches.shape),
        patches_grad.reshape(patches.shape),
        jnp.stack([attn_grad, second_attn])[None],
        attn_state,
        attn_copy,
        jnp.stack([mlp_grad, second_mlp])[None],
        mlp_state,
        mlp_copy,
        jnp.stack([vector_grad, second_vector])[None],
        vector_state,
        vector_copy,
    )


def solution(mesh):
    placed = (
        P("group", None, ("fsdp", "tensor"), None, None),
        P("group", None, ("fsdp", "tensor"), None, None),
        P("group", None, None),
        P(None, "fsdp", "tensor"),
        P(None, "fsdp", "tensor"),
        P(),
        P("group", None, None, "fsdp", "tensor"),
        P("group", None, None, "fsdp", "tensor"),
        P("group", None, None, None),
        P(None, "fsdp", "tensor"),
        P(None, "fsdp", "tensor"),
        P(),
    )
    return jax.shard_map(
        local,
        mesh=mesh,
        in_specs=placed,
        out_specs=(
            P("group", None, ("fsdp", "tensor"), None, None),
            P("group", None, ("fsdp", "tensor"), None, None),
            P("group", None, None, "fsdp", "tensor"),
            P(None, None, "fsdp", "tensor"),
            P(None, "fsdp", "tensor"),
            P("group", None, None, "fsdp", "tensor"),
            P(None, None, "fsdp", "tensor"),
            P(None, "fsdp", "tensor"),
            P("group", None, None, None),
            P(),
            P(),
        ),
        check_vma=False,
    )
```

time: 1130 us -> 638 us (0.56)
  Pallas kernels: 0 us -> 409 us
  waiting for transfers between devices: 474 us -> 73.8 us
  matrix products: 303 us -> 0 us
  other arithmetic: 182 us -> 67.8 us
  local copies, waits for them, and re-layouts: 108 us -> 20.9 us
    pallas_call x0 -> x11, Pallas kernels: none -> 409 us  [the longest x4 140 us: mlp(): pl.pallas_call(functools.partial(mlp_kernel, first, pairwise, rows // 4),...]
    dot_general x17 -> x0, matrix products: 280 us -> none  [the longest x1 39.2 us: local(): jnp.einsum('iqhe,ikhe->ihqk', grad_attended, values, preferred_element_ty...]
    all_gather x8 -> x0, waiting for transfers between devices: 268 us -> none  [the longest x4 251 us: gather_weight(): whole = lax.all_gather(low, 'tensor', axis=2, tiled=True)]
    reduce_scatter x8 -> x6, waiting for transfers between devices: 204 us -> 46.3 us  [scatter_gradient(): return lax.psum_scatter(half, 'tensor', scatter_dimension=0)]
    convert_element_type x11 -> x10, other arithmetic: 115 us -> 40.4 us  [the longest x3 16.9 us: outer_nesterov(): return (jnp.stack([difference, momentum, updated]), updated.astype(LOW))]
    unnamed x157 -> x46, local copies, waits for them, and re-layouts: 53.4 us -> 15.7 us
    slice x11 -> x4, local copies, waits for them, and re-layouts: 37.7 us -> 0.86 us  [the longest x1 0.76 us: local(): bias = vec[8:].reshape(tensor_size, 1, -1)]
    psum x1, waiting for transfers between devices: 0.01 us -> 26.8 us  [local(): lax.psum(((attn_master - new_attn).astype(LOW), (mlp_master - new_mlp).as...]
  transfers between devices with their start and end apart: 17 -> 7, of which waited for: 9 -> 2; matrix products, arithmetic and copies ran while one was open for 36% -> 6% of each run, Pallas kernels for 0% -> 34%
where the time goes in v2:
time: 638 us; the launch traced here: 634 us
  Pallas kernels  409 us (64%)
  waiting for transfers between devices  73.8 us (12%)
  other arithmetic  67.8 us (11%)
  blocking collectives  47.1 us (7%)
  local copies, waits for them, and re-layouts  20.9 us (3%)
  between operations  14.7 us (2%)
    pallas_call x4, Pallas kernels, mlp(): pl.pallas_call(functools.partial(mlp_kernel, first, pairwise, rows // 4),...  140 us
    pallas_call x1, Pallas kernels, gather(): pl.pallas_call(gather_kernel, in_specs=[anywhere, anywhere], out_specs=[a...  102 us
    pallas_call x1, Pallas kernels, unattend(): pl.pallas_call(functools.partial(unattend_kernel, seq), grid=(images, wid...  54.7 us
    reduce_scatter x6, waiting for transfers between devices, scatter_gradient(): return lax.psum_scatter(half, 'tensor', scatter_dimension=0)  46.3 us
    pallas_call x1, Pallas kernels, attend(): pl.pallas_call(functools.partial(attend_kernel, seq), grid=(images, width...  32.6 us
    pallas_call x1, Pallas kernels, close(): pl.pallas_call(functools.partial(close_kernel, seq, images, pairwise), gr...  32.2 us
    psum x1, blocking collectives, local(): vector_grad = lax.psum(vector_part, ('fsdp', 'tensor'))  28.5 us
    psum x1, waiting for transfers between devices, local(): lax.psum(((attn_master - new_attn).astype(LOW), (mlp_master - new_mlp).as...  26.8 us
  transfers between devices with their start and end apart: 7, of which 2 were waited for; matrix products, arithmetic and copies ran while one was open for 6% of the time, Pallas kernels for 34%

profile of v2, /device:TPU:0, one launch (start us, length us, event | category | flops | bytes accessed | tf_op | source)
XLA Modules:
  0.0 633.5 jit_solution(16892746115069929647)
XLA Ops:
  19.0 102.1 %gather.6 = (bf16[4,4,1024,256]{3,2,1,0:T(8,128)(2,1)}, bf16[4,2,1024,1024]{3,2,1,0:T(8,128)(2,1)}) custom-call(bf16[4,512,256]{2,1,0:T(8,128)(2,1)} %convert_element_type.70.a_in, bf16[2,512,1024]{2,1,0:T(8,128)(2,1)} %convert_element_type.71.m_in), custom_call_target="tpu_custom_call" | custom-call | tf_op jit(solution)/shard_map/gather/pallas_call | solution.py:787
  121.1 17.1 %project.1 = (bf16[1184,1024]{1,0:T(8,128)(2,1)}, bf16[3,1184,1024]{2,1,0:T(8,128)(2,1)}) custom-call(bf16[2,577,1024]{2,1,0:T(8,128)(2,1)} %get-tuple-element.124.x_ref, bf16[4,4,1024,256]{3,2,1,0:T(8,128)(2,1)} %get-tuple-element.45.w_ref, f32[12,1024]{1,0:T(8,128)} %vec_ref.7), custom_call_target="tpu_custom_call" | custom-call | flops 7449083904 | bytes 19398656 | tf_op jit(solution)/shard_map/project/pallas_call | solution.py:122
  138.1 32.6 %attend.1.att_ref = bf16[1184,1024]{1,0:T(8,128)(2,1)} custom-call(bf16[3,1184,1024]{2,1,0:T(8,128)(2,1)} %get-tuple-element.46.q_ref.k_ref.v_ref, bf16[3,1184,1024]{2,1,0:T(8,128)(2,1)} %get-tuple-element.46.q_ref.k_ref.v_ref, bf16[3,1184,1024]{2,1,0:T(8,128)(2,1)} %get-tuple-element.46.q_ref.k_ref.v_ref), custom_call_target="tpu_custom_call" | custom-call | flops 11484004352 | bytes 9699328 | tf_op jit(solution)/shard_map/attend/pallas_call | solution.py:176
  171.5 8.9 %mix.1 = (f32[1184,1024]{1,0:T(8,128)}, bf16[1184,1024]{1,0:T(8,128)(2,1)}, bf16[1184,1024]{1,0:T(8,128)(2,1)}) custom-call(f32[2]{0:T(128)} %fusion.36.alive_ref, bf16[1184,1024]{1,0:T(8,128)(2,1)} %attend.1.att_ref, bf16[2,577,1024]{2,1,0:T(8,128)(2,1)} %get-tuple-element.124.x_ref, bf16[2,577,1024]{2,1,0:T(8,128)(2,1)} %get-tuple-element.123.g_ref, ...), custom_call_target="tpu_custom_call" | custom-call | flops 2483027968 | bytes 19398656 | tf_op jit(solution)/shard_map/mix/pallas_call | solution.py:210
  180.4 29.8 %mlp_0.1 = (f32[1184,1024]{1,0:T(8,128)}, f32[1184,1024]{1,0:T(8,128)}, bf16[4,2,512,256]{3,2,1,0:T(8,128)(2,1)}, f32[4,1,256]{2,1,0:T(1,128)}) custom-call(bf16[1184,1024]{1,0:T(8,128)(2,1)} %get-tuple-element.48.n_ref, bf16[1184,1024]{1,0:T(8,128)(2,1)} %get-tuple-element.49.g_ref.g2_ref, bf16[4,2,1024,1024]{3,2,1,0:T(8,128)(2,1)} %get-tuple-element.50.w1_ref.w2_ref, ...), custom_call_target="tpu_custom_call" | custom-call | flops 14898167808 | bytes 29097984 | tf_op jit(solution)/shard_map/mlp_0/pallas_call | solution.py:319
  210.2 44.3 %mlp_1.1 = (f32[1184,1024]{1,0:T(8,128)}, f32[1184,1024]{1,0:T(8,128)}, bf16[4,2,512,256]{3,2,1,0:T(8,128)(2,1)}, f32[4,1,256]{2,1,0:T(1,128)}) custom-call(bf16[1184,1024]{1,0:T(8,128)(2,1)} %get-tuple-element.48.n_ref, bf16[1184,1024]{1,0:T(8,128)(2,1)} %get-tuple-element.49.g_ref.g2_ref, bf16[4,2,1024,1024]{3,2,1,0:T(8,128)(2,1)} %get-tuple-element.50.w1_ref.w2_ref, ...), custom_call_target="tpu_custom_call" | custom-call | flops 14898167808 | bytes 29097984 | tf_op jit(solution)/shard_map/mlp_1/pallas_call | solution.py:319
  254.6 32.7 %mlp_2.1 = (f32[1184,1024]{1,0:T(8,128)}, f32[1184,1024]{1,0:T(8,128)}, bf16[4,2,512,256]{3,2,1,0:T(8,128)(2,1)}, f32[4,1,256]{2,1,0:T(1,128)}) custom-call(bf16[1184,1024]{1,0:T(8,128)(2,1)} %get-tuple-element.48.n_ref, bf16[1184,1024]{1,0:T(8,128)(2,1)} %get-tuple-element.49.g_ref.g2_ref, bf16[4,2,1024,1024]{3,2,1,0:T(8,128)(2,1)} %get-tuple-element.50.w1_ref.w2_ref, ...), custom_call_target="tpu_custom_call" | custom-call | flops 14898167808 | bytes 29097984 | tf_op jit(solution)/shard_map/mlp_2/pallas_call | solution.py:319
  287.3 32.7 %mlp_3.1 = (f32[1184,1024]{1,0:T(8,128)}, f32[1184,1024]{1,0:T(8,128)}, bf16[4,2,512,256]{3,2,1,0:T(8,128)(2,1)}, f32[4,1,256]{2,1,0:T(1,128)}) custom-call(bf16[1184,1024]{1,0:T(8,128)(2,1)} %get-tuple-element.48.n_ref, bf16[1184,1024]{1,0:T(8,128)(2,1)} %get-tuple-element.49.g_ref.g2_ref, bf16[4,2,1024,1024]{3,2,1,0:T(8,128)(2,1)} %get-tuple-element.50.w1_ref.w2_ref, ...), custom_call_target="tpu_custom_call" | custom-call | flops 14898167808 | bytes 29097984 | tf_op jit(solution)/shard_map/mlp_3/pallas_call | solution.py:319
  320.7 21.9 %turn.1 = (bf16[2,577,1024]{2,1,0:T(8,128)(2,1)}, f32[1184,1024]{1,0:T(8,128)}, bf16[1184,1024]{1,0:T(8,128)(2,1)}, bf16[4,1,512,256]{3,2,1,0:T(8,128)(2,1)}, f32[4,1024]{1,0:T(4,128)}) custom-call(f32[2]{0:T(128)} %fusion.36.alive_ref, f32[1184,1024]{1,0:T(8,128)} %get-tuple-element.47.resid_ref, f32[1184,1024]{1,0:T(8,128)} %get-tuple-element.57.y_ref, ...), custom_call_target="tpu_custom_call" | custom-call | flops 4966055936 | bytes 29097984 | tf_op jit(solution)/shard_map/turn/pallas_call | solution.py:414
  342.7 54.7 %unattend.1 = (bf16[1,1184,1024]{2,1,0:T(8,128)(2,1)}, bf16[1,1184,1024]{2,1,0:T(8,128)(2,1)}, bf16[1,1184,1024]{2,1,0:T(8,128)(2,1)}) custom-call(bf16[3,1184,1024]{2,1,0:T(8,128)(2,1)} %get-tuple-element.46.q_ref.k_ref.v_ref, bf16[3,1184,1024]{2,1,0:T(8,128)(2,1)} %get-tuple-element.46.q_ref.k_ref.v_ref, ...), custom_call_target="tpu_custom_call" | custom-call | flops 28710010880 | bytes 16973824 | tf_op jit(solution)/shard_map/unattend/pallas_call | solution.py:479
  397.4 32.2 %close.1 = (f32[2,577,1024]{2,1,0:T(8,128)}, bf16[4,3,512,256]{3,2,1,0:T(8,128)(2,1)}, f32[4,1024]{1,0:T(4,128)}) custom-call(bf16[1184,1024]{1,0:T(8,128)(2,1)} %get-tuple-element.60.n_ref, bf16[1,1184,1024]{2,1,0:T(8,128)(2,1)} %get-tuple-element.62.dq_ref, bf16[1,1184,1024]{2,1,0:T(8,128)(2,1)} %get-tuple-element.63.dk_ref, ...), custom_call_target="tpu_custom_call" | custom-call | flops 14898167808 | bytes 36372480 | tf_op jit(solution)/shard_map/close/pallas_call | solution.py:569
  431.3 3.8 copy.27
  435.2 9.4 %copy.28 = f32[1,2,1,577,1024]{4,2,3,1,0:T(1,128)} copy(f32[1,2,1,577,1024]{4,3,1,2,0:T(8,128)} %bitcast.89) | data formatting | bytes 9453568
  444.8 8.7 %fusion.11 = bf16[2,512,1024]{2,1,0:T(8,128)(2,1)} fusion(f32[2,512,1024]{2,1,0:T(8,128)} %param.16, f32[1,2,2,512,1024]{4,3,2,1,0:T(8,128)} %param.19, bf16[2,512,256]{2,1,0:T(8,128)(2,1)} %bitcast.92, bf16[2,512,256]{2,1,0:T(8,128)(2,1)} %bitcast.93, bf16[2,512,256]{2,1,0:T(8,128)(2,1)} %bitcast.91, bf16[2,512,256]{2,1,0:T(8,128)(2,1)} %bitcast.90), kind=kLoop, calls=%fused_computation.23 | loop fusion | flops 26214400 | bytes 16777216 | tf_op jit(solution)/shard_map/convert_element_type | solution.py:900
  453.5 46.3 %reduce-scatter.7.cloned.1.call-done = bf16[1,3,512,256]{3,2,1,0:T(8,128)(2,1)} async-done(((bf16[4,3,512,256]{3,2,1,0:T(8,128)(2,1)}), bf16[1,3,512,256]{3,2,1,0:T(8,128)(2,1)}) %reduce-scatter.7.cloned.1.call-update) | async-done | bytes 786448 | tf_op jit(solution)/shard_map/reduce_scatter | solution.py:831
  499.7 5.4 fusion.24
  505.3 28.5 %psum.30 = f32[12,1024]{1,0:T(8,128)S(1)} all-reduce(f32[12,1024]{1,0:T(8,128)S(1)} %concatenate.43), channel_id=1, replica_groups=mesh['group'=4,'fsdp'=2,'tensor'=4] {'fsdp','tensor'}, use_global_device_ids=true, to_apply=%region_8.9 | all-reduce | flops 12288 | bytes 98304 | tf_op jit(solution)/shard_map/psum | solution.py:887
  534.7 18.6 %psum.31 = f32[12,1024]{1,0:T(8,128)S(1)} all-reduce(f32[12,1024]{1,0:T(8,128)S(1)} %get-tuple-element.114), channel_id=1, replica_groups=mesh['group'=4,'fsdp'=2,'tensor'=4] {'group'}, use_global_device_ids=true, to_apply=%region_9.10 | all-reduce | flops 12288 | bytes 98304 | tf_op jit(solution)/shard_map/psum | solution.py:901
  560.0 4.4 maximum_bitcast_fusion
  567.2 26.8 %all-reduce.3.cloned.1.call-done = (bf16[4,512,256]{2,1,0:T(8,128)(2,1)}, bf16[2,512,1024]{2,1,0:T(8,128)(2,1)}) async-done(((bf16[4,512,256]{2,1,0:T(8,128)(2,1)}, bf16[2,512,1024]{2,1,0:T(8,128)(2,1)}), (bf16[4,512,256]{2,1,0:T(8,128)(2,1)}, bf16[2,512,1024]{2,1,0:T(8,128)(2,1)})) %all-reduce.3.cloned.1.call-update) | async-done | bytes 3145744 | tf_op jit(solution)/shard_map/psum | solution.py:900
  594.1 5.8 fusion.39
  599.8 10.5 %fusion.41 = (bf16[2,512,1024]{2,1,0:T(8,128)(2,1)}, f32[1,2,512,1024]{3,2,1,0:T(8,128)}, f32[1,2,512,1024]{3,2,1,0:T(8,128)}, f32[1,2,512,1024]{3,2,1,0:T(8,128)}) fusion(f32[2,512,1024]{2,1,0:T(8,128)S(1)} %copy-done, f32[2,512,1024]{2,1,0:T(8,128)} %param.22, bf16[2,512,1024]{2,1,0:T(8,128)(2,1)} %get-tuple-element.102), kind=kLoop, calls=%fused_computation.77 | loop fusion | flops 9437184 | bytes 25165824 | tf_op jit(solution)/shard_map/convert_element_type | solution.py:821
  610.3 5.6 pad_maximum_fusion.1
  615.9 10.5 %pad_maximum_fusion = f32[3,2,512,1024]{3,2,1,0:T(8,128)} fusion(f32[1,2,512,1024]{3,2,1,0:T(8,128)S(1)} %copy-done.2, f32[1,2,512,1024]{3,2,1,0:T(8,128)} %get-tuple-element.105, f32[1,2,512,1024]{3,2,1,0:T(8,128)} %get-tuple-element.109), kind=kLoop, calls=%fused_computation | loop fusion | flops 6291456 | bytes 25165824 | tf_op jit(solution)/shard_map/stack | solution.py:821
  (83 shorter events, 25.5 us)
Async XLA Ops:
  7.2 437.5 %reduce-scatter.11.cloned.1.call-start = ((), (), s32[]{:S(2)}) async-start(), calls=%async_computation.8 | async-start | bytes 2621440 | tf_op jit(solution)/shard_map/reduce_scatter | solution.py:831
  8.6 6.7 %copy-start.8 = (bf16[1,2,1,577,1024]{4,1,3,2,0:T(2,128)(2,1)S(1)}, bf16[1,2,1,577,1024]{4,1,3,2,0:T(2,128)(2,1)}, u32[]{:S(2)}) copy-start(bf16[1,2,1,577,1024]{4,1,3,2,0:T(2,128)(2,1)} %param.13) | copy-start | bytes 7090180
  8.6 6.7 %copy-start.9 = (bf16[1,2,1,577,1024]{4,1,3,2,0:T(2,128)(2,1)S(1)}, bf16[1,2,1,577,1024]{4,1,3,2,0:T(2,128)(2,1)}, u32[]{:S(2)}) copy-start(bf16[1,2,1,577,1024]{4,1,3,2,0:T(2,128)(2,1)} %param.12) | copy-start | bytes 7090180
  138.1 32.6 %copy-start.20 = (s32[1,2,2]{2,1,0:T(2,128)S(1)}, s32[1,2,2]{2,1,0:T(2,128)}, u32[]{:S(2)}) copy-start(s32[1,2,2]{2,1,0:T(2,128)} %param.14) | copy-start | bytes 52
  210.2 234.5 %reduce-scatter.13.cloned.1.call-start = ((), (), s32[]{:S(2)}) async-start(), calls=%async_computation.9 | async-start | bytes 2621440 | tf_op jit(solution)/shard_map/reduce_scatter | solution.py:831
  254.6 190.2 %reduce-scatter.17.cloned.1.call-start = ((), (), s32[]{:S(2)}) async-start(), calls=%async_computation.11 | async-start | bytes 2621440 | tf_op jit(solution)/shard_map/reduce_scatter | solution.py:831
  320.1 124.7 %reduce-scatter.15.cloned.1.call-start = ((), (), s32[]{:S(2)}) async-start(), calls=%async_computation.10 | async-start | bytes 2621440 | tf_op jit(solution)/shard_map/reduce_scatter | solution.py:831
  320.7 132.8 %reduce-scatter.9.cloned.1.call-start = ((), (), s32[]{:S(2)}) async-start(), calls=%async_computation.7 | async-start | bytes 1310720 | tf_op jit(solution)/shard_map/reduce_scatter | solution.py:831
  342.7 157.1 %reduce-scatter.7.cloned.1.call-start = ((), (), s32[]{:S(2)}) async-start(), calls=%async_computation.6 | async-start | bytes 3932160 | tf_op jit(solution)/shard_map/reduce_scatter | solution.py:831
  429.7 164.4 %all-reduce.3.cloned.1.call-start = ((), (), s32[]{:S(2)}) async-start(), calls=%async_computation.12 | async-start | bytes 6291456 | tf_op jit(solution)/shard_map/psum | solution.py:900
  435.2 9.5 %copy-start.16 = (f32[4,1,256]{2,1,0:T(1,128)S(1)}, f32[4,1,256]{2,1,0:T(1,128)}, u32[]{:S(2)}) copy-start(f32[4,1,256]{2,1,0:T(1,128)} %get-tuple-element.75) | copy-start | bytes 12292
  435.2 9.5 %copy-start.17 = (f32[4,1,256]{2,1,0:T(1,128)S(1)}, f32[4,1,256]{2,1,0:T(1,128)}, u32[]{:S(2)}) copy-start(f32[4,1,256]{2,1,0:T(1,128)} %get-tuple-element.76) | copy-start | bytes 12292
  435.2 9.5 %copy-start.18 = (f32[4,1,256]{2,1,0:T(1,128)S(1)}, f32[4,1,256]{2,1,0:T(1,128)}, u32[]{:S(2)}) copy-start(f32[4,1,256]{2,1,0:T(1,128)} %get-tuple-element.77) | copy-start | bytes 12292
  435.2 9.5 %copy-start.19 = (f32[4,1,256]{2,1,0:T(1,128)S(1)}, f32[4,1,256]{2,1,0:T(1,128)}, u32[]{:S(2)}) copy-start(f32[4,1,256]{2,1,0:T(1,128)} %get-tuple-element.78) | copy-start | bytes 12292
  444.8 54.9 %copy-start.1 = (f32[4,512,256]{2,1,0:T(8,128)S(1)}, f32[4,512,256]{2,1,0:T(8,128)}, u32[]{:S(2)}) copy-start(f32[4,512,256]{2,1,0:T(8,128)} %param.15) | copy-start | bytes 6291460
  499.7 5.5 copy-start.15
  499.7 5.5 copy-start.14
  499.7 34.1 %copy-start.12 = (f32[1,2,12,1024]{3,1,2,0:T(2,128)S(1)}, f32[1,2,12,1024]{3,1,2,0:T(2,128)}, u32[]{:S(2)}) copy-start(f32[1,2,12,1024]{3,1,2,0:T(2,128)} %param.20) | copy-start | bytes 294916
  499.7 34.2 %copy-start.11 = (f32[12,1024]{1,0:T(8,128)S(1)}, f32[12,1024]{1,0:T(8,128)}, u32[]{:S(2)}) copy-start(f32[12,1024]{1,0:T(8,128)} %vec_ref.7) | copy-start | bytes 147460
  505.2 48.1 %copy-start.13 = (f32[12,1024]{1,0:T(8,128)S(1)}, f32[12,1024]{1,0:T(8,128)}, u32[]{:S(2)}) copy-start(f32[12,1024]{1,0:T(8,128)} %param.23) | copy-start | bytes 147460
  505.2 49.5 %copy-start.6 = (bf16[1,2,512,256]{3,2,1,0:T(8,128)(2,1)S(1)}, bf16[1,2,512,256]{3,2,1,0:T(8,128)(2,1)}, u32[]{:S(2)}) copy-start(bf16[1,2,512,256]{3,2,1,0:T(8,128)(2,1)} %reduce-scatter.11.cloned.1.call-done) | copy-start | bytes 1572868
  594.1 5.8 copy-start
  599.8 10.5 %copy-start.4 = (f32[1,4,512,256]{3,2,1,0:T(8,128)S(1)}, f32[1,4,512,256]{3,2,1,0:T(8,128)}, u32[]{:S(2)}) copy-start(f32[1,4,512,256]{3,2,1,0:T(8,128)} %get-tuple-element.107) | copy-start | bytes 6291460
  610.3 5.6 copy-start.2
  (4 other events, 15.2 us)
Sparse Core Ops, SparseCore 0:
  210.3 44.1 reduce-scatter.10
  256.9 43.1 reduce-scatter.12
  320.2 44.1 reduce-scatter.16
  366.7 43.1 reduce-scatter.14
  412.0 26.4 reduce-scatter.8
  440.7 58.9 reduce-scatter.6
  505.3 88.7 all-reduce.2

commit v3 on v2

--- a/solution.py
+++ b/solution.py
@@ -17,6 +17,7 @@
 OUTER_RATE = 0.7
 OUTER_MOMENTUM = 0.9
 QUARTERS = 4
+PARTS = 2
 LOW = jnp.bfloat16
 F32 = jnp.float32
 NN = (((1,), (0,)), ((), ()))
@@ -466,72 +467,96 @@
     dv_ref[0] = jnp.where(lane, parts[0][2], parts[1][2]).astype(LOW)
 
 
-def unattend(qkv, grad_attended, images, seq):
+def unattend(qkv, grad_attended, images, seq, part, parts, shards):
     _, rows, width = qkv.shape
     span = rows // images
     pair = 2 * HD
+    each = width // shards // parts // pair
+
+    def spot(h):
+        return (h // each) * (each * parts) + part * each + h % each
 
     def take(j):
-        return pl.BlockSpec((1, span, pair), lambda i, h: (j, i, h))
+        return pl.BlockSpec((1, span, pair), lambda i, h: (j, i, spot(h)))
 
     out = pl.BlockSpec((1, span, pair), lambda i, h: (0, i, h))
-    shape = jax.ShapeDtypeStruct((1, rows, width), LOW)
+    shape = jax.ShapeDtypeStruct((1, rows, width // parts), LOW)
     return pl.pallas_call(
         functools.partial(unattend_kernel, seq),
-        grid=(images, width // pair),
-        in_specs=[take(0), take(1), take(2), pl.BlockSpec((span, pair), lambda i, h: (i, h))],
+        grid=(images, width // pair // parts),
+        in_specs=[take(0), take(1), take(2), pl.BlockSpec((span, pair), lambda i, h: (i, spot(h)))],
         out_specs=[out, out, out],
         out_shape=[shape, shape, shape],
         compiler_params=params(),
-        cost_estimate=cost(40 * rows * span * width, 14 * rows * width, rows * span * (width // HD)),
-        name="unattend",
+        cost_estimate=cost(
+            40 * rows * span * width // parts, 14 * rows * width // parts, rows * span * (width // HD) // parts
+        ),
+        name=f"unattend_{part}",
     )(qkv, qkv, qkv, grad_attended)
 
 
-def close_kernel(seq, images, pairwise, n_ref, dq_ref, dk_ref, dv_ref, w_ref, x_ref, gr_ref, vec_ref,
-                 out_ref, dw_ref, sums_ref, acc_scr, nt_scr, *exchange):
+def close_kernel(seq, images, pairwise, first, final, n_ref, dq_ref, dk_ref, dv_ref, w_ref, *refs):
+    if not first:
+        carry_ref, *refs = refs
+    if final:
+        x_ref, gr_ref, vec_ref, out_ref, norm_ref, *refs = refs
+    else:
+        acc_ref, *refs = refs
+    dw_ref, sums_ref, acc_scr, nt_scr, *exchange = refs
     j = pl.program_id(0)
+    shards, _, _, cols = w_ref.shape
+    span = n_ref.shape[0] // images
     if pairwise:
         own, sent, received, sends, receives = exchange
         pl.when(j == 0)(greet_partner)
-    shards, _, _, cols = w_ref.shape
-    span = n_ref.shape[0] // images
 
     @pl.when(j == 0)
     def _():
         nt_scr[...] = n_ref[...].T
-        acc_scr[...] = jnp.zeros_like(acc_scr)
-        sums_ref[2:3, :] = jnp.sum(dq_ref[0].astype(F32), axis=0, keepdims=True)
-        sums_ref[3:4, :] = jnp.sum(dv_ref[0].astype(F32), axis=0, keepdims=True)
-
-    def part(ref):
+        acc_scr[...] = jnp.zeros_like(acc_scr) if first else carry_ref[...]
+        sums_ref[0:1, :] = jnp.sum(dq_ref[0].astype(F32), axis=0, keepdims=True)
+        sums_ref[1:2, :] = jnp.sum(dv_ref[0].astype(F32), axis=0, keepdims=True)
+
+    def spread(n, total, f=None):
+        for t in range(shards):
+            piece = total[:, t * cols : (t + 1) * cols]
+            if f is None:
+                dw_ref[t, n] = piece
+            else:
+                dw_ref[f, t, 0] = piece
+
+    def step(ref):
+        weight = jnp.concatenate([w_ref[t, 0] for t in range(shards)], axis=1)
         if pairwise:
             ours, theirs = bands(nt_scr.shape[0] // 2)
-            for t in range(shards):
-                sent[j, t] = dot(nt_scr[theirs, :], ref[0, :, t * cols : (t + 1) * cols]).astype(LOW)
+            sent[j] = dot(nt_scr[theirs, :], ref[0]).astype(LOW)
             to_partner(sent, received, sends, receives, j).start()
-        for t in range(shards):
-            block = ref[0, :, t * cols : (t + 1) * cols]
-            acc_scr[...] += dot(block, w_ref[t, 0], NT)
-            if pairwise:
-                own[j, t] = dot(nt_scr[ours, :], block)
-                continue
+            own[j] = dot(nt_scr[ours, :], ref[0])
+        else:
             depth = dw_ref.shape[3]
-            dw = dot(nt_scr[...], block).astype(LOW)
+            dw = dot(nt_scr[...], ref[0]).astype(LOW)
             for f in range(dw_ref.shape[0]):
-                dw_ref[f, t, 0] = dw[f * depth : (f + 1) * depth]
+                spread(0, dw[f * depth : (f + 1) * depth], f)
+        acc_scr[...] += dot(ref[0], weight, NT)
 
     @pl.when(j == 0)
     def _():
-        part(dq_ref)
+        step(dq_ref)
 
     @pl.when(j == 1)
     def _():
-        part(dk_ref)
+        step(dk_ref)
 
     @pl.when(j == 2)
     def _():
-        part(dv_ref)
+        step(dv_ref)
+        if pairwise:
+            for n in range(own.shape[0]):
+                to_partner(sent, received, sends, receives, n).wait()
+                spread(n, (own[n] + received[n].astype(F32)).astype(LOW))
+        if not final:
+            acc_ref[...] = acc_scr[...]
+            return
         gain = jnp.zeros((1, vec_ref.shape[1]), F32)
         shift = jnp.zeros((1, vec_ref.shape[1]), F32)
         for i in range(images):
@@ -540,57 +565,51 @@
             out_ref[i] = gr_ref[i * span : i * span + seq, :] + norm_back(upstream, normal, inverse, vec_ref[0:1])
             gain += jnp.sum(upstream * normal, axis=0, keepdims=True)
             shift += jnp.sum(upstream, axis=0, keepdims=True)
-        sums_ref[0:1, :] = gain
-        sums_ref[1:2, :] = shift
-        if pairwise:
-            for n in range(own.shape[0]):
-                to_partner(sent, received, sends, receives, n).wait()
-                for t in range(shards):
-                    dw_ref[t, n] = (own[n, t] + received[n, t].astype(F32)).astype(LOW)
-
-
-def close(normed, grads, w_attn, patches, grad_resid, vec, fsdp):
-    images, seq, width = patches.shape
-    rows = normed.shape[0]
+        norm_ref[0:1, :] = gain
+        norm_ref[1:2, :] = shift
+
+
+def close(part, parts, normed, grads, w_attn, carry, ending, fsdp, images, seq):
+    rows, width = normed.shape
     shards, _, _, cols = w_attn.shape
+    cols = cols // parts
+    lanes = shards * cols
     depth = width // fsdp
-    pairwise = fsdp == 2
+    pairwise, first, final = fsdp == 2, carry is None, ending is not None
+    single = pl.Buffered(1)
+    stack = pl.BlockSpec((1, rows, lanes), lambda j: (0, 0, 0), pipeline_mode=single)
+    full = pl.BlockSpec((rows, width), lambda j: (0, 0), pipeline_mode=single)
+    image = pl.BlockSpec((images, seq, width), lambda j: (0, 0, 0), pipeline_mode=single)
     if pairwise:
-        dw_spec = pl.BlockSpec((shards, 3, depth, cols), lambda j: (0, 0, 0, 0), pipeline_mode=pl.Buffered(1))
+        dw_spec = pl.BlockSpec((shards, 3, depth, cols), lambda j: (0, 0, 0, 0), pipeline_mode=single)
         dw_shape = jax.ShapeDtypeStruct((shards, 3, depth, cols), LOW)
-        extra = exchange_scratch(3, (shards, depth, cols))
+        extra = exchange_scratch(3, (depth, lanes))
     else:
         dw_spec = pl.BlockSpec((fsdp, shards, 1, depth, cols), lambda j: (0, 0, j, 0, 0))
         dw_shape = jax.ShapeDtypeStruct((fsdp, shards, 3, depth, cols), LOW)
         extra = []
-    single = pl.Buffered(1)
-    stack = pl.BlockSpec((1, rows, width), lambda j: (0, 0, 0), pipeline_mode=single)
-    full = pl.BlockSpec((rows, width), lambda j: (0, 0), pipeline_mode=single)
+    in_specs = [full, stack, stack, stack, pl.BlockSpec((shards, 1, width, cols), lambda j: (0, j, 0, part))]
+    out_specs, out_shape = [], []
+    if not first:
+        in_specs.append(full)
+    if final:
+        in_specs += [image, full, pl.BlockSpec((12, width), lambda j: (0, 0))]
+        out_specs += [image, pl.BlockSpec((2, width), lambda j: (0, 0))]
+        out_shape += [jax.ShapeDtypeStruct((images, seq, width), F32), jax.ShapeDtypeStruct((2, width), F32)]
+    else:
+        out_specs.append(full)
+        out_shape.append(jax.ShapeDtypeStruct((rows, width), F32))
     return pl.pallas_call(
-        functools.partial(close_kernel, seq, images, pairwise),
+        functools.partial(close_kernel, seq, images, pairwise, first, final),
         grid=(3,),
-        in_specs=[
-            full, stack, stack, stack,
-            pl.BlockSpec((shards, 1, width, cols), lambda j: (0, j, 0, 0)),
-            pl.BlockSpec((images, seq, width), lambda j: (0, 0, 0), pipeline_mode=single),
-            full,
-            pl.BlockSpec(vec.shape, lambda j: (0, 0)),
-        ],
-        out_specs=[
-            pl.BlockSpec((images, seq, width), lambda j: (0, 0, 0), pipeline_mode=single),
-            dw_spec,
-            pl.BlockSpec((4, width), lambda j: (0, 0)),
-        ],
-        out_shape=[
-            jax.ShapeDtypeStruct((images, seq, width), F32),
-            dw_shape,
-            jax.ShapeDtypeStruct((4, width), F32),
-        ],
+        in_specs=in_specs,
+        out_specs=[*out_specs, dw_spec, pl.BlockSpec((2, lanes), lambda j: (0, 0))],
+        out_shape=[*out_shape, dw_shape, jax.ShapeDtypeStruct((2, lanes), F32)],
         scratch_shapes=[pltpu.VMEM((rows, width), F32), pltpu.VMEM((width, rows), LOW), *extra],
-        compiler_params=params(7 if pairwise else None),
-        cost_estimate=cost(12 * rows * width * width, 30 * rows * width),
-        name="close",
-    )(normed, *grads, w_attn, patches, grad_resid, vec)
+        compiler_params=params(7 + part if pairwise else None),
+        cost_estimate=cost(12 * rows * width * lanes, 20 * rows * width),
+        name=f"close_{part}",
+    )(normed, *grads, w_attn, *([] if first else [carry]), *(ending if final else []))
 
 
 def gather_kernel(a_in, m_in, a_out, m_out, a_hold, m_hold, zs, zr, xs, xr, ys, yr, xfs, xfr, yfs, yfr, cs, cr, ls):
@@ -817,8 +836,228 @@
 
 def outer_nesterov(master, outer_old, difference):
     momentum = OUTER_MOMENTUM * outer_old + difference
-    updated = master - OUTER_RATE * (difference + OUTER_MOMENTUM * momentum)
-    return (jnp.stack([difference, momentum, updated]), updated.astype(LOW))
+    return momentum, master - OUTER_RATE * (difference + OUTER_MOMENTUM * momentum)
+
+
+def inner_kernel(join, count, *refs):
+    pieces, (master_ref, moment_ref, inner_ref, diff_ref) = refs[:count], refs[count:]
+    gradient = join(*[piece[0] for piece in pieces]).astype(F32)
+    master = master_ref[0]
+    new, second = inner_adamw(master, gradient, moment_ref[0, 0, 0], moment_ref[0, 1, 0], INNER_RATE, WEIGHT_DECAY)
+    inner_ref[0, 0, 0] = gradient
+    inner_ref[0, 1, 0] = second
+    diff_ref[0] = (master - new).astype(LOW)
+
+
+def inner_step(join, places, pieces, master, moments, name):
+    many, depth, cols = master.shape
+    rows = min(depth, 131072 // cols)
+    block = pl.BlockSpec((1, rows, cols), lambda j, r: (j, r, 0))
+    both = pl.BlockSpec((1, 2, 1, rows, cols), lambda j, r: (0, 0, j, r, 0))
+
+    def piece_spec(piece, place):
+        return pl.BlockSpec((1, rows, piece.shape[2]), lambda j, r: (place(j), r, 0))
+
+    return pl.pallas_call(
+        functools.partial(inner_kernel, join, len(pieces)),
+        grid=(many, depth // rows),
+        in_specs=[piece_spec(piece, place) for piece, place in zip(pieces, places)] + [block, both],
+        out_specs=[both, block],
+        out_shape=[jax.ShapeDtypeStruct(moments.shape, F32), jax.ShapeDtypeStruct(master.shape, LOW)],
+        compiler_params=params(),
+        cost_estimate=cost(30 * master.size, 24 * master.size),
+        name=name,
+    )(*pieces, master, moments)
+
+
+def outer_kernel(groups, total_ref, master_ref, outer_ref, state_ref, copy_ref):
+    difference = total_ref[0].astype(F32) / groups
+    momentum, fresh = outer_nesterov(master_ref[0], outer_ref[0], difference)
+    state_ref[0, 0] = difference
+    state_ref[1, 0] = momentum
+    state_ref[2, 0] = fresh
+    copy_ref[0] = fresh.astype(LOW)
+
+
+def outer_step(groups, total, master, outer_old, name):
+    many, depth, cols = master.shape
+    rows = min(depth, 131072 // cols)
+    block = pl.BlockSpec((1, rows, cols), lambda j, r: (j, r, 0))
+    return pl.pallas_call(
+        functools.partial(outer_kernel, groups),
+        grid=(many, depth // rows),
+        in_specs=[block, block, block],
+        out_specs=[pl.BlockSpec((3, 1, rows, cols), lambda j, r: (0, j, r, 0)), block],
+        out_shape=[jax.ShapeDtypeStruct((3, *master.shape), F32), jax.ShapeDtypeStruct(master.shape, LOW)],
+        compiler_params=params(),
+        cost_estimate=cost(10 * master.size, 24 * master.size),
+        name=name,
+    )(total, master, outer_old)
+
+
+def group_kernel(groups, diff_ref, total_ref, landed, summed, sends, receives, sends_two, receives_two):
+    g, f, t = lax.axis_index("group"), lax.axis_index("fsdp"), lax.axis_index("tensor")
+    span = landed.shape[1]
+
+    def rows(n):
+        return pl.ds(pl.multiple_of(n * span, span), span)
+
+    def other(k):
+        return lax.rem(g + k, groups)
+
+    barrier = pltpu.get_barrier_semaphore()
+    for k in range(1, groups):
+        pl.semaphore_signal(barrier, inc=1, device_id=(other(k), f, t), device_id_type=MESH)
+    pl.semaphore_wait(barrier, groups - 1)
+
+    def part(k):
+        return pltpu.make_async_remote_copy(
+            src_ref=diff_ref.at[rows(other(k)), :],
+            dst_ref=landed.at[k],
+            send_sem=sends.at[k],
+            recv_sem=receives.at[k],
+            device_id=(other(k), f, t),
+            device_id_type=MESH,
+        )
+
+    def result(k):
+        return pltpu.make_async_remote_copy(
+            src_ref=summed,
+            dst_ref=landed.at[groups + k],
+            send_sem=sends_two.at[k],
+            recv_sem=receives_two.at[k],
+            device_id=(other(k), f, t),
+            device_id_type=MESH,
+        )
+
+    for k in range(1, groups):
+        part(k).start()
+    total = diff_ref[rows(g), :].astype(F32)
+    for k in range(1, groups):
+        part(k).wait_recv()
+        total = total + landed[k].astype(F32)
+    summed[...] = total.astype(LOW)
+    for k in range(1, groups):
+        result(k).start()
+    total_ref[rows(g), :] = summed[...]
+    for k in range(1, groups):
+        result(k).wait_recv()
+        total_ref[rows(lax.rem(g + groups - k, groups)), :] = landed[groups + k]
+    for k in range(1, groups):
+        part(k).wait_send()
+        result(k).wait_send()
+
+
+def group_sum(diff, groups, identity, name):
+    flat = diff.reshape(-1, diff.shape[-1])
+    span, cols = flat.shape[0] // groups, flat.shape[1]
+    dma = pltpu.SemaphoreType.DMA
+    whole = pl.BlockSpec(memory_space=pltpu.VMEM)
+    total = pl.pallas_call(
+        functools.partial(group_kernel, groups),
+        in_specs=[whole],
+        out_specs=whole,
+        out_shape=jax.ShapeDtypeStruct(flat.shape, LOW),
+        scratch_shapes=[
+            pltpu.VMEM((2 * groups, span, cols), LOW),
+            pltpu.VMEM((span, cols), LOW),
+            *[dma((groups,))] * 4,
+        ],
+        compiler_params=params(identity),
+        cost_estimate=cost(4 * flat.size, 8 * flat.size),
+        name=name,
+    )(flat)
+    return total.reshape(diff.shape)
+
+
+def vector_kernel(groups, shards, fsdp, part_ref, master_ref, moment_ref, outer_ref, inner_ref, state_ref, copy_ref,
+                  landed, mine, sends, receives, sends_two, receives_two):
+    g, f, t = lax.axis_index("group"), lax.axis_index("fsdp"), lax.axis_index("tensor")
+    me = f * shards + t
+    members = fsdp * shards
+
+    def place(k):
+        at = lax.rem(me + k, members)
+        return (g, at // shards, at % shards)
+
+    def column(k):
+        return (lax.rem(g + k, groups), f, t)
+
+    barrier = pltpu.get_barrier_semaphore()
+    for k in range(1, members):
+        pl.semaphore_signal(barrier, inc=1, device_id=place(k), device_id_type=MESH)
+    for k in range(1, groups):
+        pl.semaphore_signal(barrier, inc=1, device_id=column(k), device_id_type=MESH)
+    pl.semaphore_wait(barrier, members + groups - 2)
+
+    def part(k):
+        return pltpu.make_async_remote_copy(
+            src_ref=part_ref, dst_ref=landed.at[k], send_sem=sends.at[k], recv_sem=receives.at[k],
+            device_id=place(k), device_id_type=MESH,
+        )
+
+    def share(k):
+        return pltpu.make_async_remote_copy(
+            src_ref=mine, dst_ref=landed.at[members + k], send_sem=sends_two.at[k], recv_sem=receives_two.at[k],
+            device_id=column(k), device_id_type=MESH,
+        )
+
+    for k in range(1, members):
+        part(k).start()
+    landed[0] = part_ref[...]
+    for k in range(1, members):
+        part(k).wait_recv()
+    gradient = jnp.zeros(part_ref.shape, F32)
+    for n in range(members):
+        gradient = gradient + landed[lax.rem(me + members - n, members)]
+    master = master_ref[...]
+    new, second = inner_adamw(master, gradient, moment_ref[0], moment_ref[1], VECTOR_RATE, 0.0)
+    inner_ref[0] = gradient
+    inner_ref[1] = second
+    mine[...] = master - new
+    for k in range(1, groups):
+        share(k).start()
+    landed[members] = mine[...]
+    for k in range(1, groups):
+        share(k).wait_recv()
+    difference = jnp.zeros(part_ref.shape, F32)
+    for n in range(groups):
+        difference = difference + landed[members + lax.rem(g + groups - n, groups)]
+    difference = difference / groups
+    momentum, fresh = outer_nesterov(master, outer_ref[...], difference)
+    state_ref[0] = difference
+    state_ref[1] = momentum
+    state_ref[2] = fresh
+    copy_ref[...] = fresh.astype(LOW)
+    for k in range(1, members):
+        part(k).wait_send()
+    for k in range(1, groups):
+        share(k).wait_send()
+
+
+def vector_step(part, master, moments, outer_old, groups, shards, fsdp, identity):
+    dma = pltpu.SemaphoreType.DMA
+    whole = pl.BlockSpec(memory_space=pltpu.VMEM)
+    return pl.pallas_call(
+        functools.partial(vector_kernel, groups, shards, fsdp),
+        in_specs=[whole] * 4,
+        out_specs=[whole] * 3,
+        out_shape=[
+            jax.ShapeDtypeStruct((2, *part.shape), F32),
+            jax.ShapeDtypeStruct((3, *part.shape), F32),
+            jax.ShapeDtypeStruct(part.shape, LOW),
+        ],
+        scratch_shapes=[
+            pltpu.VMEM((fsdp * shards + groups, *part.shape), F32),
+            pltpu.VMEM(part.shape, F32),
+            dma((fsdp * shards,)),
+            dma((fsdp * shards,)),
+            dma((groups,)),
+            dma((groups,)),
+        ],
+        compiler_params=params(identity),
+        name="vector_step",
+    )(part, master, moments, outer_old)
 
 
 def gather_weights(shard):
@@ -870,48 +1109,78 @@
     carried = None
     mlp_grads, bias_parts = [], []
     for quarter in range(QUARTERS):
+        if quarter == 3:
+            carried[0], mlp_grads[0] = lax.optimization_barrier((carried[0], mlp_grads[0]))
         *carried, dw, db = mlp(quarter, QUARTERS, normed_two, grad_two, w_mlp, bias, carried, fsdp)
         mlp_grads.append(scatter_gradient(dw))
         bias_parts.append(db)
     branch, grad_normed = carried
+    branch, mlp_grads[1] = lax.optimization_barrier((branch, mlp_grads[1]))
     block_output, grad_resid, grad_attended, dw_out, sums_two = turn(
         alive, resid, branch, grad_normed, grad_two, attended, w_attn, vec, images, seq, fsdp
     )
     out_grad = scatter_gradient(dw_out)
-    grads = unattend(qkv, grad_attended, images, seq)
-    patches_grad, dw_qkv, sums_one = close(normed_one, grads, w_attn, x, grad_resid, vec, fsdp)
-    qkv_grad = scatter_gradient(dw_qkv)
-
+    qkv_grads, head_sums, carry = [], [], None
+    for part in range(PARTS):
+        grads = unattend(qkv, grad_attended, images, seq, part, PARTS, tensor_size)
+        final = part == PARTS - 1
+        head_grad, mlp_grads[2 + part] = lax.optimization_barrier((grads[0], mlp_grads[2 + part]))
+        grads = (head_grad, *grads[1:])
+        ending = [x, grad_resid, vec] if final else None
+        *carry, dw_qkv, sums = close(part, PARTS, normed_one, grads, w_attn, carry, ending, fsdp, images, seq)
+        if not final:
+            (carry,) = carry
+        qkv_grads.append(scatter_gradient(dw_qkv))
+        head_sums.append(sums.reshape(2, tensor_size, -1))
+    patches_grad, sums_one = carry
+
+    head_rows = jnp.concatenate(head_sums, axis=-1).reshape(2, width)
     hidden_bias = jnp.concatenate(bias_parts, axis=-1).reshape(-1, width)
-    vector_part = jnp.concatenate([sums_one[:2], sums_two[:2], sums_one[2:], sums_two[2:], hidden_bias])
-    vector_grad = lax.psum(vector_part, ("fsdp", "tensor"))
-
-    attn_grad = jnp.concatenate([qkv_grad, out_grad]).astype(F32)
-    mlp_grad = jnp.concatenate(mlp_grads, axis=-1).astype(F32)
-    attn_first, attn_second = attn_moments[0]
-    mlp_first, mlp_second = mlp_moments[0]
-    new_attn, second_attn = inner_adamw(
-        attn_master, attn_grad, attn_first, attn_second, INNER_RATE, WEIGHT_DECAY
+    vector_part = jnp.concatenate([sums_one, sums_two[:2], head_rows, sums_two[2:], hidden_bias])
+    if fsdp == 2:
+        vector_inner, vector_state, vector_copy = vector_step(
+            vector_part, vec, vector_moments[0], vector_outer, groups, tensor_size, fsdp, 12
+        )
+    else:
+        vector_grad = lax.psum(vector_part, ("fsdp", "tensor"))
+        new_vector, second_vector = inner_adamw(
+            vec, vector_grad, vector_moments[0, 0], vector_moments[0, 1], VECTOR_RATE, 0.0
+        )
+        diff_vector = lax.psum(vec - new_vector, "group") / groups
+        momentum, fresh = outer_nesterov(vec, vector_outer, diff_vector)
+        vector_inner = jnp.stack([vector_grad, second_vector])
+        vector_state, vector_copy = jnp.stack([diff_vector, momentum, fresh]), fresh.astype(LOW)
+
+    def beside(*parts):
+        return jnp.concatenate(parts, axis=-1)
+
+    def beside_or_last(*parts):
+        return jnp.where(pl.program_id(0) == 3, parts[-1], beside(*parts[:-1]))
+
+    mlp_inner, mlp_diff = inner_step(beside, [lambda j: j] * QUARTERS, mlp_grads, mlp_master, mlp_moments, "inner_mlp")
+    mlp_total = group_sum(mlp_diff, groups, 10, "group_mlp")
+    mlp_state, mlp_copy = outer_step(groups, mlp_total, mlp_master, mlp_outer, "outer_mlp")
+    out_grad, mlp_state = lax.optimization_barrier((out_grad, mlp_state))
+    attn_inner, attn_diff = inner_step(
+        beside_or_last,
+        [lambda j: jnp.minimum(j, 2)] * PARTS + [lambda j: 0],
+        [*qkv_grads, out_grad],
+        attn_master,
+        attn_moments,
+        "inner_attn",
     )
-    new_mlp, second_mlp = inner_adamw(mlp_master, mlp_grad, mlp_first, mlp_second, INNER_RATE, WEIGHT_DECAY)
-    new_vector, second_vector = inner_adamw(
-        vec, vector_grad, vector_moments[0, 0], vector_moments[0, 1], VECTOR_RATE, 0.0
-    )
-    diff_attn, diff_mlp = lax.psum(((attn_master - new_attn).astype(LOW), (mlp_master - new_mlp).astype(LOW)), "group")
-    diff_vector = lax.psum(vec - new_vector, "group")
-    attn_state, attn_copy = outer_nesterov(attn_master, attn_outer, diff_attn.astype(F32) / groups)
-    mlp_state, mlp_copy = outer_nesterov(mlp_master, mlp_outer, diff_mlp.astype(F32) / groups)
-    vector_state, vector_copy = outer_nesterov(vec, vector_outer, diff_vector / groups)
+    attn_total = group_sum(attn_diff, groups, 11, "group_attn")
+    attn_state, attn_copy = outer_step(groups, attn_total, attn_master, attn_outer, "outer_attn")
     return (
         block_output.reshape(patches.shape),
         patches_grad.reshape(patches.shape),
-        jnp.stack([attn_grad, second_attn])[None],
+        attn_inner,
         attn_state,
         attn_copy,
-        jnp.stack([mlp_grad, second_mlp])[None],
+        mlp_inner,
         mlp_state,
         mlp_copy,
-        jnp.stack([vector_grad, second_vector])[None],
+        vector_inner[None],
         vector_state,
         vector_copy,
     )

time: 638 us -> 605 us (0.948)
  Pallas kernels: 409 us -> 555 us
  waiting for transfers between devices: 73.8 us -> 0.2 us
  other arithmetic: 67.8 us -> 7.36 us
  blocking collectives: 47.1 us -> 0 us
    pallas_call x1 -> x9, Pallas kernels: 32.2 us -> 188 us  [the longest x2 82.4 us: group_sum(): pl.pallas_call(functools.partial(group_kernel, groups), in_specs=[whole],...]
    psum x2 -> x0, blocking collectives: 47.1 us -> none  [the longest x1 28.5 us: local(): vector_grad = lax.psum(vector_part, ('fsdp', 'tensor'))]
    reduce_scatter x6 -> x7, waiting for transfers between devices: 46.3 us -> 0.08 us  [scatter_gradient(): return lax.psum_scatter(half, 'tensor', scatter_dimension=0)]
    convert_element_type x7 -> x0, other arithmetic: 33.1 us -> none  [the longest x3 16.9 us: outer_nesterov(): return (jnp.stack([difference, momentum, updated]), updated.astype(LOW))]
    psum x1 -> x0, waiting for transfers between devices: 26.8 us -> none  [local(): lax.psum(((attn_master - new_attn).astype(LOW), (mlp_master - new_mlp).as...]
    another operation x3 -> x0, other arithmetic: 16.8 us -> none  [outer_nesterov(): return (jnp.stack([difference, momentum, updated]), updated.astype(LOW))]
    pallas_call x4, Pallas kernels: 140 us -> 128 us  [mlp(): pl.pallas_call(functools.partial(mlp_kernel, first, pairwise, rows // 4),...]
    broadcast_in_dim x3 -> x0, other arithmetic: 6.73 us -> none  [the longest x1 4.43 us: local(): jnp.stack([mlp_grad, second_mlp])[None]]
  transfers between devices with their start and end apart: 7 -> 7, of which waited for: 2 -> 0; matrix products, arithmetic and copies ran while one was open for 6% -> 3% of each run, Pallas kernels for 34% -> 53%
where the time goes in v3:
time: 605 us; the launch traced here: 601 us
  Pallas kernels  555 us (92%)
  local copies, waits for them, and re-layouts  23.3 us (4%)
  between operations  14.7 us (2%)
  other arithmetic  7.36 us (1%)
    pallas_call x4, Pallas kernels, mlp(): pl.pallas_call(functools.partial(mlp_kernel, first, pairwise, rows // 4),...  128 us
    pallas_call x1, Pallas kernels, gather(): pl.pallas_call(gather_kernel, in_specs=[anywhere, anywhere], out_specs=[a...  102 us
    pallas_call x2, Pallas kernels, group_sum(): pl.pallas_call(functools.partial(group_kernel, groups), in_specs=[whole],...  82.4 us
    pallas_call x2, Pallas kernels, unattend(): pl.pallas_call(functools.partial(unattend_kernel, seq), grid=(images, wid...  57.1 us
    pallas_call x2, Pallas kernels, close(): pl.pallas_call(functools.partial(close_kernel, seq, images, pairwise, fir...  41.2 us
    pallas_call x1, Pallas kernels, attend(): pl.pallas_call(functools.partial(attend_kernel, seq), grid=(images, width...  32.6 us
    pallas_call x1, Pallas kernels, vector_step(): pl.pallas_call(functools.partial(vector_kernel, groups, shards, fsdp), in...  26.7 us
    pallas_call x1, Pallas kernels, turn(): pl.pallas_call(functools.partial(turn_kernel, seq, pairwise), grid=(image...  21.3 us
  transfers between devices with their start and end apart: 7, of which 0 were waited for; matrix products, arithmetic and copies ran while one was open for 3% of the time, Pallas kernels for 53%

profile of v3, /device:TPU:0, one launch (start us, length us, event | category | flops | bytes accessed | tf_op | source)
XLA Modules:
  0.0 601.0 jit_solution(13341371886787658686)
XLA Ops:
  11.3 4.0 convert_element_type.18.m_in
  15.3 3.6 copy_bitcast_fusion
  18.9 102.1 %gather.6 = (bf16[4,4,1024,256]{3,2,1,0:T(8,128)(2,1)}, bf16[4,2,1024,1024]{3,2,1,0:T(8,128)(2,1)}) custom-call(bf16[4,512,256]{2,1,0:T(8,128)(2,1)} %convert_element_type.17.a_in, bf16[2,512,1024]{2,1,0:T(8,128)(2,1)} %convert_element_type.18.m_in), custom_call_target="tpu_custom_call" | custom-call | tf_op jit(solution)/shard_map/gather/pallas_call | solution.py:806
  121.1 17.2 %project.1 = (bf16[1184,1024]{1,0:T(8,128)(2,1)}, bf16[3,1184,1024]{2,1,0:T(8,128)(2,1)}) custom-call(bf16[2,577,1024]{2,1,0:T(8,128)(2,1)} %get-tuple-element.160.x_ref.refs_1_, bf16[4,4,1024,256]{3,2,1,0:T(8,128)(2,1)} %get-tuple-element.73.w_ref, f32[12,1024]{1,0:T(8,128)} %master_ref.5), custom_call_target="tpu_custom_call" | custom-call | flops 7449083904 | bytes 19398656 | tf_op jit(solution)/shard_map/project/pallas_call | solution.py:123
  138.2 32.6 %attend.1.att_ref = bf16[1184,1024]{1,0:T(8,128)(2,1)} custom-call(bf16[3,1184,1024]{2,1,0:T(8,128)(2,1)} %get-tuple-element.74.q_ref.k_ref.v_ref, bf16[3,1184,1024]{2,1,0:T(8,128)(2,1)} %get-tuple-element.74.q_ref.k_ref.v_ref, bf16[3,1184,1024]{2,1,0:T(8,128)(2,1)} %get-tuple-element.74.q_ref.k_ref.v_ref), custom_call_target="tpu_custom_call" | custom-call | flops 11484004352 | bytes 9699328 | tf_op jit(solution)/shard_map/attend/pallas_call | solution.py:177
  171.6 8.9 %mix.1 = (f32[1184,1024]{1,0:T(8,128)}, bf16[1184,1024]{1,0:T(8,128)(2,1)}, bf16[1184,1024]{1,0:T(8,128)(2,1)}) custom-call(f32[2]{0:T(128)} %fusion.alive_ref, bf16[1184,1024]{1,0:T(8,128)(2,1)} %attend.1.att_ref, bf16[2,577,1024]{2,1,0:T(8,128)(2,1)} %get-tuple-element.160.x_ref.refs_1_, bf16[2,577,1024]{2,1,0:T(8,128)(2,1)} %get-tuple-element.159.g_ref, ...), custom_call_target="tpu_custom_call" | custom-call | flops 2483027968 | bytes 19398656 | tf_op jit(solution)/shard_map/mix/pallas_call | solution.py:211
  180.5 29.8 %mlp_0.1 = (f32[1184,1024]{1,0:T(8,128)}, f32[1184,1024]{1,0:T(8,128)}, bf16[4,2,512,256]{3,2,1,0:T(8,128)(2,1)}, f32[4,1,256]{2,1,0:T(1,128)}) custom-call(bf16[1184,1024]{1,0:T(8,128)(2,1)} %get-tuple-element.76.n_ref, bf16[1184,1024]{1,0:T(8,128)(2,1)} %get-tuple-element.77.g_ref.g2_ref, bf16[4,2,1024,1024]{3,2,1,0:T(8,128)(2,1)} %get-tuple-element.78.w1_ref.w2_ref, ...), custom_call_target="tpu_custom_call" | custom-call | flops 14898167808 | bytes 29097984 | tf_op jit(solution)/shard_map/mlp_0/pallas_call | solution.py:320
  210.4 32.8 %mlp_1.1 = (f32[1184,1024]{1,0:T(8,128)}, f32[1184,1024]{1,0:T(8,128)}, bf16[4,2,512,256]{3,2,1,0:T(8,128)(2,1)}, f32[4,1,256]{2,1,0:T(1,128)}) custom-call(bf16[1184,1024]{1,0:T(8,128)(2,1)} %get-tuple-element.76.n_ref, bf16[1184,1024]{1,0:T(8,128)(2,1)} %get-tuple-element.77.g_ref.g2_ref, bf16[4,2,1024,1024]{3,2,1,0:T(8,128)(2,1)} %get-tuple-element.78.w1_ref.w2_ref, ...), custom_call_target="tpu_custom_call" | custom-call | flops 14898167808 | bytes 29097984 | tf_op jit(solution)/shard_map/mlp_1/pallas_call | solution.py:320
  243.3 32.7 %mlp_2.1 = (f32[1184,1024]{1,0:T(8,128)}, f32[1184,1024]{1,0:T(8,128)}, bf16[4,2,512,256]{3,2,1,0:T(8,128)(2,1)}, f32[4,1,256]{2,1,0:T(1,128)}) custom-call(bf16[1184,1024]{1,0:T(8,128)(2,1)} %get-tuple-element.76.n_ref, bf16[1184,1024]{1,0:T(8,128)(2,1)} %get-tuple-element.77.g_ref.g2_ref, bf16[4,2,1024,1024]{3,2,1,0:T(8,128)(2,1)} %get-tuple-element.78.w1_ref.w2_ref, ...), custom_call_target="tpu_custom_call" | custom-call | flops 14898167808 | bytes 29097984 | tf_op jit(solution)/shard_map/mlp_2/pallas_call | solution.py:320
  276.1 33.0 %mlp_3.1 = (f32[1184,1024]{1,0:T(8,128)}, f32[1184,1024]{1,0:T(8,128)}, bf16[4,2,512,256]{3,2,1,0:T(8,128)(2,1)}, f32[4,1,256]{2,1,0:T(1,128)}) custom-call(bf16[1184,1024]{1,0:T(8,128)(2,1)} %get-tuple-element.76.n_ref, bf16[1184,1024]{1,0:T(8,128)(2,1)} %get-tuple-element.77.g_ref.g2_ref, bf16[4,2,1024,1024]{3,2,1,0:T(8,128)(2,1)} %get-tuple-element.78.w1_ref.w2_ref, ...), custom_call_target="tpu_custom_call" | custom-call | flops 14898167808 | bytes 29097984 | tf_op jit(solution)/shard_map/mlp_3/pallas_call | solution.py:320
  309.2 21.3 %turn.1 = (bf16[2,577,1024]{2,1,0:T(8,128)(2,1)}, f32[1184,1024]{1,0:T(8,128)}, bf16[1184,1024]{1,0:T(8,128)(2,1)}, bf16[4,1,512,256]{3,2,1,0:T(8,128)(2,1)}, f32[4,1024]{1,0:T(4,128)}) custom-call(f32[2]{0:T(128)} %fusion.alive_ref, f32[1184,1024]{1,0:T(8,128)} %get-tuple-element.75.resid_ref, f32[1184,1024]{1,0:T(8,128)} %get-tuple-element.89.y_ref, ...), custom_call_target="tpu_custom_call" | custom-call | flops 4966055936 | bytes 29097984 | tf_op jit(solution)/shard_map/turn/pallas_call | solution.py:415
  330.6 28.8 %unattend_0.1 = (bf16[1,1184,512]{2,1,0:T(8,128)(2,1)}, bf16[1,1184,512]{2,1,0:T(8,128)(2,1)}, bf16[1,1184,512]{2,1,0:T(8,128)(2,1)}) custom-call(bf16[3,1184,1024]{2,1,0:T(8,128)(2,1)} %get-tuple-element.74.q_ref.k_ref.v_ref, bf16[3,1184,1024]{2,1,0:T(8,128)(2,1)} %get-tuple-element.74.q_ref.k_ref.v_ref, ...), custom_call_target="tpu_custom_call" | custom-call | flops 14355005440 | bytes 8486912 | tf_op jit(solution)/shard_map/unattend_0/pallas_call | solution.py:484
  359.4 16.9 %close_0.1 = (f32[1184,1024]{1,0:T(8,128)}, bf16[4,3,512,128]{3,2,1,0:T(8,128)(2,1)}, f32[2,512]{1,0:T(2,128)}) custom-call(bf16[1184,1024]{1,0:T(8,128)(2,1)} %get-tuple-element.92.n_ref, bf16[1,1184,512]{2,1,0:T(8,128)(2,1)} %get-tuple-element.101.dq_ref, bf16[1,1184,512]{2,1,0:T(8,128)(2,1)} %get-tuple-element.102.dk_ref, ...), custom_call_target="tpu_custom_call" | custom-call | flops 7449083904 | bytes 24248320 | tf_op jit(solution)/shard_map/close_0/pallas_call | solution.py:602
  376.3 28.3 %unattend_1.1 = (bf16[1,1184,512]{2,1,0:T(8,128)(2,1)}, bf16[1,1184,512]{2,1,0:T(8,128)(2,1)}, bf16[1,1184,512]{2,1,0:T(8,128)(2,1)}) custom-call(bf16[3,1184,1024]{2,1,0:T(8,128)(2,1)} %get-tuple-element.74.q_ref.k_ref.v_ref, bf16[3,1184,1024]{2,1,0:T(8,128)(2,1)} %get-tuple-element.74.q_ref.k_ref.v_ref, ...), custom_call_target="tpu_custom_call" | custom-call | flops 14355005440 | bytes 8486912 | tf_op jit(solution)/shard_map/unattend_1/pallas_call | solution.py:484
  404.7 24.3 %close_1.1 = (f32[2,577,1024]{2,1,0:T(8,128)}, f32[2,1024]{1,0:T(2,128)}, bf16[4,3,512,128]{3,2,1,0:T(8,128)(2,1)}, f32[2,512]{1,0:T(2,128)}) custom-call(bf16[1184,1024]{1,0:T(8,128)(2,1)} %get-tuple-element.92.n_ref, bf16[1,1184,512]{2,1,0:T(8,128)(2,1)} %get-tuple-element.96.dq_ref, bf16[1,1184,512]{2,1,0:T(8,128)(2,1)} %get-tuple-element.97.dk_ref, ...), custom_call_target="tpu_custom_call" | custom-call | flops 7449083904 | bytes 24248320 | tf_op jit(solution)/shard_map/close_1/pallas_call | solution.py:602
  429.9 3.8 copy.30
  433.8 9.4 %copy.31 = f32[1,2,1,577,1024]{4,2,3,1,0:T(1,128)} copy(f32[1,2,1,577,1024]{4,3,1,2,0:T(8,128)} %bitcast.31) | data formatting | bytes 9453568
  444.6 26.7 %vector_step.1 = (f32[2,12,1024]{2,1,0:T(8,128)}, f32[3,12,1024]{2,1,0:T(8,128)}, bf16[12,1024]{1,0:T(8,128)(2,1)}) custom-call(f32[12,1024]{1,0:T(8,128)} %concatenate.11.part_ref, f32[12,1024]{1,0:T(8,128)} %master_ref.5, f32[2,12,1024]{2,1,0:T(8,128)} %bitcast.40, f32[12,1024]{1,0:T(8,128)} %outer_ref.5), custom_call_target="tpu_custom_call" | custom-call | tf_op jit(solution)/shard_map/vector_step/pallas_call | solution.py:1041
  472.8 13.1 %inner_mlp.1 = (f32[1,2,2,512,1024]{4,3,2,1,0:T(8,128)}, bf16[2,512,1024]{2,1,0:T(8,128)(2,1)}) custom-call(bf16[2,512,256]{2,1,0:T(8,128)(2,1)} %bitcast.36, bf16[2,512,256]{2,1,0:T(8,128)(2,1)} %bitcast.37, bf16[2,512,256]{2,1,0:T(8,128)(2,1)} %bitcast.38, bf16[2,512,256]{2,1,0:T(8,128)(2,1)} %bitcast.39, f32[2,512,1024]{2,1,0:T(8,128)} %master_ref.3, ...), custom_call_target="tpu_custom_call" | custom-call | flops 31457280 | bytes 25165824 | tf_op jit(solution)/shard_map/inner_mlp/pallas_call | solution.py:861
  485.9 52.3 %group_mlp.1 = bf16[1024,1024]{1,0:T(8,128)(2,1)} custom-call(bf16[1024,1024]{1,0:T(8,128)(2,1)} %bitcast.34), custom_call_target="tpu_custom_call" | custom-call | flops 4194304 | bytes 8388608 | tf_op jit(solution)/shard_map/group_mlp/pallas_call | solution.py:956
  538.2 11.2 %outer_mlp.1 = (f32[3,2,512,1024]{3,2,1,0:T(8,128)}, bf16[2,512,1024]{2,1,0:T(8,128)(2,1)}) custom-call(bf16[2,512,1024]{2,1,0:T(8,128)(2,1)} %bitcast.30, f32[2,512,1024]{2,1,0:T(8,128)} %master_ref.3, f32[2,512,1024]{2,1,0:T(8,128)} %outer_ref.3), custom_call_target="tpu_custom_call" | custom-call | flops 10485760 | bytes 25165824 | tf_op jit(solution)/shard_map/outer_mlp/pallas_call | solution.py:886
  549.4 7.0 %inner_attn.1 = (f32[1,2,4,512,256]{4,3,2,1,0:T(8,128)}, bf16[4,512,256]{2,1,0:T(8,128)(2,1)}) custom-call(bf16[3,512,128]{2,1,0:T(8,128)(2,1)} %bitcast.41, bf16[3,512,128]{2,1,0:T(8,128)(2,1)} %bitcast.42, bf16[1,512,256]{2,1,0:T(8,128)(2,1)} %bitcast.43, f32[4,512,256]{2,1,0:T(8,128)} %master_ref.4, f32[1,2,4,512,256]{4,3,2,1,0:T(8,128)} %refs_4_.3), custom_call_target="tpu_custom_call" | custom-call | flops 15728640 | bytes 12582912 | tf_op jit(solution)/shard_map/inner_attn/pallas_call | solution.py:861
  556.4 30.1 %group_attn.1 = bf16[2048,256]{1,0:T(8,128)(2,1)} custom-call(bf16[2048,256]{1,0:T(8,128)(2,1)} %bitcast.35), custom_call_target="tpu_custom_call" | custom-call | flops 2097152 | bytes 4194304 | tf_op jit(solution)/shard_map/group_attn/pallas_call | solution.py:956
  586.5 6.1 %outer_attn.1 = (f32[3,4,512,256]{3,2,1,0:T(8,128)}, bf16[4,512,256]{2,1,0:T(8,128)(2,1)}) custom-call(bf16[4,512,256]{2,1,0:T(8,128)(2,1)} %bitcast.32, f32[4,512,256]{2,1,0:T(8,128)} %master_ref.4, f32[4,512,256]{2,1,0:T(8,128)} %outer_ref.4), custom_call_target="tpu_custom_call" | custom-call | flops 5242880 | bytes 12582912 | tf_op jit(solution)/shard_map/outer_attn/pallas_call | solution.py:886
  (70 shorter events, 10.2 us)
Async XLA Ops:
  7.2 268.9 %reduce-scatter.8.cloned.1.call-start = ((), (), s32[]{:S(2)}) async-start(), calls=%async_computation.7 | async-start | bytes 2621440 | tf_op jit(solution)/shard_map/reduce_scatter | solution.py:1070
  11.3 4.0 copy-start.1
  11.3 4.0 copy-start.2
  138.2 32.6 %copy-start.14 = (s32[1,2,2]{2,1,0:T(2,128)S(1)}, s32[1,2,2]{2,1,0:T(2,128)}, u32[]{:S(2)}) copy-start(s32[1,2,2]{2,1,0:T(2,128)} %param.14) | copy-start | bytes 52
  210.3 98.8 %reduce-scatter.10.cloned.1.call-start = ((), (), s32[]{:S(2)}) async-start(), calls=%async_computation.8 | async-start | bytes 2621440 | tf_op jit(solution)/shard_map/reduce_scatter | solution.py:1070
  243.2 116.1 %reduce-scatter.14.cloned.1.call-start = ((), (), s32[]{:S(2)}) async-start(), calls=%async_computation.10 | async-start | bytes 2621440 | tf_op jit(solution)/shard_map/reduce_scatter | solution.py:1070
  276.0 128.7 %reduce-scatter.12.cloned.1.call-start = ((), (), s32[]{:S(2)}) async-start(), calls=%async_computation.9 | async-start | bytes 2621440 | tf_op jit(solution)/shard_map/reduce_scatter | solution.py:1070
  309.1 240.3 %reduce-scatter.20.cloned.1.call-start = ((), (), s32[]{:S(2)}) async-start(), calls=%async_computation.13 | async-start | bytes 1310720 | tf_op jit(solution)/shard_map/reduce_scatter | solution.py:1070
  330.5 218.9 %reduce-scatter.16.cloned.1.call-start = ((), (), s32[]{:S(2)}) async-start(), calls=%async_computation.11 | async-start | bytes 1966080 | tf_op jit(solution)/shard_map/reduce_scatter | solution.py:1070
  376.3 173.1 %reduce-scatter.18.cloned.1.call-start = ((), (), s32[]{:S(2)}) async-start(), calls=%async_computation.12 | async-start | bytes 1966080 | tf_op jit(solution)/shard_map/reduce_scatter | solution.py:1070
  404.7 24.4 %copy-start.4 = (f32[1,2,12,1024]{3,1,2,0:T(2,128)S(1)}, f32[1,2,12,1024]{3,1,2,0:T(2,128)}, u32[]{:S(2)}) copy-start(f32[1,2,12,1024]{3,1,2,0:T(2,128)} %param.20) | copy-start | bytes 294916
  404.7 25.1 %copy-start.8 = (f32[4,1,256]{2,1,0:T(1,128)S(1)}, f32[4,1,256]{2,1,0:T(1,128)}, u32[]{:S(2)}) copy-start(f32[4,1,256]{2,1,0:T(1,128)} %get-tuple-element.128) | copy-start | bytes 12292
  404.7 25.1 %copy-start.9 = (f32[4,1,256]{2,1,0:T(1,128)S(1)}, f32[4,1,256]{2,1,0:T(1,128)}, u32[]{:S(2)}) copy-start(f32[4,1,256]{2,1,0:T(1,128)} %get-tuple-element.129) | copy-start | bytes 12292
  404.7 25.1 %copy-start.10 = (f32[4,1,256]{2,1,0:T(1,128)S(1)}, f32[4,1,256]{2,1,0:T(1,128)}, u32[]{:S(2)}) copy-start(f32[4,1,256]{2,1,0:T(1,128)} %get-tuple-element.130) | copy-start | bytes 12292
  404.7 25.1 %copy-start = (bf16[2,577,1024]{2,1,0:T(8,128)(2,1)S(1)}, bf16[2,577,1024]{2,1,0:T(8,128)(2,1)}, u32[]{:S(2)}) copy-start(bf16[2,577,1024]{2,1,0:T(8,128)(2,1)} %get-tuple-element.91) | copy-start | bytes 7090180
  429.8 3.9 copy-start.11
  429.8 3.9 copy-start.12
  429.8 3.9 copy-start.6
  433.8 9.5 %copy-start.13 = (f32[2,512]{1,0:T(2,128)S(1)}, f32[2,512]{1,0:T(2,128)}, u32[]{:S(2)}) copy-start(f32[2,512]{1,0:T(2,128)} %get-tuple-element.127) | copy-start | bytes 12292
  433.8 9.5 %copy-start.7 = (f32[2,1024]{1,0:T(2,128)S(1)}, f32[2,1024]{1,0:T(2,128)}, u32[]{:S(2)}) copy-start(f32[2,1024]{1,0:T(2,128)} %get-tuple-element.124) | copy-start | bytes 24580
  586.5 6.1 %copy-start.3 = (f32[3,12,1024]{2,1,0:T(8,128)S(1)}, f32[3,12,1024]{2,1,0:T(8,128)}, u32[]{:S(2)}) copy-start(f32[3,12,1024]{2,1,0:T(8,128)} %get-tuple-element.181) | copy-start | bytes 442372
  586.5 6.8 %copy-start.5 = (bf16[12,1024]{1,0:T(8,128)(2,1)S(1)}, bf16[12,1024]{1,0:T(8,128)(2,1)}, u32[]{:S(2)}) copy-start(bf16[12,1024]{1,0:T(8,128)(2,1)} %get-tuple-element.182) | copy-start | bytes 73732
Sparse Core Ops, SparseCore 0:
  210.5 44.1 reduce-scatter.7
  257.1 43.1 reduce-scatter.9
  302.6 43.1 reduce-scatter.13
  348.0 43.1 reduce-scatter.11
  393.4 26.4 reduce-scatter.19
  422.2 37.2 reduce-scatter.15
  461.9 37.3 reduce-scatter.17

commit v4 on v3

--- a/solution.py
+++ b/solution.py
@@ -16,7 +16,7 @@
 WEIGHT_DECAY = 0.1
 OUTER_RATE = 0.7
 OUTER_MOMENTUM = 0.9
-QUARTERS = 4
+PIECES = ((0, 256), (256, 256), (512, 512))
 PARTS = 2
 LOW = jnp.bfloat16
 F32 = jnp.float32
@@ -228,81 +228,94 @@
     )(alive, attended, patches, cotangent, w_attn, vec)
 
 
-def mlp_kernel(first, pairwise, chunk, n_ref, g_ref, w1_ref, w2_ref, bias_ref, *refs):
+def mlp_kernel(first, pairwise, n_ref, g_ref, w1_ref, w2_ref, bias_ref, *refs):
     if not first:
         yi_ref, gi_ref, *refs = refs
-    y_ref, gn_ref, dw_ref, db_ref, h_scr, p_scr, nt_scr, gt_scr, *exchange = refs
+    y_ref, gn_ref, dw_ref, db_ref, h_scr, p_scr, loaded, *exchange = refs
     step = pl.program_id(0)
-    rows = n_ref.shape[0]
     each, _, width, cols = w1_ref.shape
+    if not first:
+        loads = (
+            pltpu.make_async_copy(yi_ref, y_ref, loaded.at[0]),
+            pltpu.make_async_copy(gi_ref, gn_ref, loaded.at[1]),
+        )
 
     @pl.when(step == 0)
     def _():
+        if not first:
+            for load in loads:
+                load.start()
+        else:
+            y_ref[...] = jnp.zeros_like(y_ref)
+            gn_ref[...] = jnp.zeros_like(gn_ref)
         if pairwise:
             greet_partner()
-        nt_scr[...] = n_ref[...].T
-        gt_scr[...] = g_ref[...].T
-        if first:
-            y_ref[...] = jnp.zeros_like(y_ref)
-            gn_ref[...] = jnp.zeros_like(gn_ref)
-        else:
-            y_ref[...] = yi_ref[...]
-            gn_ref[...] = gi_ref[...]
 
     w1 = jnp.concatenate([w1_ref[t, 0] for t in range(each)], axis=1)
     w2 = jnp.concatenate([w2_ref[t, 0] for t in range(each)], axis=1)
     bias = jnp.concatenate([bias_ref[t] for t in range(each)], axis=1)
-
-    def body(c, sums):
-        at = pl.ds(pl.multiple_of(c * chunk, chunk), chunk)
-        pre = dot(n_ref[at, :], w1) + bias
-        cdf = 0.5 * (1.0 + lax.erf(pre * 0.7071067811865476))
-        hidden = (pre * cdf).astype(LOW)
-        slope = cdf + pre * jnp.exp(-0.5 * pre * pre) * 0.3989422804014327
-        gp = dot(g_ref[at, :], w2) * slope
-        gl = gp.astype(LOW)
-        h_scr[at, :] = hidden
-        p_scr[at, :] = gl
-        y_ref[at, :] += dot(hidden, w2, NT)
-        gn_ref[at, :] += dot(gl, w1, NT)
-        return sums + jnp.sum(gl.astype(F32), axis=0, keepdims=True)
-
-    sums = lax.fori_loop(0, rows // chunk, body, jnp.zeros((1, each * cols), F32))
+    pre = dot(n_ref[...], w1) + bias
+    cdf = 0.5 * (1.0 + lax.erf(pre * 0.7071067811865476))
+    h_scr[...] = (pre * cdf).astype(LOW)
+    slope = cdf + pre * jnp.exp(-0.5 * pre * pre) * 0.3989422804014327
+    p_scr[...] = (dot(g_ref[...], w2) * slope).astype(LOW)
+    sums = jnp.sum(p_scr[...].astype(F32), axis=0, keepdims=True)
     for t in range(each):
         db_ref[t] = sums[:, t * cols : (t + 1) * cols]
+
     if pairwise:
         own, sent, received, sends, receives = exchange
         ours, theirs = bands(width // 2)
-        sent[step, 0] = dot(nt_scr[theirs, :], p_scr[...]).astype(LOW)
-        sent[step, 1] = dot(gt_scr[theirs, :], h_scr[...]).astype(LOW)
-        to_partner(sent, received, sends, receives, step).start()
-        own[step, 0] = dot(nt_scr[ours, :], p_scr[...])
-        own[step, 1] = dot(gt_scr[ours, :], h_scr[...])
+
+        def collect(n):
+            to_partner(sent, received, sends, receives, n % 2).wait()
+            for which in range(2):
+                total = (own[n % 2, which] + received[n % 2, which].astype(F32)).astype(LOW)
+                for t in range(each):
+                    dw_ref[n * each + t, which] = total[:, t * cols : (t + 1) * cols]
+
+        for n in range(dw_ref.shape[0] // each):
+
+            @pl.when(step == n)
+            def _():
+                if n:
+                    collect(n - 1)
+                sent[n % 2, 0] = dot(n_ref[:, theirs], p_scr[...], TN).astype(LOW)
+                sent[n % 2, 1] = dot(g_ref[:, theirs], h_scr[...], TN).astype(LOW)
+                to_partner(sent, received, sends, receives, n % 2).start()
+                own[n % 2, 0] = dot(n_ref[:, ours], p_scr[...], TN)
+                own[n % 2, 1] = dot(g_ref[:, ours], h_scr[...], TN)
+
+    else:
+        shards, depth = dw_ref.shape[0], dw_ref.shape[3]
+        d1 = dot(n_ref[...], p_scr[...], TN).astype(LOW)
+        d2 = dot(g_ref[...], h_scr[...], TN).astype(LOW)
+        for f in range(shards):
+            for t in range(each):
+                dw_ref[f, t, 0] = d1[f * depth : (f + 1) * depth, t * cols : (t + 1) * cols]
+                dw_ref[f, t, 1] = d2[f * depth : (f + 1) * depth, t * cols : (t + 1) * cols]
+
+    if not first:
+
+        @pl.when(step == 0)
+        def _():
+            for load in loads:
+                load.wait()
+
+    y_ref[...] += dot(h_scr[...], w2, NT)
+    gn_ref[...] += dot(p_scr[...], w1, NT)
+    if pairwise:
 
         @pl.when(step == pl.num_programs(0) - 1)
         def _():
-            for n in range(own.shape[0]):
-                to_partner(sent, received, sends, receives, n).wait()
-                for which in range(2):
-                    total = (own[n, which] + received[n, which].astype(F32)).astype(LOW)
-                    for t in range(each):
-                        dw_ref[n * each + t, which] = total[:, t * cols : (t + 1) * cols]
-
-        return
-    shards, depth = dw_ref.shape[0], dw_ref.shape[3]
-    d1 = dot(nt_scr[...], p_scr[...]).astype(LOW)
-    d2 = dot(gt_scr[...], h_scr[...]).astype(LOW)
-    for f in range(shards):
-        for t in range(each):
-            dw_ref[f, t, 0] = d1[f * depth : (f + 1) * depth, t * cols : (t + 1) * cols]
-            dw_ref[f, t, 1] = d2[f * depth : (f + 1) * depth, t * cols : (t + 1) * cols]
-
-
-def mlp(quarter, quarters, normed, grad_two, w_mlp, bias, carried, fsdp):
+            collect(dw_ref.shape[0] // each - 1)
+
+
+def mlp(part, start, cols, normed, grad_two, w_mlp, bias, carried, fsdp):
     rows, width = normed.shape
-    shards, _, _, hidden = w_mlp.shape
-    cols = hidden // quarters
-    each = 2
+    shards = w_mlp.shape[0]
+    each = max(512 // cols, 1)
+    at = start // cols
     first, pairwise = carried is None, fsdp == 2
     single = pl.Buffered(1)
     full = pl.BlockSpec((rows, width), lambda s: (0, 0), pipeline_mode=single)
@@ -312,34 +325,33 @@
     if pairwise:
         out_w = pl.BlockSpec((shards, 2, depth, cols), lambda s: (0, 0, 0, 0), pipeline_mode=single)
         w_shape = jax.ShapeDtypeStruct((shards, 2, depth, cols), LOW)
-        extra = exchange_scratch(steps, (2, depth, each * cols))
+        extra = exchange_scratch(2, (2, depth, each * cols))
     else:
         out_w = pl.BlockSpec((fsdp, each, 2, depth, cols), lambda s: (0, s, 0, 0, 0))
         w_shape = jax.ShapeDtypeStruct((fsdp, shards, 2, depth, cols), LOW)
         extra = []
     return pl.pallas_call(
-        functools.partial(mlp_kernel, first, pairwise, rows // 4),
+        functools.partial(mlp_kernel, first, pairwise),
         grid=(steps,),
         in_specs=[
             full,
             full,
-            pl.BlockSpec((each, 1, width, cols), lambda s: (s, 0, 0, quarter)),
-            pl.BlockSpec((each, 1, width, cols), lambda s: (s, 1, 0, quarter)),
-            pl.BlockSpec((each, 1, cols), lambda s: (s, 0, quarter)),
+            pl.BlockSpec((each, 1, width, cols), lambda s: (s, 0, 0, at)),
+            pl.BlockSpec((each, 1, width, cols), lambda s: (s, 1, 0, at)),
+            pl.BlockSpec((each, 1, cols), lambda s: (s, 0, at)),
         ]
-        + ([] if first else [full, full]),
+        + ([] if first else [pl.BlockSpec(memory_space=pl.ANY)] * 2),
         out_specs=[full, full, out_w, pl.BlockSpec((each, 1, cols), lambda s: (s, 0, 0))],
         out_shape=[acc_shape, acc_shape, w_shape, jax.ShapeDtypeStruct((shards, 1, cols), F32)],
         scratch_shapes=[
             pltpu.VMEM((rows, each * cols), LOW),
             pltpu.VMEM((rows, each * cols), LOW),
-            pltpu.VMEM((width, rows), LOW),
-            pltpu.VMEM((width, rows), LOW),
+            pltpu.SemaphoreType.DMA((2,)),
             *extra,
         ],
-        compiler_params=params(2 + quarter if pairwise else None),
+        compiler_params=params(2 + part if pairwise else None),
         cost_estimate=cost(12 * rows * width * cols * shards, 24 * rows * width),
-        name=f"mlp_{quarter}",
+        name=f"mlp_{part}",
     )(normed, grad_two, w_mlp, w_mlp, bias, *([] if first else carried))
 
 
@@ -375,7 +387,7 @@
 
     for t in range(shards):
         ga_ref[:, t * cols : (t + 1) * cols] = dot(low, w_ref[t, 0]).astype(LOW)
-    part = dot(low.T, att_ref[...])
+    part = dot(low, att_ref[...], TN)
 
     @pl.when(i == 0)
     def _():
@@ -502,7 +514,7 @@
         x_ref, gr_ref, vec_ref, out_ref, norm_ref, *refs = refs
     else:
         acc_ref, *refs = refs
-    dw_ref, sums_ref, acc_scr, nt_scr, *exchange = refs
+    dw_ref, sums_ref, acc_scr, *exchange = refs
     j = pl.program_id(0)
     shards, _, _, cols = w_ref.shape
     span = n_ref.shape[0] // images
@@ -512,7 +524,6 @@
 
     @pl.when(j == 0)
     def _():
-        nt_scr[...] = n_ref[...].T
         acc_scr[...] = jnp.zeros_like(acc_scr) if first else carry_ref[...]
         sums_ref[0:1, :] = jnp.sum(dq_ref[0].astype(F32), axis=0, keepdims=True)
         sums_ref[1:2, :] = jnp.sum(dv_ref[0].astype(F32), axis=0, keepdims=True)
@@ -528,13 +539,13 @@
     def step(ref):
         weight = jnp.concatenate([w_ref[t, 0] for t in range(shards)], axis=1)
         if pairwise:
-            ours, theirs = bands(nt_scr.shape[0] // 2)
-            sent[j] = dot(nt_scr[theirs, :], ref[0]).astype(LOW)
+            ours, theirs = bands(n_ref.shape[1] // 2)
+            sent[j] = dot(n_ref[:, theirs], ref[0], TN).astype(LOW)
             to_partner(sent, received, sends, receives, j).start()
-            own[j] = dot(nt_scr[ours, :], ref[0])
+            own[j] = dot(n_ref[:, ours], ref[0], TN)
         else:
             depth = dw_ref.shape[3]
-            dw = dot(nt_scr[...], ref[0]).astype(LOW)
+            dw = dot(n_ref[...], ref[0], TN).astype(LOW)
             for f in range(dw_ref.shape[0]):
                 spread(0, dw[f * depth : (f + 1) * depth], f)
         acc_scr[...] += dot(ref[0], weight, NT)
@@ -605,22 +616,45 @@
         in_specs=in_specs,
         out_specs=[*out_specs, dw_spec, pl.BlockSpec((2, lanes), lambda j: (0, 0))],
         out_shape=[*out_shape, dw_shape, jax.ShapeDtypeStruct((2, lanes), F32)],
-        scratch_shapes=[pltpu.VMEM((rows, width), F32), pltpu.VMEM((width, rows), LOW), *extra],
+        scratch_shapes=[pltpu.VMEM((rows, width), F32), *extra],
         compiler_params=params(7 + part if pairwise else None),
         cost_estimate=cost(12 * rows * width * lanes, 20 * rows * width),
         name=f"close_{part}",
     )(normed, *grads, w_attn, *([] if first else [carry]), *(ending if final else []))
 
 
-def gather_kernel(a_in, m_in, a_out, m_out, a_hold, m_hold, zs, zr, xs, xr, ys, yr, xfs, xfr, yfs, yfr, cs, cr, ls):
+def attend_pair(seq, q, k, v):
+    scale = HD**-0.5
+    parts = []
+    for h in range(2):
+        scores = dot(q, half_lanes(k, h), NT)
+        lane = lax.broadcasted_iota(jnp.int32, scores.shape, 1)
+        scores = jnp.where(lane < seq, scores, -1e30)
+        top = jnp.max(scores, axis=1, keepdims=True)
+        raised = jnp.exp((scores - top) * scale)
+        total = jnp.sum(raised, axis=1, keepdims=True)
+        probs = (raised * (1.0 / total)).astype(LOW)
+        parts.append(dot(probs, v))
+    lane = lax.broadcasted_iota(jnp.int32, parts[0].shape, 1)
+    return jnp.where(lane < HD, parts[0], parts[1]).astype(LOW)
+
+
+def front_kernel(
+    images, seq, alive_ref, a_in, m_in, x_ref, g_ref, vec_ref,
+    a_out, m_out, n_out, qkv_out, att_out, resid_out, n2_out, g2_out,
+    a_wide, m_wide, a_hold, m_hold, n_scr, qkv_scr, att_scr, w_scr, o_scr, x_scr, resid_scr, n2_scr, g2_scr,
+    zs, zr, xs, xr, ys, yr, xfs, xfr, yfs, yfr, cs, cr, ls, ws,
+):
     g, f, z = lax.axis_index("group"), lax.axis_index("fsdp"), lax.axis_index("tensor")
-    last = lax.axis_size("tensor") - 1
+    shards = lax.axis_size("tensor")
+    last = shards - 1
     x_at, y_at = g % 2, g // 2
     east, north = y_at * 2 + (1 - x_at), (1 - y_at) * 2 + x_at
-    depth = a_in.shape[1]
+    depth, cols = a_in.shape[1:]
     band = depth // 4
     shared = band * 3 // 8
     rest = band - 2 * shared
+    span = n_scr.shape[0] // images
 
     def place(column):
         cx, cy = column % 2, column // 2
@@ -630,28 +664,25 @@
     z_row = mine * band - shared * (mine % 2)
     lead_east = of_east * band + shared * (of_east % 2)
     lead_north = of_north * band + shared * (of_north % 2)
-    chunks = ((a_in, a_out, 0, a_in.shape[0]), (m_in, m_out, 0, 1), (m_in, m_out, 1, 1))
+    chunks = ((a_out, 0, 3), (a_out, 3, 1), (m_out, 0, 1), (m_out, 1, 1))
 
     def tile(n):
         return pl.multiple_of(n, 16)
 
     def held(n, t, row, rows):
-        _, out, j, many = chunks[n]
+        out, j, many = chunks[n]
         return out.at[t, pl.ds(j, many), pl.ds(tile(f * depth + row), rows), :]
 
-    def owned(n, row, rows):
-        source, _, j, many = chunks[n]
-        return source.at[pl.ds(j, many), pl.ds(tile(row), rows), :]
-
-    def send(src, dst, sems, semr, n, t, to):
+    def send(part, sems, semr, n, t, to):
         return pltpu.make_async_remote_copy(
-            src_ref=src, dst_ref=dst, send_sem=sems.at[n, t], recv_sem=semr.at[n, t], device_id=to, device_id_type=MESH
+            src_ref=part, dst_ref=part, send_sem=sems.at[n, t], recv_sem=semr.at[n, t], device_id=to, device_id_type=MESH
         )
 
-    def along(n, t, up, src):
+    def along(n, t, up):
+        part = held(n, t, z_row, band + shared)
         return pltpu.make_async_remote_copy(
-            src_ref=src,
-            dst_ref=held(n, t, z_row, band + shared),
+            src_ref=part,
+            dst_ref=part,
             send_sem=zs.at[n, t, 0 if up else 1],
             recv_sem=zr.at[n, t],
             device_id=(g, f, z + 1 if up else z - 1),
@@ -659,23 +690,30 @@
         )
 
     def to_east(n, t):
-        part = held(n, t, mine * band, band)
-        return send(part, part, xs, xr, n, t, (east, f, z))
+        return send(held(n, t, mine * band, band), xs, xr, n, t, (east, f, z))
 
     def to_north(n, t):
-        part = held(n, t, mine * band, band)
-        return send(part, part, ys, yr, n, t, (north, f, z))
+        return send(held(n, t, mine * band, band), ys, yr, n, t, (north, f, z))
 
     def north_to_east(n, t):
-        part = held(n, t, lead_north, shared)
-        return send(part, part, xfs, xfr, n, t, (east, f, z))
+        return send(held(n, t, lead_north, shared), xfs, xfr, n, t, (east, f, z))
 
     def east_to_north(n, t):
-        part = held(n, t, lead_east + shared, rest)
-        return send(part, part, yfs, yfr, n, t, (north, f, z))
-
-    def across(n, t, src):
-        return send(src, held(n, t, 0, depth), cs, cr, n, t, (g, 1 - f, z))
+        return send(held(n, t, lead_east + shared, rest), yfs, yfr, n, t, (north, f, z))
+
+    def across(n, t):
+        return send(held(n, t, 0, depth), cs, cr, n, t, (g, 1 - f, z))
+
+    rows = pl.ds(tile(f * depth), depth)
+    loads = (
+        pltpu.make_async_copy(a_in, a_wide, ls.at[0]),
+        pltpu.make_async_copy(m_in, m_wide, ls.at[1]),
+    )
+    keeps = (
+        pltpu.make_async_copy(a_hold, a_out.at[z, :, rows, :], ls.at[2]),
+        pltpu.make_async_copy(m_hold, m_out.at[z, :, rows, :], ls.at[3]),
+    )
+    loads[0].start()
 
     barrier = pltpu.get_barrier_semaphore()
 
@@ -693,14 +731,13 @@
     def _():
         greet((g, f, z + 1))
 
+    loads[0].wait()
+    a_hold[...] = a_wide[...].astype(LOW)
+    keeps[0].start()
     pl.semaphore_wait(barrier, 3 + jnp.minimum(z, 1) + jnp.minimum(last - z, 1))
-
-    load_a = pltpu.make_async_copy(a_in, a_hold, ls.at[0])
-    load_m = pltpu.make_async_copy(m_in, m_hold, ls.at[1])
-    load_a.start()
-    load_m.start()
-
-    items = [(n, k, up) for n in range(3) for k in range(1, last + 1) for up in (True, False)]
+    keeps[0].wait()
+
+    count = len(chunks)
 
     def when_real(k, up, run):
         @pl.when(z - k >= 0 if up else z + k <= last)
@@ -710,21 +747,21 @@
     def own(n):
         @pl.when(z < last)
         def _():
-            along(n, z, True, owned(n, z_row, band + shared)).start()
+            along(n, z, True).start()
 
         @pl.when(z > 0)
         def _():
-            along(n, z, False, owned(n, z_row, band + shared)).start()
-
-        across(n, z, owned(n, 0, depth)).start()
+            along(n, z, False).start()
+
+        across(n, z).start()
 
     def land(n, k, up):
         def run(t):
-            along(n, t, up, held(n, t, z_row, band + shared)).wait_recv()
+            along(n, t, up).wait_recv()
 
             @pl.when(z < last if up else z > 0)
             def _():
-                along(n, t, up, held(n, t, z_row, band + shared)).start()
+                along(n, t, up).start()
 
             to_east(n, t).start()
             to_north(n, t).start()
@@ -744,85 +781,205 @@
         def run(t):
             east_to_north(n, t).wait_recv()
             north_to_east(n, t).wait_recv()
-            across(n, t, held(n, t, 0, depth)).start()
+            across(n, t).start()
 
         when_real(k, up, run)
 
-    for at in range(len(items) + 4):
-        if at % (2 * last) == 0 and at // (2 * last) < 3:
-            own(at // (2 * last))
-        if at < len(items):
-            land(*items[at])
-        if 0 <= at - 2 < len(items):
-            relay(*items[at - 2])
-        if 0 <= at - 4 < len(items):
-            finish(*items[at - 4])
-
-    load_a.wait()
-    load_m.wait()
-    rows = pl.ds(tile(f * depth), depth)
-    keep_a = pltpu.make_async_copy(a_hold, a_out.at[z, :, rows, :], ls.at[2])
-    keep_m = pltpu.make_async_copy(m_hold, m_out.at[z, :, rows, :], ls.at[3])
-    keep_a.start()
-    keep_m.start()
-    keep_a.wait()
-    keep_m.wait()
-
-    for n in range(3):
+    def both(run, n, k):
+        for up in (True, False):
+            run(n, k, up)
+
+    def fetch(t):
+        return pltpu.make_async_copy(a_out.at[t, pl.ds(0, 3)], w_scr, ws.at[0])
+
+    def maps(t):
+        across(0, t).wait_recv()
+        fetch(t).start()
+        fetch(t).wait()
+        here = pl.ds(pl.multiple_of(t * cols, cols), cols)
+        for j in range(3):
+            out = dot(n_scr[...], w_scr[j])
+            if j != 1:
+                out = out + vec_ref[4 + j // 2 : 5 + j // 2, here]
+            qkv_scr[j, :, here] = out.astype(LOW)
+
+    def project(n, k, up):
+        when_real(k, up, maps)
+
+    own(0)
+    loads[1].start()
+    n_scr[...] = jnp.zeros_like(n_scr)
+    for i in range(images):
+        normal, _ = centred(x_ref[i].astype(F32))
+        n_scr[pl.ds(i * span, seq), :] = (normal * vec_ref[0:1] + vec_ref[1:2]).astype(LOW)
+    puts = [pltpu.make_async_copy(n_scr, n_out, ws.at[1])]
+    puts[0].start()
+    both(land, 0, 1)
+    loads[1].wait()
+    m_hold[...] = m_wide[...].astype(LOW)
+    keeps[1].start()
+    maps(z)
+    both(land, 0, 2)
+    both(relay, 0, 1)
+    keeps[1].wait()
+    both(land, 0, 3)
+    for n in range(1, count):
+        own(n)
+    both(relay, 0, 2)
+    both(finish, 0, 1)
+    both(relay, 0, 3)
+    both(finish, 0, 2)
+    both(project, 0, 1)
+    both(finish, 0, 3)
+    both(project, 0, 2)
+
+    rest_items = [(n, k) for k in range(1, last + 1) for n in range(1, count)]
+    total = len(rest_items) + 2
+
+    def advance(at):
+        if at < len(rest_items):
+            both(land, *rest_items[at])
+        if 0 <= at - 1 < len(rest_items):
+            both(relay, *rest_items[at - 1])
+        if 0 <= at - 2 < len(rest_items):
+            both(finish, *rest_items[at - 2])
+
+    advance(0)
+    both(project, 0, 3)
+    puts.append(pltpu.make_async_copy(qkv_scr, qkv_out, ws.at[2]))
+    puts[-1].start()
+
+    pair = 2 * HD
+    pairs = qkv_scr.shape[2] // pair
+    stretch = max(pairs // 4, 1)
+    at = 1
+    for i in range(images):
+        for start in range(0, pairs, stretch):
+
+            def body(h, carry):
+                lanes = pl.ds(pl.multiple_of(h * pair, pair), pair)
+                here = pl.ds(i * span, span)
+                att_scr[here, lanes] = attend_pair(
+                    seq, qkv_scr[0, here, lanes], qkv_scr[1, here, lanes], qkv_scr[2, here, lanes]
+                )
+                return carry
+
+            lax.fori_loop(start, start + stretch, body, 0)
+            if at < total:
+                advance(at)
+                at += 1
+    puts.append(pltpu.make_async_copy(att_scr, att_out, ws.at[3]))
+    puts[-1].start()
+    while at < total - 2:
+        advance(at)
+        at += 1
+
+    for t in range(shards):
+        across(1, t).wait_recv()
+    take = pltpu.make_async_copy(a_out.at[:, 3], o_scr, ws.at[0])
+    take.start()
+    take.wait()
+    x_scr[...] = jnp.zeros_like(x_scr)
+    for i in range(images):
+        here = pl.ds(i * span, span)
+        x_scr[0:seq, :] = x_ref[i].astype(F32)
+        out = x_scr[...] + vec_ref[6:7]
+        for t in range(shards):
+            out = out + dot(att_scr[here, t * cols : (t + 1) * cols], o_scr[t], NT)
+        resid_scr[here, :] = out
+        normal, _ = centred(out)
+        n2_scr[here, :] = (normal * vec_ref[2:3] + vec_ref[3:4]).astype(LOW)
+        x_scr[0:seq, :] = g_ref[i].astype(F32) * alive_ref[i]
+        g2_scr[here, :] = x_scr[...].astype(LOW)
+        if at < total:
+            advance(at)
+            at += 1
+    for n, (src, dst) in enumerate(((resid_scr, resid_out), (n2_scr, n2_out), (g2_scr, g2_out))):
+        puts.append(pltpu.make_async_copy(src, dst, ws.at[4 + n]))
+        puts[-1].start()
+    while at < total:
+        advance(at)
+        at += 1
+    for put in puts:
+        put.wait()
+
+    for n in range(count):
         @pl.when(z < last)
         def _():
-            along(n, z, True, owned(n, z_row, band + shared)).wait_send()
+            along(n, z, True).wait_send()
 
         @pl.when(z > 0)
         def _():
-            along(n, z, False, owned(n, z_row, band + shared)).wait_send()
-
-        across(n, z, owned(n, 0, depth)).wait()
+            along(n, z, False).wait_send()
+
+        for t in range(shards):
+            across(n, t).wait_send()
+            if n > 1:
+                across(n, t).wait_recv()
 
     def settle(n, k, up):
         def run(t):
             @pl.when(z < last if up else z > 0)
             def _():
-                along(n, t, up, held(n, t, z_row, band + shared)).wait_send()
+                along(n, t, up).wait_send()
 
             to_east(n, t).wait_send()
             to_north(n, t).wait_send()
             east_to_north(n, t).wait_send()
             north_to_east(n, t).wait_send()
-            across(n, t, held(n, t, 0, depth)).wait()
 
         when_real(k, up, run)
 
-    for item in items:
-        settle(*item)
-
-
-def gather(attn_low, mlp_low, shards):
-    _, depth, a_cols = attn_low.shape
-    _, _, m_cols = mlp_low.shape
-    width = 2 * depth
+    for n in range(count):
+        for k in range(1, last + 1):
+            both(settle, n, k)
+
+
+def front(alive, attn_master, mlp_master, patches, cotangent, vec, shards):
+    _, depth, a_cols = attn_master.shape
+    _, _, m_cols = mlp_master.shape
+    images, seq, width = patches.shape
+    rows = images * padded(seq)
     anywhere = pl.BlockSpec(memory_space=pl.ANY)
+    inside = pl.BlockSpec(memory_space=pltpu.VMEM)
     dma = pltpu.SemaphoreType.DMA
+    low = jax.ShapeDtypeStruct((rows, width), LOW)
     return pl.pallas_call(
-        gather_kernel,
-        in_specs=[anywhere, anywhere],
-        out_specs=[anywhere, anywhere],
+        functools.partial(front_kernel, images, seq),
+        in_specs=[pl.BlockSpec(memory_space=pltpu.SMEM), anywhere, anywhere, inside, inside, inside],
+        out_specs=[anywhere] * 8,
         out_shape=[
             jax.ShapeDtypeStruct((shards, 4, width, a_cols), LOW),
             jax.ShapeDtypeStruct((shards, 2, width, m_cols), LOW),
+            low,
+            jax.ShapeDtypeStruct((3, rows, width), LOW),
+            low,
+            jax.ShapeDtypeStruct((rows, width), F32),
+            low,
+            low,
         ],
         scratch_shapes=[
-            pltpu.VMEM(attn_low.shape, LOW),
-            pltpu.VMEM(mlp_low.shape, LOW),
-            dma((3, shards, 2)),
+            pltpu.VMEM(attn_master.shape, F32),
+            pltpu.VMEM(mlp_master.shape, F32),
+            pltpu.VMEM(attn_master.shape, LOW),
+            pltpu.VMEM(mlp_master.shape, LOW),
+            pltpu.VMEM((rows, width), LOW),
+            pltpu.VMEM((3, rows, width), LOW),
+            pltpu.VMEM((rows, width), LOW),
+            pltpu.VMEM((3, width, a_cols), LOW),
+            pltpu.VMEM((shards, width, a_cols), LOW),
+            pltpu.VMEM((rows // images, width), F32),
+            pltpu.VMEM((rows, width), F32),
+            pltpu.VMEM((rows, width), LOW),
+            pltpu.VMEM((rows, width), LOW),
+            dma((4, shards, 2)),
         ]
-        + [dma((3, shards))] * 11
-        + [dma((4,))],
-        compiler_params=pltpu.CompilerParams(
-            collective_id=1, has_side_effects=True, vmem_limit_bytes=60 * 2**20
-        ),
-        name="gather",
-    )(attn_low, mlp_low)
+        + [dma((4, shards))] * 11
+        + [dma((4,)), dma((7,))],
+        compiler_params=params(1),
+        cost_estimate=cost(8 * rows * width * width, 30 * rows * width),
+        name="front",
+    )(alive, attn_master, mlp_master, patches, cotangent, vec)
 
 
 def inner_adamw(master, gradient, first, second, step_rate, decay_rate):
@@ -895,7 +1052,12 @@
     )(total, master, outer_old)
 
 
-def group_kernel(groups, diff_ref, total_ref, landed, summed, sends, receives, sends_two, receives_two):
+def group_kernel(groups, shards, fsdp, diff_ref, *refs):
+    if fsdp:
+        part_ref, master_ref, moment_ref, outer_ref, total_ref, inner_ref, state_ref, copy_ref, *refs = refs
+    else:
+        total_ref, *refs = refs
+    landed, summed, sends, receives, sends_two, receives_two, *small = refs
     g, f, t = lax.axis_index("group"), lax.axis_index("fsdp"), lax.axis_index("tensor")
     span = landed.shape[1]
 
@@ -904,34 +1066,62 @@
 
     def other(k):
         return lax.rem(g + k, groups)
+
+    def back(k):
+        return lax.rem(g + groups - k, groups)
+
+    def copy(src, dst, sems, semr, k, to):
+        return pltpu.make_async_remote_copy(
+            src_ref=src, dst_ref=dst, send_sem=sems.at[k], recv_sem=semr.at[k], device_id=to, device_id_type=MESH
+        )
+
+    def part(k):
+        return copy(diff_ref.at[rows(other(k)), :], landed.at[k], sends, receives, k, (other(k), f, t))
+
+    def result(k):
+        return copy(summed, landed.at[groups + k], sends_two, receives_two, k, (other(k), f, t))
 
     barrier = pltpu.get_barrier_semaphore()
     for k in range(1, groups):
         pl.semaphore_signal(barrier, inc=1, device_id=(other(k), f, t), device_id_type=MESH)
-    pl.semaphore_wait(barrier, groups - 1)
-
-    def part(k):
-        return pltpu.make_async_remote_copy(
-            src_ref=diff_ref.at[rows(other(k)), :],
-            dst_ref=landed.at[k],
-            send_sem=sends.at[k],
-            recv_sem=receives.at[k],
-            device_id=(other(k), f, t),
-            device_id_type=MESH,
-        )
-
-    def result(k):
-        return pltpu.make_async_remote_copy(
-            src_ref=summed,
-            dst_ref=landed.at[groups + k],
-            send_sem=sends_two.at[k],
-            recv_sem=receives_two.at[k],
-            device_id=(other(k), f, t),
-            device_id_type=MESH,
-        )
+    members = shards * fsdp
+    if fsdp:
+        few, mine, one, two, three, four = small
+        me = f * shards + t
+
+        def place(k):
+            at = lax.rem(me + k, members)
+            return (g, at // shards, lax.rem(at, shards))
+
+        def piece(k):
+            return copy(part_ref, few.at[k], one, two, k, place(k))
+
+        def share(k):
+            return copy(mine, few.at[members + k], three, four, k, (other(k), f, t))
+
+        for k in range(1, members):
+            pl.semaphore_signal(barrier, inc=1, device_id=place(k), device_id_type=MESH)
+    pl.semaphore_wait(barrier, groups - 1 + max(members - 1, 0))
 
     for k in range(1, groups):
         part(k).start()
+    if fsdp:
+        for k in range(1, members):
+            piece(k).start()
+        few[0] = part_ref[...]
+        for k in range(1, members):
+            piece(k).wait_recv()
+        gradient = jnp.zeros(part_ref.shape, F32)
+        for n in range(members):
+            gradient = gradient + few[lax.rem(me + members - n, members)]
+        master = master_ref[...]
+        new, second = inner_adamw(master, gradient, moment_ref[0], moment_ref[1], VECTOR_RATE, 0.0)
+        inner_ref[0] = gradient
+        inner_ref[1] = second
+        mine[...] = master - new
+        for k in range(1, groups):
+            share(k).start()
+        few[members] = mine[...]
     total = diff_ref[rows(g), :].astype(F32)
     for k in range(1, groups):
         part(k).wait_recv()
@@ -940,124 +1130,69 @@
     for k in range(1, groups):
         result(k).start()
     total_ref[rows(g), :] = summed[...]
+    if fsdp:
+        for k in range(1, groups):
+            share(k).wait_recv()
+        difference = jnp.zeros(part_ref.shape, F32)
+        for n in range(groups):
+            difference = difference + few[members + lax.rem(g + groups - n, groups)]
+        difference = difference / groups
+        momentum, fresh = outer_nesterov(master, outer_ref[...], difference)
+        state_ref[0] = difference
+        state_ref[1] = momentum
+        state_ref[2] = fresh
+        copy_ref[...] = fresh.astype(LOW)
     for k in range(1, groups):
         result(k).wait_recv()
-        total_ref[rows(lax.rem(g + groups - k, groups)), :] = landed[groups + k]
+        total_ref[rows(back(k)), :] = landed[groups + k]
     for k in range(1, groups):
         part(k).wait_send()
         result(k).wait_send()
-
-
-def group_sum(diff, groups, identity, name):
+    if fsdp:
+        for k in range(1, members):
+            piece(k).wait_send()
+        for k in range(1, groups):
+            share(k).wait_send()
+
+
+def group_sum(diff, groups, identity, name, vectors=None, shards=0, fsdp=0):
     flat = diff.reshape(-1, diff.shape[-1])
     span, cols = flat.shape[0] // groups, flat.shape[1]
     dma = pltpu.SemaphoreType.DMA
     whole = pl.BlockSpec(memory_space=pltpu.VMEM)
-    total = pl.pallas_call(
-        functools.partial(group_kernel, groups),
-        in_specs=[whole],
-        out_specs=whole,
-        out_shape=jax.ShapeDtypeStruct(flat.shape, LOW),
+    out_shape = [jax.ShapeDtypeStruct(flat.shape, LOW)]
+    extra = []
+    if fsdp:
+        shape = vectors[0].shape
+        out_shape += [
+            jax.ShapeDtypeStruct((2, *shape), F32),
+            jax.ShapeDtypeStruct((3, *shape), F32),
+            jax.ShapeDtypeStruct(shape, LOW),
+        ]
+        extra = [
+            pltpu.VMEM((fsdp * shards + groups, *shape), F32),
+            pltpu.VMEM(shape, F32),
+            dma((fsdp * shards,)),
+            dma((fsdp * shards,)),
+            dma((groups,)),
+            dma((groups,)),
+        ]
+    total, *rest = pl.pallas_call(
+        functools.partial(group_kernel, groups, shards, fsdp),
+        in_specs=[whole] * (5 if fsdp else 1),
+        out_specs=[whole] * len(out_shape),
+        out_shape=out_shape,
         scratch_shapes=[
             pltpu.VMEM((2 * groups, span, cols), LOW),
             pltpu.VMEM((span, cols), LOW),
             *[dma((groups,))] * 4,
+            *extra,
         ],
         compiler_params=params(identity),
         cost_estimate=cost(4 * flat.size, 8 * flat.size),
         name=name,
-    )(flat)
-    return total.reshape(diff.shape)
-
-
-def vector_kernel(groups, shards, fsdp, part_ref, master_ref, moment_ref, outer_ref, inner_ref, state_ref, copy_ref,
-                  landed, mine, sends, receives, sends_two, receives_two):
-    g, f, t = lax.axis_index("group"), lax.axis_index("fsdp"), lax.axis_index("tensor")
-    me = f * shards + t
-    members = fsdp * shards
-
-    def place(k):
-        at = lax.rem(me + k, members)
-        return (g, at // shards, at % shards)
-
-    def column(k):
-        return (lax.rem(g + k, groups), f, t)
-
-    barrier = pltpu.get_barrier_semaphore()
-    for k in range(1, members):
-        pl.semaphore_signal(barrier, inc=1, device_id=place(k), device_id_type=MESH)
-    for k in range(1, groups):
-        pl.semaphore_signal(barrier, inc=1, device_id=column(k), device_id_type=MESH)
-    pl.semaphore_wait(barrier, members + groups - 2)
-
-    def part(k):
-        return pltpu.make_async_remote_copy(
-            src_ref=part_ref, dst_ref=landed.at[k], send_sem=sends.at[k], recv_sem=receives.at[k],
-            device_id=place(k), device_id_type=MESH,
-        )
-
-    def share(k):
-        return pltpu.make_async_remote_copy(
-            src_ref=mine, dst_ref=landed.at[members + k], send_sem=sends_two.at[k], recv_sem=receives_two.at[k],
-            device_id=column(k), device_id_type=MESH,
-        )
-
-    for k in range(1, members):
-        part(k).start()
-    landed[0] = part_ref[...]
-    for k in range(1, members):
-        part(k).wait_recv()
-    gradient = jnp.zeros(part_ref.shape, F32)
-    for n in range(members):
-        gradient = gradient + landed[lax.rem(me + members - n, members)]
-    master = master_ref[...]
-    new, second = inner_adamw(master, gradient, moment_ref[0], moment_ref[1], VECTOR_RATE, 0.0)
-    inner_ref[0] = gradient
-    inner_ref[1] = second
-    mine[...] = master - new
-    for k in range(1, groups):
-        share(k).start()
-    landed[members] = mine[...]
-    for k in range(1, groups):
-        share(k).wait_recv()
-    difference = jnp.zeros(part_ref.shape, F32)
-    for n in range(groups):
-        difference = difference + landed[members + lax.rem(g + groups - n, groups)]
-    difference = difference / groups
-    momentum, fresh = outer_nesterov(master, outer_ref[...], difference)
-    state_ref[0] = difference
-    state_ref[1] = momentum
-    state_ref[2] = fresh
-    copy_ref[...] = fresh.astype(LOW)
-    for k in range(1, members):
-        part(k).wait_send()
-    for k in range(1, groups):
-        share(k).wait_send()
-
-
-def vector_step(part, master, moments, outer_old, groups, shards, fsdp, identity):
-    dma = pltpu.SemaphoreType.DMA
-    whole = pl.BlockSpec(memory_space=pltpu.VMEM)
-    return pl.pallas_call(
-        functools.partial(vector_kernel, groups, shards, fsdp),
-        in_specs=[whole] * 4,
-        out_specs=[whole] * 3,
-        out_shape=[
-            jax.ShapeDtypeStruct((2, *part.shape), F32),
-            jax.ShapeDtypeStruct((3, *part.shape), F32),
-            jax.ShapeDtypeStruct(part.shape, LOW),
-        ],
-        scratch_shapes=[
-            pltpu.VMEM((fsdp * shards + groups, *part.shape), F32),
-            pltpu.VMEM(part.shape, F32),
-            dma((fsdp * shards,)),
-            dma((fsdp * shards,)),
-            dma((groups,)),
-            dma((groups,)),
-        ],
-        compiler_params=params(identity),
-        name="vector_step",
-    )(part, master, moments, outer_old)
+    )(flat, *(vectors or []))
+    return total.reshape(diff.shape), *rest
 
 
 def gather_weights(shard):
@@ -1097,69 +1232,58 @@
     images = x.shape[0]
 
     if (groups, fsdp) == (4, 2):
-        w_attn, w_mlp = gather(attn_master.astype(LOW), mlp_master.astype(LOW), tensor_size)
+        w_attn, w_mlp, normed_one, qkv, attended, resid, normed_two, grad_two = front(
+            alive, attn_master, mlp_master, x, cotangent, vec, tensor_size
+        )
     else:
         w_attn = gather_weights(attn_master.astype(LOW))
         w_mlp = gather_weights(mlp_master.astype(LOW))
-
-    normed_one, qkv = project(x, w_attn, vec)
-    attended = attend(qkv, images, seq)
-    resid, normed_two, grad_two = mix(alive, attended, x, cotangent, w_attn, vec)
+        normed_one, qkv = project(x, w_attn, vec)
+        attended = attend(qkv, images, seq)
+        resid, normed_two, grad_two = mix(alive, attended, x, cotangent, w_attn, vec)
     bias = vec[8:].reshape(tensor_size, 1, -1)
     carried = None
     mlp_grads, bias_parts = [], []
-    for quarter in range(QUARTERS):
-        if quarter == 3:
-            carried[0], mlp_grads[0] = lax.optimization_barrier((carried[0], mlp_grads[0]))
-        *carried, dw, db = mlp(quarter, QUARTERS, normed_two, grad_two, w_mlp, bias, carried, fsdp)
+    for part, (start, cols) in enumerate(PIECES):
+        *carried, dw, db = mlp(part, start, cols, normed_two, grad_two, w_mlp, bias, carried, fsdp)
         mlp_grads.append(scatter_gradient(dw))
         bias_parts.append(db)
     branch, grad_normed = carried
-    branch, mlp_grads[1] = lax.optimization_barrier((branch, mlp_grads[1]))
     block_output, grad_resid, grad_attended, dw_out, sums_two = turn(
         alive, resid, branch, grad_normed, grad_two, attended, w_attn, vec, images, seq, fsdp
     )
     out_grad = scatter_gradient(dw_out)
-    qkv_grads, head_sums, carry = [], [], None
-    for part in range(PARTS):
-        grads = unattend(qkv, grad_attended, images, seq, part, PARTS, tensor_size)
-        final = part == PARTS - 1
-        head_grad, mlp_grads[2 + part] = lax.optimization_barrier((grads[0], mlp_grads[2 + part]))
-        grads = (head_grad, *grads[1:])
-        ending = [x, grad_resid, vec] if final else None
-        *carry, dw_qkv, sums = close(part, PARTS, normed_one, grads, w_attn, carry, ending, fsdp, images, seq)
-        if not final:
-            (carry,) = carry
-        qkv_grads.append(scatter_gradient(dw_qkv))
-        head_sums.append(sums.reshape(2, tensor_size, -1))
-    patches_grad, sums_one = carry
-
-    head_rows = jnp.concatenate(head_sums, axis=-1).reshape(2, width)
+
+    def beside(*parts):
+        return jnp.concatenate(parts, axis=-1)
+
+    def beside_or_last(*parts):
+        return jnp.where(pl.program_id(0) == 3, parts[-1], beside(*parts[:-1]))
+
+    grads = unattend(qkv, grad_attended, images, seq, 0, PARTS, tensor_size)
+    head_grad, mlp_grads[0] = lax.optimization_barrier((grads[0], mlp_grads[0]))
+    carry, dw_qkv, head_sums = close(
+        0, PARTS, normed_one, (head_grad, *grads[1:]), w_attn, None, None, fsdp, images, seq
+    )
+    qkv_grads, head_sums = [scatter_gradient(dw_qkv)], [head_sums]
+    carry, mlp_grads[1] = lax.optimization_barrier((carry, mlp_grads[1]))
+    grads = unattend(qkv, grad_attended, images, seq, 1, PARTS, tensor_size)
+    mlp_grads[0], head_grad = lax.optimization_barrier((mlp_grads[0], grads[0]))
+    mlp_inner, mlp_diff = inner_step(beside, [lambda j: j] * len(PIECES), mlp_grads, mlp_master, mlp_moments, "inner_mlp")
+    carry, mlp_diff = lax.optimization_barrier((carry, mlp_diff))
+    patches_grad, sums_one, dw_qkv, sums = close(
+        1, PARTS, normed_one, (head_grad, *grads[1:]), w_attn, carry, [x, grad_resid, vec], fsdp, images, seq
+    )
+    qkv_grads.append(scatter_gradient(dw_qkv))
+    head_sums.append(sums)
+    mlp_diff, sums_one = lax.optimization_barrier((mlp_diff, sums_one))
+    (mlp_total,) = group_sum(mlp_diff, groups, 10, "group_mlp")
+    mlp_state, mlp_copy = outer_step(groups, mlp_total, mlp_master, mlp_outer, "outer_mlp")
+
+    head_rows = jnp.concatenate([v.reshape(2, tensor_size, -1) for v in head_sums], axis=-1).reshape(2, width)
     hidden_bias = jnp.concatenate(bias_parts, axis=-1).reshape(-1, width)
     vector_part = jnp.concatenate([sums_one, sums_two[:2], head_rows, sums_two[2:], hidden_bias])
-    if fsdp == 2:
-        vector_inner, vector_state, vector_copy = vector_step(
-            vector_part, vec, vector_moments[0], vector_outer, groups, tensor_size, fsdp, 12
-        )
-    else:
-        vector_grad = lax.psum(vector_part, ("fsdp", "tensor"))
-        new_vector, second_vector = inner_adamw(
-            vec, vector_grad, vector_moments[0, 0], vector_moments[0, 1], VECTOR_RATE, 0.0
-        )
-        diff_vector = lax.psum(vec - new_vector, "group") / groups
-        momentum, fresh = outer_nesterov(vec, vector_outer, diff_vector)
-        vector_inner = jnp.stack([vector_grad, second_vector])
-        vector_state, vector_copy = jnp.stack([diff_vector, momentum, fresh]), fresh.astype(LOW)
-
-    def beside(*parts):
-        return jnp.concatenate(parts, axis=-1)
-
-    def beside_or_last(*parts):
-        return jnp.where(pl.program_id(0) == 3, parts[-1], beside(*parts[:-1]))
-
-    mlp_inner, mlp_diff = inner_step(beside, [lambda j: j] * QUARTERS, mlp_grads, mlp_master, mlp_moments, "inner_mlp")
-    mlp_total = group_sum(mlp_diff, groups, 10, "group_mlp")
-    mlp_state, mlp_copy = outer_step(groups, mlp_total, mlp_master, mlp_outer, "outer_mlp")
+
     out_grad, mlp_state = lax.optimization_barrier((out_grad, mlp_state))
     attn_inner, attn_diff = inner_step(
         beside_or_last,
@@ -1169,7 +1293,26 @@
         attn_moments,
         "inner_attn",
     )
-    attn_total = group_sum(attn_diff, groups, 11, "group_attn")
+    if fsdp == 2:
+        attn_total, vector_inner, vector_state, vector_copy = group_sum(
+            attn_diff,
+            groups,
+            11,
+            "group_attn",
+            [vector_part, vec, vector_moments[0], vector_outer],
+            tensor_size,
+            fsdp,
+        )
+    else:
+        (attn_total,) = group_sum(attn_diff, groups, 11, "group_attn")
+        vector_grad = lax.psum(vector_part, ("fsdp", "tensor"))
+        new_vector, second_vector = inner_adamw(
+            vec, vector_grad, vector_moments[0, 0], vector_moments[0, 1], VECTOR_RATE, 0.0
+        )
+        diff_vector = lax.psum(vec - new_vector, "group") / groups
+        momentum, fresh = outer_nesterov(vec, vector_outer, diff_vector)
+        vector_inner = jnp.stack([vector_grad, second_vector])
+        vector_state, vector_copy = jnp.stack([diff_vector, momentum, fresh]), fresh.astype(LOW)
     attn_state, attn_copy = outer_step(groups, attn_total, attn_master, attn_outer, "outer_attn")
     return (
         block_output.reshape(patches.shape),

time: 605 us -> 525 us (0.87)
  Pallas kernels: 555 us -> 473 us
  other arithmetic: 7.36 us -> 0.71 us
    pallas_call x11 -> x6, Pallas kernels: 398 us -> 317 us  [the longest x1 130 us: front(): pl.pallas_call(functools.partial(front_kernel, images, seq), in_specs=[pl...]
    convert_element_type x2 -> x0, other arithmetic: 6.65 us -> none  [the longest x1 3.99 us: local(): mlp_master.astype(LOW)]
    unnamed x37 -> x31, local copies, waits for them, and re-layouts: 17 us -> 16.9 us
  transfers between devices with their start and end apart: 7 -> 6, of which waited for: 0 -> 1; matrix products, arithmetic and copies ran while one was open for 3% -> 3% of each run, Pallas kernels for 53% -> 52%
where the time goes in v4:
time: 525 us; the launch traced here: 516 us
  Pallas kernels  473 us (90%)
  local copies, waits for them, and re-layouts  25.7 us (5%)
  between operations  14.5 us (3%)
    pallas_call x1, Pallas kernels, front(): pl.pallas_call(functools.partial(front_kernel, images, seq), in_specs=[pl...  130 us
    pallas_call x3, Pallas kernels, mlp(): pl.pallas_call(functools.partial(mlp_kernel, first, pairwise), grid=(step...  98.1 us
    pallas_call x2, Pallas kernels, group_sum(): pl.pallas_call(functools.partial(group_kernel, groups, shards, fsdp), in_...  88.3 us
    pallas_call x2, Pallas kernels, unattend(): pl.pallas_call(functools.partial(unattend_kernel, seq), grid=(images, wid...  56.6 us
    pallas_call x2, Pallas kernels, close(): pl.pallas_call(functools.partial(close_kernel, seq, images, pairwise, fir...  41.2 us
    pallas_call x1, Pallas kernels, turn(): pl.pallas_call(functools.partial(turn_kernel, seq, pairwise), grid=(image...  21.4 us
    pallas_call x2, Pallas kernels, inner_step(): pl.pallas_call(functools.partial(inner_kernel, join, len(pieces)), grid=(...  20 us
    pallas_call x2, Pallas kernels, outer_step(): pl.pallas_call(functools.partial(outer_kernel, groups), grid=(many, depth...  17.2 us
  transfers between devices with their start and end apart: 6, of which 1 were waited for; matrix products, arithmetic and copies ran while one was open for 3% of the time, Pallas kernels for 52%

profile of v4, /device:TPU:0, one launch (start us, length us, event | category | flops | bytes accessed | tf_op | source)
XLA Modules:
  0.0 515.9 jit_solution(15624796769281241842)
XLA Ops:
  7.3 0.8 slice.9
  8.6 6.1 %copy_bitcast_fusion = (bf16[2,577,1024]{2,1,0:T(8,128)(2,1)}, bf16[2,577,1024]{2,1,0:T(8,128)(2,1)}) fusion(bf16[1,2,1,577,1024]{4,1,3,2,0:T(2,128)(2,1)} %param.13, bf16[1,2,1,577,1024]{4,1,3,2,0:T(2,128)(2,1)} %param.12), kind=kLoop, calls=%fused_computation | loop fusion | bytes 9453568 | tf_op jit(solution)/shard_map/reshape | solution.py:1231
  14.7 0.7 fusion.alive_ref
  15.4 130.2 %front.1 = (bf16[4,4,1024,256]{3,2,1,0:T(8,128)(2,1)}, bf16[4,2,1024,1024]{3,2,1,0:T(8,128)(2,1)}, bf16[1184,1024]{1,0:T(8,128)(2,1)}, bf16[3,1184,1024]{2,1,0:T...) custom-call(f32[2]{0:T(128)} %fusion.alive_ref, ...), custom_call_target="tpu_custom_call" | custom-call | flops 9932111872 | bytes 36372480 | tf_op jit(solution)/shard_map/front/pallas_call | solution.py:947
  145.6 26.4 %mlp_0.1 = (f32[1184,1024]{1,0:T(8,128)}, f32[1184,1024]{1,0:T(8,128)}, bf16[4,2,512,256]{3,2,1,0:T(8,128)(2,1)}, f32[4,1,256]{2,1,0:T(1,128)}) custom-call(bf16[1184,1024]{1,0:T(8,128)(2,1)} %get-tuple-element.74.n_ref, bf16[1184,1024]{1,0:T(8,128)(2,1)} %get-tuple-element.75.g_ref.g2_ref, bf16[4,2,1024,1024]{3,2,1,0:T(8,128)(2,1)} %get-tuple-element.76.w1_ref.w2_ref, ...), custom_call_target="tpu_custom_call" | custom-call | flops 14898167808 | bytes 29097984 | tf_op jit(solution)/shard_map/mlp_0/pallas_call | solution.py:333
  172.1 26.1 %mlp_1.1 = (f32[1184,1024]{1,0:T(8,128)}, f32[1184,1024]{1,0:T(8,128)}, bf16[4,2,512,256]{3,2,1,0:T(8,128)(2,1)}, f32[4,1,256]{2,1,0:T(1,128)}) custom-call(bf16[1184,1024]{1,0:T(8,128)(2,1)} %get-tuple-element.74.n_ref, bf16[1184,1024]{1,0:T(8,128)(2,1)} %get-tuple-element.75.g_ref.g2_ref, bf16[4,2,1024,1024]{3,2,1,0:T(8,128)(2,1)} %get-tuple-element.76.w1_ref.w2_ref, ...), custom_call_target="tpu_custom_call" | custom-call | flops 14898167808 | bytes 29097984 | tf_op jit(solution)/shard_map/mlp_1/pallas_call | solution.py:333
  198.3 45.5 %mlp_2.1 = (f32[1184,1024]{1,0:T(8,128)}, f32[1184,1024]{1,0:T(8,128)}, bf16[4,2,512,512]{3,2,1,0:T(8,128)(2,1)}, f32[4,1,512]{2,1,0:T(1,128)}) custom-call(bf16[1184,1024]{1,0:T(8,128)(2,1)} %get-tuple-element.74.n_ref, bf16[1184,1024]{1,0:T(8,128)(2,1)} %get-tuple-element.75.g_ref.g2_ref, bf16[4,2,1024,1024]{3,2,1,0:T(8,128)(2,1)} %get-tuple-element.76.w1_ref.w2_ref, ...), custom_call_target="tpu_custom_call" | custom-call | flops 29796335616 | bytes 29097984 | tf_op jit(solution)/shard_map/mlp_2/pallas_call | solution.py:333
  243.9 21.4 %turn.1 = (bf16[2,577,1024]{2,1,0:T(8,128)(2,1)}, f32[1184,1024]{1,0:T(8,128)}, bf16[1184,1024]{1,0:T(8,128)(2,1)}, bf16[4,1,512,256]{3,2,1,0:T(8,128)(2,1)}, f32[4,1024]{1,0:T(4,128)}) custom-call(f32[2]{0:T(128)} %fusion.alive_ref, f32[1184,1024]{1,0:T(8,128)} %get-tuple-element.73.resid_ref, f32[1184,1024]{1,0:T(8,128)} %get-tuple-element.81.y_ref, ...), custom_call_target="tpu_custom_call" | custom-call | flops 4966055936 | bytes 29097984 | tf_op jit(solution)/shard_map/turn/pallas_call | solution.py:427
  265.4 28.3 %unattend_0.1 = (bf16[1,1184,512]{2,1,0:T(8,128)(2,1)}, bf16[1,1184,512]{2,1,0:T(8,128)(2,1)}, bf16[1,1184,512]{2,1,0:T(8,128)(2,1)}) custom-call(bf16[3,1184,1024]{2,1,0:T(8,128)(2,1)} %get-tuple-element.87.q_ref.k_ref.v_ref, bf16[3,1184,1024]{2,1,0:T(8,128)(2,1)} %get-tuple-element.87.q_ref.k_ref.v_ref, ...), custom_call_target="tpu_custom_call" | custom-call | flops 14355005440 | bytes 8486912 | tf_op jit(solution)/shard_map/unattend_0/pallas_call | solution.py:496
  293.7 16.9 %close_0.1 = (f32[1184,1024]{1,0:T(8,128)}, bf16[4,3,512,128]{3,2,1,0:T(8,128)(2,1)}, f32[2,512]{1,0:T(2,128)}) custom-call(bf16[1184,1024]{1,0:T(8,128)(2,1)} %get-tuple-element.86.n_ref, bf16[1,1184,512]{2,1,0:T(8,128)(2,1)} %get-tuple-element.96.dq_ref, bf16[1,1184,512]{2,1,0:T(8,128)(2,1)} %get-tuple-element.97.dk_ref, ...), custom_call_target="tpu_custom_call" | custom-call | flops 7449083904 | bytes 24248320 | tf_op jit(solution)/shard_map/close_0/pallas_call | solution.py:613
  310.7 28.3 %unattend_1.1 = (bf16[1,1184,512]{2,1,0:T(8,128)(2,1)}, bf16[1,1184,512]{2,1,0:T(8,128)(2,1)}, bf16[1,1184,512]{2,1,0:T(8,128)(2,1)}) custom-call(bf16[3,1184,1024]{2,1,0:T(8,128)(2,1)} %get-tuple-element.87.q_ref.k_ref.v_ref, bf16[3,1184,1024]{2,1,0:T(8,128)(2,1)} %get-tuple-element.87.q_ref.k_ref.v_ref, ...), custom_call_target="tpu_custom_call" | custom-call | flops 14355005440 | bytes 8486912 | tf_op jit(solution)/shard_map/unattend_1/pallas_call | solution.py:496
  339.0 1.5 reduce-scatter.11.cloned.1.call-done
  340.5 13.0 %inner_mlp.1 = (f32[1,2,2,512,1024]{4,3,2,1,0:T(8,128)}, bf16[2,512,1024]{2,1,0:T(8,128)(2,1)}) custom-call(bf16[2,512,256]{2,1,0:T(8,128)(2,1)} %bitcast.36, bf16[2,512,256]{2,1,0:T(8,128)(2,1)} %bitcast.37, bf16[2,512,512]{2,1,0:T(8,128)(2,1)} %bitcast.33, f32[2,512,1024]{2,1,0:T(8,128)} %master_ref.2, f32[1,2,2,512,1024]{4,3,2,1,0:T(8,128)} %refs_4_.2), custom_call_target="tpu_custom_call" | custom-call | flops 31457280 | bytes 25165824 | tf_op jit(solution)/shard_map/inner_mlp/pallas_call | solution.py:1018
  353.5 24.4 %close_1.1 = (f32[2,577,1024]{2,1,0:T(8,128)}, f32[2,1024]{1,0:T(2,128)}, bf16[4,3,512,128]{3,2,1,0:T(8,128)(2,1)}, f32[2,512]{1,0:T(2,128)}) custom-call(bf16[1184,1024]{1,0:T(8,128)(2,1)} %get-tuple-element.86.n_ref, bf16[1,1184,512]{2,1,0:T(8,128)(2,1)} %get-tuple-element.93.dq_ref, bf16[1,1184,512]{2,1,0:T(8,128)(2,1)} %get-tuple-element.94.dk_ref, ...), custom_call_target="tpu_custom_call" | custom-call | flops 7449083904 | bytes 24248320 | tf_op jit(solution)/shard_map/close_1/pallas_call | solution.py:613
  377.9 0.7 copy.36
  378.7 3.8 copy.29
  382.6 9.4 %copy.30 = f32[1,2,1,577,1024]{4,2,3,1,0:T(1,128)} copy(f32[1,2,1,577,1024]{4,3,1,2,0:T(8,128)} %bitcast.30) | data formatting | bytes 9453568
  392.1 54.9 %group_mlp.1 = bf16[1024,1024]{1,0:T(8,128)(2,1)} custom-call(bf16[1024,1024]{1,0:T(8,128)(2,1)} %bitcast.32), custom_call_target="tpu_custom_call" | custom-call | flops 4194304 | bytes 8388608 | tf_op jit(solution)/shard_map/group_mlp/pallas_call | solution.py:1180
  447.0 11.2 %outer_mlp.1 = (f32[3,2,512,1024]{3,2,1,0:T(8,128)}, bf16[2,512,1024]{2,1,0:T(8,128)(2,1)}) custom-call(bf16[2,512,1024]{2,1,0:T(8,128)(2,1)} %bitcast.29, f32[2,512,1024]{2,1,0:T(8,128)} %master_ref.2, f32[2,512,1024]{2,1,0:T(8,128)} %outer_ref.2), custom_call_target="tpu_custom_call" | custom-call | flops 10485760 | bytes 25165824 | tf_op jit(solution)/shard_map/outer_mlp/pallas_call | solution.py:1043
  458.2 1.3 concatenate.11.refs_0_
  459.4 7.0 %inner_attn.1 = (f32[1,2,4,512,256]{4,3,2,1,0:T(8,128)}, bf16[4,512,256]{2,1,0:T(8,128)(2,1)}) custom-call(bf16[3,512,128]{2,1,0:T(8,128)(2,1)} %bitcast.39, bf16[3,512,128]{2,1,0:T(8,128)(2,1)} %bitcast.40, bf16[1,512,256]{2,1,0:T(8,128)(2,1)} %bitcast.41, f32[4,512,256]{2,1,0:T(8,128)} %master_ref.3, f32[1,2,4,512,256]{4,3,2,1,0:T(8,128)} %refs_4_.3), custom_call_target="tpu_custom_call" | custom-call | flops 15728640 | bytes 12582912 | tf_op jit(solution)/shard_map/inner_attn/pallas_call | solution.py:1018
  466.4 33.4 %group_attn.1 = (bf16[2048,256]{1,0:T(8,128)(2,1)}, f32[2,12,1024]{2,1,0:T(8,128)}, f32[3,12,1024]{2,1,0:T(8,128)}, bf16[12,1024]{1,0:T(8,128)(2,1)}) custom-call(bf16[2048,256]{1,0:T(8,128)(2,1)} %bitcast.35, f32[12,1024]{1,0:T(8,128)} %concatenate.11.refs_0_, f32[12,1024]{1,0:T(8,128)} %refs_1_.1, f32[2,12,1024]{2,1,0:T(8,128)} %bitcast.38, f32[12,1024]{1,0:T(8,128)} %refs_3_.7), custom_call_target="tpu_custom_call" | custom-call | flops 2097152 | bytes 4194304 | tf_op jit(solution)/shard_map/group_attn/pallas_call | solution.py:1180
  499.8 1.6 copy.31
  501.5 6.1 %outer_attn.1 = (f32[3,4,512,256]{3,2,1,0:T(8,128)}, bf16[4,512,256]{2,1,0:T(8,128)(2,1)}) custom-call(bf16[4,512,256]{2,1,0:T(8,128)(2,1)} %bitcast.34, f32[4,512,256]{2,1,0:T(8,128)} %master_ref.3, f32[4,512,256]{2,1,0:T(8,128)} %outer_ref.3), custom_call_target="tpu_custom_call" | custom-call | flops 5242880 | bytes 12582912 | tf_op jit(solution)/shard_map/outer_attn/pallas_call | solution.py:1043
  (53 shorter events, 2.4 us)
Async XLA Ops:
  7.2 286.5 %reduce-scatter.7.cloned.1.call-start = ((), (), s32[]{:S(2)}) async-start(), calls=%async_computation.6 | async-start | bytes 2621440 | tf_op jit(solution)/shard_map/reduce_scatter | solution.py:1205
  8.6 6.1 %copy-start.11 = (s32[1,2,2]{2,1,0:T(2,128)S(1)}, s32[1,2,2]{2,1,0:T(2,128)}, u32[]{:S(2)}) copy-start(s32[1,2,2]{2,1,0:T(2,128)} %param.14) | copy-start | bytes 52
  172.0 166.9 %reduce-scatter.9.cloned.1.call-start = ((), (), s32[]{:S(2)}) async-start(), calls=%async_computation.7 | async-start | bytes 2621440 | tf_op jit(solution)/shard_map/reduce_scatter | solution.py:1205
  198.3 142.2 %reduce-scatter.11.cloned.1.call-start = ((), (), s32[]{:S(2)}) async-start(), calls=%async_computation.8 | async-start | bytes 5242880 | tf_op jit(solution)/shard_map/reduce_scatter | solution.py:1205
  243.8 214.3 %reduce-scatter.17.cloned.1.call-start = ((), (), s32[]{:S(2)}) async-start(), calls=%async_computation.11 | async-start | bytes 1310720 | tf_op jit(solution)/shard_map/reduce_scatter | solution.py:1205
  265.4 194.1 %reduce-scatter.13.cloned.1.call-start = ((), (), s32[]{:S(2)}) async-start(), calls=%async_computation.9 | async-start | bytes 1966080 | tf_op jit(solution)/shard_map/reduce_scatter | solution.py:1205
  310.6 148.8 %reduce-scatter.15.cloned.1.call-start = ((), (), s32[]{:S(2)}) async-start(), calls=%async_computation.10 | async-start | bytes 1966080 | tf_op jit(solution)/shard_map/reduce_scatter | solution.py:1205
  353.5 24.4 %copy-start.2 = (f32[1,2,12,1024]{3,1,2,0:T(2,128)S(1)}, f32[1,2,12,1024]{3,1,2,0:T(2,128)}, u32[]{:S(2)}) copy-start(f32[1,2,12,1024]{3,1,2,0:T(2,128)} %param.20) | copy-start | bytes 294916
  353.5 25.1 %copy-start.7 = (f32[4,1,256]{2,1,0:T(1,128)S(1)}, f32[4,1,256]{2,1,0:T(1,128)}, u32[]{:S(2)}) copy-start(f32[4,1,256]{2,1,0:T(1,128)} %get-tuple-element.123) | copy-start | bytes 12292
  353.5 25.1 %copy-start = (bf16[2,577,1024]{2,1,0:T(8,128)(2,1)S(1)}, bf16[2,577,1024]{2,1,0:T(8,128)(2,1)}, u32[]{:S(2)}) copy-start(bf16[2,577,1024]{2,1,0:T(8,128)(2,1)} %get-tuple-element.85) | copy-start | bytes 7090180
  378.6 3.9 copy-start.8
  378.6 3.9 copy-start.6
  378.6 3.9 copy-start.4
  378.7 3.9 copy-start.9
  382.6 9.5 %copy-start.10 = (f32[2,512]{1,0:T(2,128)S(1)}, f32[2,512]{1,0:T(2,128)}, u32[]{:S(2)}) copy-start(f32[2,512]{1,0:T(2,128)} %get-tuple-element.122) | copy-start | bytes 12292
  446.9 11.2 %copy-start.5 = (f32[2,1024]{1,0:T(2,128)S(1)}, f32[2,1024]{1,0:T(2,128)}, u32[]{:S(2)}) copy-start(f32[2,1024]{1,0:T(2,128)} %get-tuple-element.119) | copy-start | bytes 24580
  501.5 6.1 %copy-start.1 = (f32[3,12,1024]{2,1,0:T(8,128)S(1)}, f32[3,12,1024]{2,1,0:T(8,128)}, u32[]{:S(2)}) copy-start(f32[3,12,1024]{2,1,0:T(8,128)} %get-tuple-element.181) | copy-start | bytes 442372
  501.5 6.7 %copy-start.3 = (bf16[12,1024]{1,0:T(8,128)(2,1)S(1)}, bf16[12,1024]{1,0:T(8,128)(2,1)}, u32[]{:S(2)}) copy-start(bf16[12,1024]{1,0:T(8,128)(2,1)} %get-tuple-element.182) | copy-start | bytes 73732
Sparse Core Ops, SparseCore 0:
  172.2 44.3 reduce-scatter.6
  219.0 43.1 reduce-scatter.8
  264.4 75.9 reduce-scatter.10
  342.7 27.6 reduce-scatter.16
  372.5 33.9 reduce-scatter.12
  408.7 34.2 reduce-scatter.14
